TPU v7x, 32 devices: a whole 2x2x4 slice. The times are simulated.
32 devices in a mesh: dp: 8 (over y, x, core), tensor: 4 (over z).
Axes of the slice: x: 2, y: 2, z: 4, core: 2. Of those that a mesh axis runs over, the one named last changes fastest.
Arguments:
- inputs: bfloat16 [8192, 512], P(('dp', 'tensor'))
- out_grad: bfloat16 [8192, 512], P(('dp', 'tensor')), may hold values from -6 to 6
- norm_gains: float32 [5, 512], P(None, ('dp', 'tensor')), may hold values from 0.5 to 1.5
- first_up: bfloat16 [512, 2048], P('dp', 'tensor'), may hold values from -0.25 to 0.25
- first_down: bfloat16 [2048, 512], P('tensor', 'dp'), may hold values from -0.125 to 0.125
- attend_in: bfloat16 [4, 512, 512], P(None, 'dp', 'tensor'), may hold values from -0.25 to 0.25
- attend_out: bfloat16 [512, 512], P('tensor', 'dp'), may hold values from -1 to 1
- position_bias: bfloat16 [2, 8, 64], P(None, 'tensor', 'dp'), may hold values from -3 to 3
- convolve_in: bfloat16 [512, 2, 512], P('dp', None, 'tensor'), may hold values from -0.25 to 0.25
- depth_kernel: float32 [512, 31], P('tensor'), may hold values from -1 to 1
- batch_norm: float32 [2, 512], P(None, 'tensor'), may hold values from 0.5 to 1.5
- convolve_out: bfloat16 [512, 512], P('tensor', 'dp'), may hold values from -0.25 to 0.25
- second_up: bfloat16 [512, 2048], P('dp', 'tensor'), may hold values from -0.25 to 0.25
- second_down: bfloat16 [2048, 512], P('tensor', 'dp'), may hold values from -0.125 to 0.125
Outputs:
- output_rows: float32 [8192, 512], P(('dp', 'tensor'))
- input_grad: float32 [8192, 512], P(('dp', 'tensor'))
- grad_norm_gains: float32 [5, 512], P(None, ('dp', 'tensor'))
- grad_first_up: float32 [512, 2048], P('dp', 'tensor')
- grad_first_down: float32 [2048, 512], P('tensor', 'dp')
- grad_attend_in: float32 [4, 512, 512], P(None, 'dp', 'tensor')
- grad_attend_out: float32 [512, 512], P('tensor', 'dp')
- grad_position_bias: float32 [2, 8, 64], P(None, 'tensor', 'dp')
- grad_convolve_in: float32 [512, 2, 512], P('dp', None, 'tensor')
- grad_depth_kernel: float32 [512, 31], P('tensor')
- grad_batch_norm: float32 [2, 512], P(None, 'tensor')
- grad_convolve_out: float32 [512, 512], P('tensor', 'dp')
- grad_second_up: float32 [512, 2048], P('dp', 'tensor')
- grad_second_down: float32 [2048, 512], P('tensor', 'dp')
All inputs are finite; a program needn't handle non-finite values.
Results may differ from a plain program's by a relative error of at most 0.023.
Values may be sent and summed in bfloat16 or wider, within the bound.
A program may use at most 128 MiB of HBM per device.

v0:
```python
import math

import jax
import jax.numpy as jnp
from jax import lax
from jax.sharding import PartitionSpec as P

D = 512
KERNEL = 31
FRAMES = 1024
UTT_DEV = 1
BLOCK = 512


norm_eps = 1e-05


def norm_rows(values, gain_row):
    centred = values - jnp.mean(values, axis=-1, keepdims=True)
    inverse = lax.rsqrt(jnp.mean(centred * centred, axis=-1, keepdims=True) + norm_eps)
    scaled = centred * inverse
    return (scaled * gain_row, (scaled, inverse))


def norm_back(incoming, gain_row, norm_saved):
    scaled, inverse = norm_saved
    grad_scaled = incoming * gain_row
    inner = jnp.mean(grad_scaled * scaled, axis=-1, keepdims=True)
    grad_in = inverse * (
        grad_scaled - jnp.mean(grad_scaled, axis=-1, keepdims=True) - scaled * inner
    )
    return (grad_in, jnp.sum(incoming * scaled, axis=0))


def swish_grad(pre_act):
    sigmoid_val = jax.nn.sigmoid(pre_act)
    return sigmoid_val * (1.0 + pre_act * (1.0 - sigmoid_val))


def contract_rows(left, right):
    return lax.dot_general(
        left, right, (((0,), (0,)), ((), ())), preferred_element_type=jnp.float32
    )


def times_transposed(left, right):
    return lax.dot_general(
        left, right, (((1,), (1,)), ((), ())), preferred_element_type=jnp.float32
    )


def spread_rows(row_block):
    return lax.all_gather(row_block, "tensor", axis=0, tiled=True)


def fold_rows(source, weight, contract):
    return lax.psum_scatter(
        lax.dot_general(
            source, weight, (((1,), (contract,)), ((), ())), preferred_element_type=jnp.float32
        ),
        "tensor",
        scatter_dimension=0,
        tiled=True,
    )


def position_table():
    row_index = jnp.arange(2 * FRAMES - 1, dtype=jnp.float32)
    distance = FRAMES - 1 - row_index
    frequency = jnp.exp(jnp.arange(D // 2, dtype=jnp.float32) * (-2.0 * math.log(10000.0) / D))
    angles = distance[:, None] * frequency[None, :]
    return jnp.concatenate([jnp.sin(angles), jnp.cos(angles)], axis=1).astype(jnp.bfloat16)


def skew_rows(wide_scores, frames):
    head_count, block_rows, full_width = wide_scores.shape
    flattened = wide_scores.reshape(head_count, block_rows * full_width)
    trimmed = lax.slice_in_dim(
        flattened, block_rows - 1, block_rows - 1 + block_rows * (full_width - 1), axis=1
    )
    return trimmed.reshape(head_count, block_rows, full_width - 1)[:, :, :frames]


def unskew_rows(grad_scores, full_width):
    head_count, block_rows, frames = grad_scores.shape
    padded = jnp.pad(grad_scores, ((0, 0), (0, 0), (0, full_width - 1 - frames)))
    flattened = jnp.pad(
        padded.reshape(head_count, block_rows * (full_width - 1)), ((0, 0), (block_rows - 1, 1))
    )
    return flattened.reshape(head_count, block_rows, full_width)


def add_into(target, update, utterance_index):
    current = lax.dynamic_index_in_dim(target, utterance_index, 0, keepdims=False)
    return lax.dynamic_update_index_in_dim(target, current + update, utterance_index, 0)


def block_scores(pieces, block_index):
    content_q, position_q, key_rows, value_rows, positions = pieces
    frames = content_q.shape[1]
    head_count = content_q.shape[2]
    head_dim = content_q.shape[3]
    per_utterance = frames // BLOCK
    utterance_index = block_index // per_utterance
    row_start = block_index % per_utterance * BLOCK
    corner = (utterance_index, row_start, 0, 0)
    extent = (1, BLOCK, head_count, head_dim)
    content_blk = lax.dynamic_slice(content_q, corner, extent)[0]
    position_blk = lax.dynamic_slice(position_q, corner, extent)[0]
    key_utt = lax.dynamic_index_in_dim(key_rows, utterance_index, 0, keepdims=False)
    value_utt = lax.dynamic_index_in_dim(value_rows, utterance_index, 0, keepdims=False)
    offset = frames - BLOCK - row_start
    pos_blk = lax.dynamic_slice_in_dim(positions, offset, BLOCK + frames - 1, 0)
    content = jnp.einsum("bhe,fhe->hbf", content_blk, key_utt, preferred_element_type=jnp.float32)
    wide_scores = jnp.einsum(
        "bhe,mhe->hbm", position_blk, pos_blk, preferred_element_type=jnp.float32
    )
    scores = (content + skew_rows(wide_scores, frames)) * head_dim ** (-0.5)
    return (
        scores,
        (
            content_blk,
            position_blk,
            key_utt,
            value_utt,
            pos_blk,
            utterance_index,
            row_start,
            offset,
        ),
    )


def feed_forward(residual, gain_row, up_weight, down_weight, spread, folding):
    normed, norm_saved = norm_rows(residual, gain_row)
    gathered = spread(normed.astype(jnp.bfloat16))
    pre_act = jnp.dot(gathered, up_weight, preferred_element_type=jnp.float32)
    hidden = (pre_act * jax.nn.sigmoid(pre_act)).astype(jnp.bfloat16)
    branch = folding(hidden, down_weight, 0)
    return (residual + 0.5 * branch, (norm_saved, gathered, pre_act, hidden))


def feed_backward(incoming, gain_row, up_weight, down_weight, stored, spread, folding):
    norm_saved, gathered, pre_act, hidden = stored
    grad_branch = spread((0.5 * incoming).astype(jnp.bfloat16))
    grad_down = contract_rows(hidden, grad_branch)
    grad_hidden = times_transposed(grad_branch, down_weight)
    grad_pre = (grad_hidden * swish_grad(pre_act)).astype(jnp.bfloat16)
    grad_up = contract_rows(gathered, grad_pre)
    grad_normed = folding(grad_pre, up_weight, 1)
    grad_resid, gain_grad = norm_back(grad_normed, gain_row, norm_saved)
    return (incoming + grad_resid, gain_grad, grad_up, grad_down)


def attention_forward(residual, gain_row, attend_w, attend_w_out, bias_pair, sinusoid):
    normed, norm_saved = norm_rows(residual, gain_row)
    gathered = spread_rows(normed.astype(jnp.bfloat16))
    local_width = attend_w.shape[2]
    head_dim = bias_pair.shape[2]
    head_count = local_width // head_dim
    shape_four = (UTT_DEV, FRAMES, head_count, head_dim)
    projected = jnp.einsum(
        "rd,kde->kre", gathered, attend_w[:3], preferred_element_type=jnp.float32
    )
    bias_float = bias_pair.astype(jnp.float32).reshape(2, local_width)
    content_q = (projected[0] + bias_float[0]).astype(jnp.bfloat16).reshape(shape_four)
    position_q = (projected[0] + bias_float[1]).astype(jnp.bfloat16).reshape(shape_four)
    key_rows = projected[1].astype(jnp.bfloat16).reshape(shape_four)
    value_rows = projected[2].astype(jnp.bfloat16).reshape(shape_four)
    positions = jnp.dot(sinusoid, attend_w[3], preferred_element_type=jnp.float32).astype(
        jnp.bfloat16
    )
    positions = positions.reshape(2 * FRAMES - 1, head_count, head_dim)
    pieces = (content_q, position_q, key_rows, value_rows, positions)

    def forward_block(block_index):
        scores, block_parts = block_scores(pieces, block_index)
        row_peak = jnp.max(scores, axis=-1, keepdims=True)
        exponent = jnp.exp(scores - row_peak)
        row_total = jnp.sum(exponent, axis=-1, keepdims=True)
        softmax_w = (exponent / row_total).astype(jnp.bfloat16)
        mixture = jnp.einsum(
            "hbf,fhe->bhe", softmax_w, block_parts[3], preferred_element_type=jnp.float32
        )
        return (mixture.astype(jnp.bfloat16), (row_peak + jnp.log(row_total))[:, :, 0])

    blocks = jnp.arange(UTT_DEV * (FRAMES // BLOCK), dtype=jnp.int32)
    mixture, log_total = lax.map(forward_block, blocks)
    mixture = mixture.reshape(UTT_DEV * FRAMES, local_width)
    branch = fold_rows(mixture, attend_w_out, 0)
    return (residual + branch, (norm_saved, gathered, pieces, mixture, log_total))


def attention_backward(incoming, gain_row, attend_w, attend_w_out, sinusoid, stored):
    norm_saved, gathered, pieces, mixture, log_total = stored
    content_q, position_q, key_rows, value_rows, positions = pieces
    head_count = content_q.shape[2]
    head_dim = content_q.shape[3]
    local_width = head_count * head_dim
    all_rows = UTT_DEV * FRAMES
    score_scale = head_dim ** (-0.5)
    pos_span = BLOCK + FRAMES - 1
    grad_branch = spread_rows(incoming.astype(jnp.bfloat16))
    grad_w_out = contract_rows(mixture, grad_branch)
    grad_mixture = times_transposed(grad_branch, attend_w_out).astype(jnp.bfloat16)
    grad_mixture = grad_mixture.reshape(UTT_DEV, FRAMES, head_count, head_dim)

    def backward_block(carried, block_index):
        grad_keys, grad_values, grad_pos = carried
        scores, block_parts = block_scores(pieces, block_index)
        (
            content_blk,
            position_blk,
            key_utt,
            value_utt,
            pos_blk,
            utterance_index,
            row_start,
            offset,
        ) = block_parts
        softmax_w = jnp.exp(scores - log_total[block_index][:, :, None])
        grad_out_blk = lax.dynamic_slice(
            grad_mixture, (utterance_index, row_start, 0, 0), (1, BLOCK, head_count, head_dim)
        )[0]
        value_step = jnp.einsum(
            "hbf,bhe->fhe",
            softmax_w.astype(jnp.bfloat16),
            grad_out_blk,
            preferred_element_type=jnp.float32,
        )
        grad_weights = jnp.einsum(
            "bhe,fhe->hbf", grad_out_blk, value_utt, preferred_element_type=jnp.float32
        )
        grad_scores = softmax_w * (
            grad_weights - jnp.sum(grad_weights * softmax_w, axis=-1, keepdims=True)
        )
        grad_scores = grad_scores.astype(jnp.bfloat16)
        grad_content = (
            jnp.einsum("hbf,fhe->bhe", grad_scores, key_utt, preferred_element_type=jnp.float32)
            * score_scale
        )
        key_step = (
            jnp.einsum("hbf,bhe->fhe", grad_scores, content_blk, preferred_element_type=jnp.float32)
            * score_scale
        )
        grad_wide = unskew_rows(grad_scores, pos_span)
        grad_position = (
            jnp.einsum("hbm,mhe->bhe", grad_wide, pos_blk, preferred_element_type=jnp.float32)
            * score_scale
        )
        pos_step = (
            jnp.einsum("hbm,bhe->mhe", grad_wide, position_blk, preferred_element_type=jnp.float32)
            * score_scale
        )
        grad_keys = add_into(grad_keys, key_step, utterance_index)
        grad_values = add_into(grad_values, value_step, utterance_index)
        current = lax.dynamic_slice_in_dim(grad_pos, offset, pos_span, 0)
        grad_pos = lax.dynamic_update_slice_in_dim(grad_pos, current + pos_step, offset, 0)
        return ((grad_keys, grad_values, grad_pos), (grad_content, grad_position))

    zero_rows = jnp.zeros((UTT_DEV, FRAMES, head_count, head_dim), jnp.float32)
    zero_pos = jnp.zeros((2 * FRAMES - 1, head_count, head_dim), jnp.float32)
    blocks = jnp.arange(log_total.shape[0], dtype=jnp.int32)
    carried, outputs = lax.scan(backward_block, (zero_rows, zero_rows, zero_pos), blocks)
    grad_keys, grad_values, grad_pos = carried
    grad_content = outputs[0].reshape(all_rows, local_width)
    grad_position = outputs[1].reshape(all_rows, local_width)
    grad_bias = jnp.stack([jnp.sum(grad_content, axis=0), jnp.sum(grad_position, axis=0)]).reshape(
        2, head_count, head_dim
    )
    grad_proj = jnp.concatenate(
        [
            (grad_content + grad_position).astype(jnp.bfloat16),
            grad_keys.reshape(all_rows, local_width).astype(jnp.bfloat16),
            grad_values.reshape(all_rows, local_width).astype(jnp.bfloat16),
        ],
        axis=1,
    )
    full_width = gathered.shape[1]
    grad_qkv = (
        contract_rows(gathered, grad_proj).reshape(full_width, 3, local_width).transpose(1, 0, 2)
    )
    grad_table = lax.dot_general(
        sinusoid.astype(jnp.float32),
        grad_pos.reshape(2 * FRAMES - 1, local_width),
        (((0,), (0,)), ((), ())),
        precision=lax.Precision.HIGHEST,
        preferred_element_type=jnp.float32,
    )
    grad_w = jnp.concatenate([grad_qkv, grad_table[None]], axis=0)
    stacked_w = attend_w[:3].transpose(1, 0, 2).reshape(full_width, 3 * local_width)
    grad_normed = fold_rows(grad_proj, stacked_w, 1)
    grad_resid, gain_grad = norm_back(grad_normed, gain_row, norm_saved)
    return (incoming + grad_resid, gain_grad, grad_w, grad_bias, grad_w_out)


def convolve_forward(residual, gain_row, convolve_w, kernel_rows, norm_pair, convolve_w_out):
    normed, norm_saved = norm_rows(residual, gain_row)
    gathered = spread_rows(normed.astype(jnp.bfloat16))
    full_width = convolve_w.shape[0]
    local_width = convolve_w.shape[2]
    pre_act = jnp.dot(
        gathered,
        convolve_w.reshape(full_width, 2 * local_width),
        preferred_element_type=jnp.float32,
    )
    value_half = pre_act[:, :local_width]
    sigmoid_gate = jax.nn.sigmoid(pre_act[:, local_width:])
    gated_rows = (value_half * sigmoid_gate).reshape(UTT_DEV, FRAMES, local_width)
    half_width = KERNEL // 2
    padded = jnp.pad(gated_rows, ((0, 0), (half_width, half_width), (0, 0)))
    convolved = jnp.zeros_like(gated_rows)
    for tap_index in range(KERNEL):
        convolved = (
            convolved + kernel_rows[:, tap_index] * padded[:, tap_index : tap_index + FRAMES, :]
        )
    sum_total, square_total = lax.psum(
        (jnp.sum(convolved, axis=(0, 1)), jnp.sum(convolved * convolved, axis=(0, 1))), "dp"
    )
    row_count = UTT_DEV * FRAMES * lax.axis_size("dp")
    batch_mean = sum_total / row_count
    inverse = lax.rsqrt(square_total / row_count - batch_mean * batch_mean + norm_eps)
    scaled = (convolved - batch_mean) * inverse
    normal_out = scaled * norm_pair[0] + norm_pair[1]
    activated = (
        (normal_out * jax.nn.sigmoid(normal_out))
        .astype(jnp.bfloat16)
        .reshape(UTT_DEV * FRAMES, local_width)
    )
    branch = fold_rows(activated, convolve_w_out, 0)
    stored = (
        norm_saved,
        gathered,
        value_half,
        sigmoid_gate,
        padded,
        scaled,
        inverse,
        normal_out,
        activated,
        row_count,
    )
    return (residual + branch, stored)


def convolve_backward(
    incoming, gain_row, convolve_w, kernel_rows, norm_pair, convolve_w_out, stored
):
    (
        norm_saved,
        gathered,
        value_half,
        sigmoid_gate,
        padded,
        scaled,
        inverse,
        normal_out,
        activated,
        row_count,
    ) = stored
    local_width = activated.shape[1]
    half_width = KERNEL // 2
    grad_branch = spread_rows(incoming.astype(jnp.bfloat16))
    grad_w_out = contract_rows(activated, grad_branch)
    grad_act = times_transposed(grad_branch, convolve_w_out).reshape(UTT_DEV, FRAMES, local_width)
    grad_normal = grad_act * swish_grad(normal_out)
    beta_local = jnp.sum(grad_normal, axis=(0, 1))
    gamma_local = jnp.sum(grad_normal * scaled, axis=(0, 1))
    norm_scale = norm_pair[0] * inverse
    beta_total, gamma_total = lax.psum((beta_local, gamma_local), "dp")
    grad_conv = norm_scale * (
        grad_normal - beta_total / row_count - scaled * (gamma_total / row_count)
    )
    kernel_local = jnp.stack(
        [
            jnp.sum(grad_conv * padded[:, tap_index : tap_index + FRAMES, :], axis=(0, 1))
            for tap_index in range(KERNEL)
        ],
        axis=1,
    )
    grad_kernel = lax.psum(kernel_local, "dp")
    conv_pad = jnp.pad(grad_conv, ((0, 0), (half_width, half_width), (0, 0)))
    grad_gated = jnp.zeros_like(grad_conv)
    for tap_index in range(KERNEL):
        first_row = 2 * half_width - tap_index
        grad_gated = (
            grad_gated + kernel_rows[:, tap_index] * conv_pad[:, first_row : first_row + FRAMES, :]
        )
    grad_gated = grad_gated.reshape(UTT_DEV * FRAMES, local_width)
    grad_pre = jnp.concatenate(
        [grad_gated * sigmoid_gate, grad_gated * value_half * sigmoid_gate * (1.0 - sigmoid_gate)],
        axis=1,
    ).astype(jnp.bfloat16)
    full_width = gathered.shape[1]
    grad_w = contract_rows(gathered, grad_pre).reshape(full_width, 2, local_width)
    grad_normed = fold_rows(grad_pre, convolve_w.reshape(full_width, 2 * local_width), 1)
    grad_resid, gain_grad = norm_back(grad_normed, gain_row, norm_saved)
    return (
        incoming + grad_resid,
        gain_grad,
        grad_w,
        grad_kernel,
        jnp.stack([gamma_total, beta_total]),
        grad_w_out,
    )


def per_device(
    inputs,
    out_grad,
    norm_gains,
    first_up,
    first_down,
    attend_in,
    attend_out,
    position_bias,
    convolve_in,
    depth_kernel,
    batch_norm,
    convolve_out,
    second_up,
    second_down,
):
    gain_rows = lax.all_gather(norm_gains, ("dp", "tensor"), axis=1, tiled=True)
    (
        whole_first_up,
        whole_first_down,
        whole_attend_in,
        whole_attend_out,
        whole_bias,
        whole_convolve_in,
        whole_convolve_out,
        whole_second_up,
        whole_second_down,
    ) = (
        lax.all_gather(first_up, "dp", axis=0, tiled=True),
        lax.all_gather(first_down, "dp", axis=1, tiled=True),
        lax.all_gather(attend_in, "dp", axis=1, tiled=True),
        lax.all_gather(attend_out, "dp", axis=1, tiled=True),
        lax.all_gather(position_bias, "dp", axis=2, tiled=True),
        lax.all_gather(convolve_in, "dp", axis=0, tiled=True),
        lax.all_gather(convolve_out, "dp", axis=1, tiled=True),
        lax.all_gather(second_up, "dp", axis=0, tiled=True),
        lax.all_gather(second_down, "dp", axis=1, tiled=True),
    )
    sinusoid = position_table()
    residual_zero = inputs.astype(jnp.float32)
    residual_one, stored_one = feed_forward(
        residual_zero, gain_rows[0], whole_first_up, whole_first_down, spread_rows, fold_rows
    )
    residual_two, stored_two = attention_forward(
        residual_one, gain_rows[1], whole_attend_in, whole_attend_out, whole_bias, sinusoid
    )
    residual_three, stored_three = convolve_forward(
        residual_two, gain_rows[2], whole_convolve_in, depth_kernel, batch_norm, whole_convolve_out
    )
    residual_four, stored_four = feed_forward(
        residual_three, gain_rows[3], whole_second_up, whole_second_down, spread_rows, fold_rows
    )
    output_rows, final_saved = norm_rows(residual_four, gain_rows[4])
    grad_four, gain_four = norm_back(out_grad.astype(jnp.float32), gain_rows[4], final_saved)
    grad_three, gain_three, grad_second_up, grad_second_down = feed_backward(
        grad_four,
        gain_rows[3],
        whole_second_up,
        whole_second_down,
        stored_four,
        spread_rows,
        fold_rows,
    )
    grad_two, gain_two, grad_convolve_in, grad_kernel, grad_norm_pair, grad_convolve_out = (
        convolve_backward(
            grad_three,
            gain_rows[2],
            whole_convolve_in,
            depth_kernel,
            batch_norm,
            whole_convolve_out,
            stored_three,
        )
    )
    grad_one, gain_one, grad_attend_in, grad_bias, grad_attend_out = attention_backward(
        grad_two, gain_rows[1], whole_attend_in, whole_attend_out, sinusoid, stored_two
    )
    grad_zero, gain_zero, grad_first_up, grad_first_down = feed_backward(
        grad_one, gain_rows[0], whole_first_up, whole_first_down, stored_one, spread_rows, fold_rows
    )
    gain_grads = lax.psum_scatter(
        jnp.stack([gain_zero, gain_one, gain_two, gain_three, gain_four]),
        ("dp", "tensor"),
        scatter_dimension=1,
        tiled=True,
    )
    shards = (
        lax.psum_scatter(grad_first_up, "dp", scatter_dimension=0, tiled=True),
        lax.psum_scatter(grad_first_down, "dp", scatter_dimension=1, tiled=True),
        lax.psum_scatter(grad_attend_in, "dp", scatter_dimension=1, tiled=True),
        lax.psum_scatter(grad_attend_out, "dp", scatter_dimension=1, tiled=True),
        lax.psum_scatter(grad_bias, "dp", scatter_dimension=2, tiled=True),
        lax.psum_scatter(grad_convolve_in, "dp", scatter_dimension=0, tiled=True),
        lax.psum_scatter(grad_convolve_out, "dp", scatter_dimension=1, tiled=True),
        lax.psum_scatter(grad_second_up, "dp", scatter_dimension=0, tiled=True),
        lax.psum_scatter(grad_second_down, "dp", scatter_dimension=1, tiled=True),
    )
    return (
        output_rows,
        grad_zero,
        gain_grads,
        shards[0],
        shards[1],
        shards[2],
        shards[3],
        shards[4],
        shards[5],
        grad_kernel,
        grad_norm_pair,
        shards[6],
        shards[7],
        shards[8],
    )


def solution(mesh):
    return jax.shard_map(
        per_device,
        mesh=mesh,
        in_specs=(
            P(("dp", "tensor"), None),
            P(("dp", "tensor"), None),
            P(None, ("dp", "tensor")),
            P("dp", "tensor"),
            P("tensor", "dp"),
            P(None, "dp", "tensor"),
            P("tensor", "dp"),
            P(None, "tensor", "dp"),
            P("dp", None, "tensor"),
            P("tensor", None),
            P(None, "tensor"),
            P("tensor", "dp"),
            P("dp", "tensor"),
            P("tensor", "dp"),
        ),
        out_specs=(
            P(("dp", "tensor"), None),
            P(("dp", "tensor"), None),
            P(None, ("dp", "tensor")),
            P("dp", "tensor"),
            P("tensor", "dp"),
            P(None, "dp", "tensor"),
            P("tensor", "dp"),
            P(None, "tensor", "dp"),
            P("dp", None, "tensor"),
            P("tensor", None),
            P(None, "tensor"),
            P("tensor", "dp"),
            P("dp", "tensor"),
            P("tensor", "dp"),
        ),
        check_vma=False,
    )
```

profile of v0, /device:TPU:0, one launch (start us, length us, event | category | flops | bytes accessed | tf_op | source)
XLA Modules:
  0.0 1555.3 jit_solution(11230159445161777462)
XLA Ops:
  9.5 70.9 %all-gather = f32[32,16,5]{1,2,0:T(8,128)S(1)} all-gather(f32[1,16,5]{1,2,0:T(8,128)} %bitcast.468), channel_id=1, replica_groups=mesh['dp'=8,'tensor'=4] {'dp','tensor'}, dimensions={0}, use_global_device_ids=true | all-gather | bytes 10560 | tf_op jit(solution)/shard_map/all_gather | solution.py:424
  113.4 43.1 %reduce-scatter.20.cloned.1.call-done = f32[256,512]{1,0:T(8,128)} async-done(((f32[1024,512]{1,0:T(8,128)}), f32[256,512]{1,0:T(8,128)}) %reduce-scatter.20.cloned.1.call-update) | async-done | bytes 524304 | tf_op jit(solution)/shard_map/reduce_scatter | solution.py:57
  201.8 113.9 %while.34 = (s32[]{:T(128)}, bf16[2,512,2,64]{1,3,2,0:T(8,128)(2,1)S(1)}, f32[2,2,512]{2,1,0:T(2,128)S(1)}, s32[2]{0:T(128)S(1)}, bf16[1,1024,2,64]{1,3,2,0:T(8,...) while((s32[]{:T(128)}, ...), condition=%wide.region_8.9_spmd, body=%wide.region_5.8_spmd.sunk | while | flops 478084096 | bytes 62116220 | solution.py:188
  318.0 42.0 %reduce-scatter.22.cloned.1.call-done = f32[256,512]{1,0:T(8,128)} async-done(((f32[1024,512]{1,0:T(8,128)}), f32[256,512]{1,0:T(8,128)}) %reduce-scatter.22.cloned.1.call-update) | async-done | bytes 524304 | tf_op jit(solution)/shard_map/reduce_scatter | solution.py:57
  410.3 41.8 %reduce-scatter.24.cloned.1.call-done = f32[256,512]{1,0:T(8,128)} async-done(((f32[1024,512]{1,0:T(8,128)}), f32[256,512]{1,0:T(8,128)}) %reduce-scatter.24.cloned.1.call-update) | async-done | bytes 524304 | tf_op jit(solution)/shard_map/reduce_scatter | solution.py:57
  488.4 43.1 %reduce-scatter.26.cloned.1.call-done = f32[256,512]{1,0:T(8,128)} async-done(((f32[1024,512]{1,0:T(8,128)}), f32[256,512]{1,0:T(8,128)}) %reduce-scatter.26.cloned.1.call-update) | async-done | bytes 524304 | tf_op jit(solution)/shard_map/reduce_scatter | solution.py:57
  537.3 27.3 %all-gather.18.cloned.1.call-done = bf16[1024,512]{1,0:T(8,128)(2,1)} async-done(((bf16[256,512]{1,0:T(8,128)(2,1)}), bf16[1024,512]{1,0:T(8,128)(2,1)}) %all-gather.18.cloned.1.call-update) | async-done | bytes 1048592 | tf_op jit(solution)/shard_map/all_gather | solution.py:53
  570.9 43.1 %reduce-scatter.28.cloned.1.call-done = f32[256,512]{1,0:T(8,128)} async-done(((f32[1024,512]{1,0:T(8,128)}), f32[256,512]{1,0:T(8,128)}) %reduce-scatter.28.cloned.1.call-update) | async-done | bytes 524304 | tf_op jit(solution)/shard_map/reduce_scatter | solution.py:57
  618.7 27.3 %all-gather.20.cloned.1.call-done = bf16[1024,512]{1,0:T(8,128)(2,1)} async-done(((bf16[256,512]{1,0:T(8,128)(2,1)}), bf16[1024,512]{1,0:T(8,128)(2,1)}) %all-gather.20.cloned.1.call-update) | async-done | bytes 1048592 | tf_op jit(solution)/shard_map/all_gather | solution.py:53
  670.6 41.9 %reduce-scatter.30.cloned.1.call-done = f32[256,512]{1,0:T(8,128)} async-done(((f32[1024,512]{1,0:T(8,128)}), f32[256,512]{1,0:T(8,128)}) %reduce-scatter.30.cloned.1.call-update) | async-done | bytes 524304 | tf_op jit(solution)/shard_map/reduce_scatter | solution.py:57
  716.6 27.3 %all-gather.22.cloned.1.call-done = bf16[1024,512]{1,0:T(8,128)(2,1)} async-done(((bf16[256,512]{1,0:T(8,128)(2,1)}), bf16[1024,512]{1,0:T(8,128)(2,1)}) %all-gather.22.cloned.1.call-update) | async-done | bytes 1048592 | tf_op jit(solution)/shard_map/all_gather | solution.py:53
  749.1 205.9 %while.35 = (s32[]{:T(128)}, f32[1,1024,2,64]{1,3,2,0:T(8,128)}, f32[1,1024,2,64]{1,3,2,0:T(8,128)}, f32[2047,2,64]{0,2,1:T(8,128)}, f32[2,512,2,64]{1,3,2,0:T(8...) while((s32[]{:T(128)}, f32[1,1024,2,64]{1,3,2,0:T(8,128)}, ...), condition=%wide.region_36.37_spmd, body=%wide.region_34.36_spmd.sunk | while | flops 1285028608 | bytes 134937072 | solution.py:264
  962.0 43.1 %reduce-scatter.32.cloned.1.call-done = f32[256,512]{1,0:T(8,128)} async-done(((f32[1024,512]{1,0:T(8,128)}), f32[256,512]{1,0:T(8,128)}) %reduce-scatter.32.cloned.1.call-update) | async-done | bytes 524304 | tf_op jit(solution)/shard_map/reduce_scatter | solution.py:57
  1008.5 27.3 %all-gather.24.cloned.1.call-done = bf16[1024,512]{1,0:T(8,128)(2,1)} async-done(((bf16[256,512]{1,0:T(8,128)(2,1)}), bf16[1024,512]{1,0:T(8,128)(2,1)}) %all-gather.24.cloned.1.call-update) | async-done | bytes 1048592 | tf_op jit(solution)/shard_map/all_gather | solution.py:53
  1042.8 41.4 %reduce-scatter.34.cloned.1.call-done = f32[256,512]{1,0:T(8,128)} async-done(((f32[1024,512]{1,0:T(8,128)}), f32[256,512]{1,0:T(8,128)}) %reduce-scatter.34.cloned.1.call-update) | async-done | bytes 524304 | tf_op jit(solution)/shard_map/reduce_scatter | solution.py:57
  1115.9 25.9 %all-reduce.11.cloned.1.call-done = f32[512,2,128]{2,1,0:T(2,128)} async-done(((f32[512,2,128]{2,1,0:T(2,128)}), f32[512,2,128]{2,1,0:T(2,128)}) %all-reduce.11.cloned.1.call-update) | async-done | bytes 524304
  1168.3 110.5 %reduce-scatter.50.cloned.1.call-done = f32[16,5]{1,0:T(8,128)} async-done(((f32[512,5]{1,0:T(8,128)}), f32[16,5]{1,0:T(8,128)}) %reduce-scatter.50.cloned.1.call-update) | async-done | bytes 336
  1280.2 34.7 %reduce-scatter.46.cloned.1.call-done = f32[64,512]{1,0:T(8,128)} async-done(((f32[512,512]{1,0:T(8,128)}), f32[64,512]{1,0:T(8,128)}) %reduce-scatter.46.cloned.1.call-update) | async-done | bytes 131088 | tf_op jit(solution)/shard_map/reduce_scatter | solution.py:502
  1314.9 39.6 %reduce-scatter.48.cloned.1.call-done = f32[512,64]{0,1:T(8,128)} async-done(((f32[512,512]{0,1:T(8,128)}), f32[512,64]{0,1:T(8,128)}) %reduce-scatter.48.cloned.1.call-update) | async-done | bytes 131088 | tf_op jit(solution)/shard_map/reduce_scatter | solution.py:503
  1354.5 37.3 %reduce-scatter.44.cloned.1.call-done = f32[128,64]{0,1:T(8,128)} async-done(((f32[128,512]{0,1:T(8,128)}), f32[128,64]{0,1:T(8,128)}) %reduce-scatter.44.cloned.1.call-update) | async-done | bytes 32784 | tf_op jit(solution)/shard_map/reduce_scatter | solution.py:501
  1391.8 37.3 %reduce-scatter.42.cloned.1.call-done = f32[128,64]{0,1:T(8,128)} async-done(((f32[128,512]{0,1:T(8,128)}), f32[128,64]{0,1:T(8,128)}) %reduce-scatter.42.cloned.1.call-update) | async-done | bytes 32784 | tf_op jit(solution)/shard_map/reduce_scatter | solution.py:498
  1429.1 39.8 %reduce-scatter.40.cloned.1.call-done = f32[4,64,128]{2,1,0:T(8,128)} async-done(((f32[4,512,128]{2,1,0:T(8,128)}), f32[4,64,128]{2,1,0:T(8,128)}) %reduce-scatter.40.cloned.1.call-update) | async-done | bytes 131088 | tf_op jit(solution)/shard_map/reduce_scatter | solution.py:497
  1468.9 39.6 %reduce-scatter.36.cloned.1.call-done = f32[64,512]{1,0:T(8,128)} async-done(((f32[512,512]{1,0:T(8,128)}), f32[64,512]{1,0:T(8,128)}) %reduce-scatter.36.cloned.1.call-update) | async-done | bytes 131088 | tf_op jit(solution)/shard_map/reduce_scatter | solution.py:495
  1508.5 39.7 %reduce-scatter.38.cloned.1.call-done = f32[512,64]{0,1:T(8,128)} async-done(((f32[512,512]{0,1:T(8,128)}), f32[512,64]{0,1:T(8,128)}) %reduce-scatter.38.cloned.1.call-update) | async-done | bytes 131088 | tf_op jit(solution)/shard_map/reduce_scatter | solution.py:496
  (520 shorter events, 583.4 us)
Async XLA Ops:
  7.2 99.7 %all-gather.10.cloned.1.call-start = ((), (), s32[]{:S(2)}) async-start(), calls=%async_computation.16 | async-start | bytes 1310720 | tf_op jit(solution)/shard_map/all_gather | solution.py:53
  82.5 74.0 %reduce-scatter.20.cloned.1.call-start = ((), (), s32[]{:S(2)}) async-start(), calls=%async_computation.17 | async-start | bytes 2621440 | tf_op jit(solution)/shard_map/reduce_scatter | solution.py:57
  113.4 84.7 %all-gather.12.cloned.1.call-start = ((), (), s32[]{:S(2)}) async-start(), calls=%async_computation.18 | async-start | bytes 1310720 | tf_op jit(solution)/shard_map/all_gather | solution.py:53
  158.9 201.1 %reduce-scatter.22.cloned.1.call-start = ((), (), s32[]{:S(2)}) async-start(), calls=%async_computation.19 | async-start | bytes 2621440 | tf_op jit(solution)/shard_map/reduce_scatter | solution.py:57
  318.0 71.7 %all-gather.14.cloned.1.call-start = ((), (), s32[]{:S(2)}) async-start(), calls=%async_computation.20 | async-start | bytes 1310720 | tf_op jit(solution)/shard_map/all_gather | solution.py:53
  362.3 89.8 %reduce-scatter.24.cloned.1.call-start = ((), (), s32[]{:S(2)}) async-start(), calls=%async_computation.21 | async-start | bytes 2621440 | tf_op jit(solution)/shard_map/reduce_scatter | solution.py:57
  454.4 77.1 %reduce-scatter.26.cloned.1.call-start = ((), (), s32[]{:S(2)}) async-start(), calls=%async_computation.23 | async-start | bytes 2621440 | tf_op jit(solution)/shard_map/reduce_scatter | solution.py:57
  488.4 76.2 %all-gather.18.cloned.1.call-start = ((), (), s32[]{:S(2)}) async-start(), calls=%async_computation.24 | async-start | bytes 1310720 | tf_op jit(solution)/shard_map/all_gather | solution.py:53
  537.3 76.8 %reduce-scatter.28.cloned.1.call-start = ((), (), s32[]{:S(2)}) async-start(), calls=%async_computation.25 | async-start | bytes 2621440 | tf_op jit(solution)/shard_map/reduce_scatter | solution.py:57
  570.9 75.1 %all-gather.20.cloned.1.call-start = ((), (), s32[]{:S(2)}) async-start(), calls=%async_computation.26 | async-start | bytes 1310720 | tf_op jit(solution)/shard_map/all_gather | solution.py:53
  618.6 93.8 %reduce-scatter.30.cloned.1.call-start = ((), (), s32[]{:S(2)}) async-start(), calls=%async_computation.27 | async-start | bytes 2621440 | tf_op jit(solution)/shard_map/reduce_scatter | solution.py:57
  670.5 73.3 %all-gather.22.cloned.1.call-start = ((), (), s32[]{:S(2)}) async-start(), calls=%async_computation.28 | async-start | bytes 1310720 | tf_op jit(solution)/shard_map/all_gather | solution.py:53
  716.5 288.6 %reduce-scatter.32.cloned.1.call-start = ((), (), s32[]{:S(2)}) async-start(), calls=%async_computation.29 | async-start | bytes 2621440 | tf_op jit(solution)/shard_map/reduce_scatter | solution.py:57
  961.9 73.9 %all-gather.24.cloned.1.call-start = ((), (), s32[]{:S(2)}) async-start(), calls=%async_computation.30 | async-start | bytes 1310720 | tf_op jit(solution)/shard_map/all_gather | solution.py:53
  1008.5 75.8 %reduce-scatter.34.cloned.1.call-start = ((), (), s32[]{:S(2)}) async-start(), calls=%async_computation.31 | async-start | bytes 2621440 | tf_op jit(solution)/shard_map/reduce_scatter | solution.py:57
  1041.1 100.6 %all-reduce.11.cloned.1.call-start = ((), (), s32[]{:S(2)}) async-start(), calls=%async_computation.40 | async-start | bytes 1048576
  1042.7 236.1 %reduce-scatter.50.cloned.1.call-start = ((), (), s32[]{:S(2)}) async-start(), calls=%async_computation.39 | async-start | bytes 270336
  1086.6 228.3 %reduce-scatter.46.cloned.1.call-start = ((), (), s32[]{:S(2)}) async-start(), calls=%async_computation.37 | async-start | bytes 1179648 | tf_op jit(solution)/shard_map/reduce_scatter | solution.py:502
  1090.0 264.5 %reduce-scatter.48.cloned.1.call-start = ((), (), s32[]{:S(2)}) async-start(), calls=%async_computation.38 | async-start | bytes 1179648 | tf_op jit(solution)/shard_map/reduce_scatter | solution.py:503
  1093.1 298.7 %reduce-scatter.44.cloned.1.call-start = ((), (), s32[]{:S(2)}) async-start(), calls=%async_computation.36 | async-start | bytes 294912 | tf_op jit(solution)/shard_map/reduce_scatter | solution.py:501
  1095.8 333.3 %reduce-scatter.42.cloned.1.call-start = ((), (), s32[]{:S(2)}) async-start(), calls=%async_computation.35 | async-start | bytes 294912 | tf_op jit(solution)/shard_map/reduce_scatter | solution.py:498
  1097.2 371.7 %reduce-scatter.40.cloned.1.call-start = ((), (), s32[]{:S(2)}) async-start(), calls=%async_computation.34 | async-start | bytes 1179648 | tf_op jit(solution)/shard_map/reduce_scatter | solution.py:497
  1104.6 403.9 %reduce-scatter.36.cloned.1.call-start = ((), (), s32[]{:S(2)}) async-start(), calls=%async_computation.32 | async-start | bytes 1179648 | tf_op jit(solution)/shard_map/reduce_scatter | solution.py:495
  1108.0 440.2 %reduce-scatter.38.cloned.1.call-start = ((), (), s32[]{:S(2)}) async-start(), calls=%async_computation.33 | async-start | bytes 1179648 | tf_op jit(solution)/shard_map/reduce_scatter | solution.py:496
  (134 other events, 3133.6 us)
Sparse Core Ops, SparseCore 0:
  113.5 43.0 reduce-scatter.19
  159.0 27.1 all-gather.11
  318.0 41.9 reduce-scatter.21
  362.4 27.1 all-gather.13
  410.3 41.7 reduce-scatter.23
  454.5 27.1 all-gather.15
  488.5 43.0 reduce-scatter.25
  537.4 27.1 all-gather.17
  571.0 43.0 reduce-scatter.27
  618.7 27.1 all-gather.19
  670.6 41.7 reduce-scatter.29
  716.6 27.1 all-gather.21
  962.0 43.0 reduce-scatter.31
  1008.6 27.1 all-gather.23
  1041.2 43.0 reduce-scatter.33
  1087.7 53.9 all-reduce.10
  1143.9 134.9 reduce-scatter.49
  1282.6 32.2 reduce-scatter.45
  1318.5 35.9 reduce-scatter.47
  1358.1 33.6 reduce-scatter.43
  1395.4 33.6 reduce-scatter.41
  1432.8 35.9 reduce-scatter.39
  1472.5 35.9 reduce-scatter.35
  1512.2 35.9 reduce-scatter.37
  (1 shorter events, 24.2 us)
where the time goes:
time: 1570 us; the launch traced here: 1560 us
  waiting for transfers between devices  873 us (56%)
  local copies, waits for them, and re-layouts  243 us (15%)
  blocking collectives  206 us (13%)
  matrix products  126 us (8%)
  other arithmetic  58.3 us (4%)
  loops' own time  30 us (2%)
  between operations  17.8 us (1%)
    reduce_scatter x8, waiting for transfers between devices, fold_rows(): lax.psum_scatter(lax.dot_general(source, weight, (((1,), (contract,)), ((...  340 us
    unnamed x27, waiting for transfers between devices  137 us
    all_gather x8, waiting for transfers between devices, spread_rows(): return lax.all_gather(row_block, 'tensor', axis=0, tiled=True)  129 us
    all_gather x1, blocking collectives, per_device(): gain_rows = lax.all_gather(norm_gains, ('dp', 'tensor'), axis=1, tiled=True)  70.9 us
    reshape x4, local copies, waits for them, and re-layouts, skew_rows(): trimmed.reshape(head_count, block_rows, full_width - 1)[:, :, :frames]  55.4 us
    reshape x4, local copies, waits for them, and re-layouts, skew_rows(): flattened = wide_scores.reshape(head_count, block_rows * full_width)  55 us
    slice x4, local copies, waits for them, and re-layouts, skew_rows(): lax.slice_in_dim(flattened, block_rows - 1, block_rows - 1 + block_rows *...  41 us
    reduce_scatter x1, waiting for transfers between devices, per_device(): lax.psum_scatter(grad_attend_in, 'dp', scatter_dimension=1, tiled=True)  39.8 us
  transfers between devices with their start and end apart: 25, of which 24 were waited for; matrix products, arithmetic and copies ran while one was open for 3% of the time, Pallas kernels for 0%

commit v1 on v0

v1 whole, which is shorter than its diff:
```python
import functools
import math

import jax
import jax.numpy as jnp
from jax import lax
from jax.experimental import pallas as pl
from jax.experimental.pallas import tpu as pltpu
from jax.sharding import PartitionSpec as P

MESH = pl.DeviceIdType.MESH
CHUNKS = 6
CORE = 1


def flip(index, mask):
    result = index
    bit = 1
    while bit <= mask:
        if mask & bit:
            result = result + bit - 2 * bit * ((index // bit) % 2)
        bit *= 2
    return result


def span(bits):
    masks = [0]
    for bit in bits:
        masks = masks + [mask ^ bit for mask in masks]
    return masks


def link_orders(n_dp):
    bits = [1 << k for k in range(1, n_dp.bit_length() - 1)]
    return (bits, bits[::-1])


def greet(peers):
    barrier = pltpu.get_barrier_semaphore()
    for peer in peers:
        pl.semaphore_signal(barrier, inc=1, device_id=peer, device_id_type=MESH)
    pl.semaphore_wait(barrier, len(peers))


def tensor_peers(d, t, n_t):
    return [(d, lax.rem(t + step, n_t)) for step in range(1, n_t)]


def remote(src, dst, send_sem, recv_sem, peer):
    return pltpu.make_async_remote_copy(
        src_ref=src, dst_ref=dst, send_sem=send_sem, recv_sem=recv_sem,
        device_id=peer, device_id_type=MESH)


def gather_body(n_dp, n_t, p_ref, e_ref, f_ref, g_ref, ge_ref, gf_ref, local_sem, z_send, z_recv, d_send, d_recv,
                fz_send, fz_recv):
    d = lax.axis_index("dp")
    t = lax.axis_index("tensor")
    rows, width = p_ref.shape[1], p_ref.shape[2]
    e_rows = e_ref.shape[0]
    half = n_t * width // 2
    orders = [order + [CORE] for order in link_orders(n_dp)]
    stages = len(orders[0])
    z_peers = tensor_peers(d, t, n_t)
    greet(z_peers + [(flip(d, bit), t) for bit in orders[0]])

    def block(c, mask, start, size):
        if c == CHUNKS:
            return ge_ref.at[:, pl.ds(pl.multiple_of(flip(d, mask) * e_rows, e_rows), e_rows), :]
        first = pl.multiple_of(flip(d, mask) * rows, rows)
        return g_ref.at[c, pl.ds(first, rows), pl.ds(start, size)]

    def own(c):
        if c == CHUNKS:
            return ge_ref.at[t, pl.ds(pl.multiple_of(d * e_rows, e_rows), e_rows), :]
        return block(c, 0, pl.multiple_of(t * width, width), width)

    def source(c):
        return e_ref if c == CHUNKS else p_ref.at[c]

    def z_copy(c, step):
        return remote(source(c), own(c), z_send.at[c, step], z_recv.at[c, step], z_peers[step])

    def f_copy(step):
        return remote(f_ref, gf_ref.at[t], fz_send.at[step], fz_recv.at[step], z_peers[step])

    def local_copy(c):
        return pltpu.make_async_copy(source(c), own(c), local_sem.at[c])

    def dp_copies(c, stage):
        copies = []
        for h in range(1 if c == CHUNKS else 2):
            bit = orders[h][stage]
            masks = span(orders[h][:stage])
            for j, mask in enumerate(masks):
                slot = len(masks) - 1 + j
                window = block(c, mask, h * half, half)
                copies.append(remote(window, window, d_send.at[c, h, slot], d_recv.at[c, h, slot], (flip(d, bit), t)))
        return copies

    everything = [CHUNKS] + list(range(CHUNKS))
    own_f = pltpu.make_async_copy(f_ref, gf_ref.at[t], local_sem.at[CHUNKS + 1])
    own_f.start()
    for c in everything:
        local_copy(c).start()
        for step in range(n_t - 1):
            z_copy(c, step).start()
        if c == CHUNKS:
            for step in range(n_t - 1):
                f_copy(step).start()
    for tick in range(len(everything) + stages):
        for stage in range(stages + 1):
            place = tick - stage
            if 0 <= place < len(everything):
                c = everything[place]
                if stage == 0:
                    local_copy(c).wait()
                    for step in range(n_t - 1):
                        z_copy(c, step).wait_recv()
                else:
                    for copy in dp_copies(c, stage - 1):
                        copy.wait_recv()
                if stage < stages:
                    for copy in dp_copies(c, stage):
                        copy.start()
    for step in range(n_t - 1):
        f_copy(step).wait()
    own_f.wait()
    for c in everything:
        for step in range(n_t - 1):
            z_copy(c, step).wait_send()
        for stage in range(stages):
            for copy in dp_copies(c, stage):
                copy.wait_send()


def gather_weights(n_dp, n_t, packed, small, taps):
    _, rows, width = packed.shape
    e_rows = small.shape[0]
    dma = pltpu.SemaphoreType.DMA
    vmem = pl.BlockSpec(memory_space=pltpu.VMEM)
    hbm = pl.BlockSpec(memory_space=pl.ANY)
    return pl.pallas_call(
        functools.partial(gather_body, n_dp, n_t),
        name="gather_weights",
        out_shape=(
            jax.ShapeDtypeStruct((CHUNKS, n_dp * rows, n_t * width), packed.dtype),
            jax.ShapeDtypeStruct((n_t, n_dp * e_rows, 128), jnp.float32),
            jax.ShapeDtypeStruct((n_t,) + taps.shape, jnp.float32)),
        in_specs=[vmem, vmem, vmem],
        out_specs=(hbm, hbm, hbm),
        scratch_shapes=[
            dma((CHUNKS + 2,)), dma((CHUNKS + 1, n_t - 1)), dma((CHUNKS + 1, n_t - 1)),
            dma((CHUNKS + 1, 2, n_dp - 1)), dma((CHUNKS + 1, 2, n_dp - 1)),
            dma((n_t - 1,)), dma((n_t - 1,))],
        compiler_params=pltpu.CompilerParams(collective_id=0, has_side_effects=True, vmem_limit_bytes=16 << 20),
    )(packed, small, taps)


def fold_body(n_dp, n_t, x_ref, s_ref, o_ref, so_ref, acc, core_buf, dp_buf, z_buf, small_acc, small_buf, small_z,
              local_sem, core_send, core_recv, d_send, d_recv, z_send, z_recv, s_send, s_recv, sz_send, sz_recv):
    d = lax.axis_index("dp")
    t = lax.axis_index("tensor")
    rows, width = o_ref.shape[1], o_ref.shape[2]
    half = n_t * width // 2
    orders = [order[::-1] for order in link_orders(n_dp)]
    stages = len(orders[0])
    z_peers = tensor_peers(d, t, n_t)
    all_bits = [CORE] + orders[0]
    greet(z_peers + [(flip(d, bit), t) for bit in all_bits])
    groups = span(link_orders(n_dp)[0])

    def x_block(c, mask):
        return x_ref.at[c, pl.ds(pl.multiple_of(flip(d, mask) * rows, rows), rows), :]

    def local_copy(c, k):
        return pltpu.make_async_copy(x_block(c, groups[k]), acc.at[c, k], local_sem.at[c, k])

    def core_copy(c, k):
        return remote(x_block(c, groups[k] ^ CORE), core_buf.at[c, k], core_send.at[c, k], core_recv.at[c, k],
                      (flip(d, CORE), t))

    def dp_moves(c, stage):
        moves = []
        for h in range(2):
            bit = orders[h][stage]
            masks = span(orders[h][stage + 1:])
            base = len(groups) - 2 * len(masks)
            for j, mask in enumerate(masks):
                slot = base + j
                cols = pl.ds(h * half, half)
                copy = remote(acc.at[c, groups.index(mask ^ bit), :, cols], dp_buf.at[c, h, slot],
                              d_send.at[c, h, slot], d_recv.at[c, h, slot], (flip(d, bit), t))
                moves.append((copy, groups.index(mask), cols, h, slot))
        return moves

    def z_copy(c, step):
        target = lax.rem(t + step + 1, n_t)
        return remote(acc.at[c, 0, :, pl.ds(pl.multiple_of(target * width, width), width)], z_buf.at[c, step],
                      z_send.at[c, step], z_recv.at[c, step], z_peers[step])

    def small_copy(k):
        return remote(small_acc.at[k], small_buf.at[k], s_send.at[k], s_recv.at[k], (flip(d, all_bits[k]), t))

    def small_z_copy(step):
        target = lax.rem(t + step + 1, n_t)
        return remote(small_acc.at[len(all_bits), target], small_z.at[step], sz_send.at[step], sz_recv.at[step],
                      z_peers[step])

    for c in range(CHUNKS):
        for k in range(len(groups)):
            core_copy(c, k).start()
            local_copy(c, k).start()
    small_acc[0] = s_ref[...]
    small_copy(0).start()
    for k in range(1, len(all_bits) + 1):
        small_copy(k - 1).wait_recv()
        small_acc[k] = small_acc[k - 1] + small_buf[k - 1]
        if k < len(all_bits):
            small_copy(k).start()
    for step in range(n_t - 1):
        small_z_copy(step).start()

    def start_stage(c, stage):
        if stage < stages:
            for move in dp_moves(c, stage):
                move[0].start()
        else:
            for step in range(n_t - 1):
                z_copy(c, step).start()

    for tick in range(CHUNKS + stages + 1):
        for stage in range(stages + 2):
            c = tick - stage
            if not 0 <= c < CHUNKS:
                continue
            if stage == 0:
                for k in range(len(groups)):
                    local_copy(c, k).wait()
                    core_copy(c, k).wait_recv()

                def add_core(step, carry, c=c):
                    k = step // 4
                    part = pl.ds(pl.multiple_of(lax.rem(step, 4) * (rows // 4), rows // 4), rows // 4)
                    acc[c, k, part, :] = (acc[c, k, part, :].astype(jnp.float32)
                                          + core_buf[c, k, part, :].astype(jnp.float32)).astype(jnp.bfloat16)
                    return carry
                lax.fori_loop(0, 4 * len(groups), add_core, 0)
                start_stage(c, 0)
            elif stage <= stages:
                for copy, k, cols, h, slot in dp_moves(c, stage - 1):
                    copy.wait_recv()

                    def add_dp(step, carry, c=c, k=k, cols=cols, h=h, slot=slot):
                        part = pl.ds(pl.multiple_of(step * (rows // 4), rows // 4), rows // 4)
                        acc[c, k, part, cols] = (acc[c, k, part, cols].astype(jnp.float32)
                                                 + dp_buf[c, h, slot, part, :].astype(jnp.float32)).astype(jnp.bfloat16)
                        return carry
                    lax.fori_loop(0, 4, add_dp, 0)
                start_stage(c, stage)
            else:
                for step in range(n_t - 1):
                    z_copy(c, step).wait_recv()
                total = acc[c, 0, :, pl.ds(pl.multiple_of(t * width, width), width)].astype(jnp.float32)
                for step in range(n_t - 1):
                    total = total + z_buf[c, step].astype(jnp.float32)
                o_ref[c] = total
    total = small_acc[len(all_bits), t]
    for step in range(n_t - 1):
        small_z_copy(step).wait_recv()
        total = total + small_z[step]
    so_ref[...] = total
    for k in range(len(all_bits)):
        small_copy(k).wait_send()
    for step in range(n_t - 1):
        small_z_copy(step).wait_send()
    for c in range(CHUNKS):
        for k in range(len(groups)):
            core_copy(c, k).wait_send()
        for stage in range(stages):
            for move in dp_moves(c, stage):
                move[0].wait_send()
        for step in range(n_t - 1):
            z_copy(c, step).wait_send()


def fold_weights(n_dp, n_t, partial, small):
    rows, width = partial.shape[1] // n_dp, partial.shape[2] // n_t
    groups = n_dp // 2
    n_bits = n_dp.bit_length() - 1
    dma = pltpu.SemaphoreType.DMA
    vmem = pl.BlockSpec(memory_space=pltpu.VMEM)
    hbm = pl.BlockSpec(memory_space=pl.ANY)
    bf16 = jnp.bfloat16
    return pl.pallas_call(
        functools.partial(fold_body, n_dp, n_t),
        name="fold_weights",
        out_shape=(jax.ShapeDtypeStruct((CHUNKS, rows, width), jnp.float32),
                   jax.ShapeDtypeStruct(small.shape[1:], jnp.float32)),
        in_specs=[hbm, vmem],
        out_specs=(vmem, vmem),
        scratch_shapes=[
            pltpu.VMEM((CHUNKS, groups, rows, n_t * width), bf16),
            pltpu.VMEM((CHUNKS, groups, rows, n_t * width), bf16),
            pltpu.VMEM((CHUNKS, 2, groups - 1, rows, n_t * width // 2), bf16),
            pltpu.VMEM((CHUNKS, n_t - 1, rows, width), bf16),
            pltpu.VMEM((n_bits + 1,) + small.shape, jnp.float32),
            pltpu.VMEM((n_bits,) + small.shape, jnp.float32),
            pltpu.VMEM((n_t - 1,) + small.shape[1:], jnp.float32),
            dma((CHUNKS, groups)), dma((CHUNKS, groups)), dma((CHUNKS, groups)),
            dma((CHUNKS, 2, groups - 1)), dma((CHUNKS, 2, groups - 1)),
            dma((CHUNKS, n_t - 1)), dma((CHUNKS, n_t - 1)),
            dma((n_bits,)), dma((n_bits,)), dma((n_t - 1,)), dma((n_t - 1,))],
        compiler_params=pltpu.CompilerParams(collective_id=1, has_side_effects=True, vmem_limit_bytes=48 << 20),
    )(partial, small)


def spread_body(n_t, x_ref, y_ref, local_sem, send, recv):
    d = lax.axis_index("dp")
    t = lax.axis_index("tensor")
    peers = tensor_peers(d, t, n_t)
    greet(peers)
    local = pltpu.make_async_copy(x_ref, y_ref.at[t], local_sem.at[0])
    local.start()
    copies = [remote(x_ref, y_ref.at[t], send.at[k], recv.at[k], peers[k]) for k in range(n_t - 1)]
    for copy in copies:
        copy.start()
    local.wait()
    for copy in copies:
        copy.wait()


def spread_frames(n_t, rows_block):
    dma = pltpu.SemaphoreType.DMA
    vmem = pl.BlockSpec(memory_space=pltpu.VMEM)
    hbm = pl.BlockSpec(memory_space=pl.ANY)
    return pl.pallas_call(
        functools.partial(spread_body, n_t),
        name="spread_frames",
        out_shape=jax.ShapeDtypeStruct((n_t,) + rows_block.shape, rows_block.dtype),
        in_specs=[vmem],
        out_specs=hbm,
        scratch_shapes=[dma((1,)), dma((n_t - 1,)), dma((n_t - 1,))],
        compiler_params=pltpu.CompilerParams(collective_id=2, has_side_effects=True),
    )(rows_block)


def reduce_frames_body(n_t, x_ref, o_ref, buf, send, recv):
    d = lax.axis_index("dp")
    t = lax.axis_index("tensor")
    peers = tensor_peers(d, t, n_t)
    greet(peers)
    copies = [remote(x_ref.at[lax.rem(t + k + 1, n_t)], buf.at[k], send.at[k], recv.at[k], peers[k])
              for k in range(n_t - 1)]
    for copy in copies:
        copy.start()
    for copy in copies:
        copy.wait_recv()
    rows = o_ref.shape[0]
    size = rows // 8

    def add_part(step, carry):
        part = pl.ds(pl.multiple_of(step * size, size), size)
        total = x_ref[t, part, :].astype(jnp.float32)
        for k in range(n_t - 1):
            total = total + buf[k, part, :].astype(jnp.float32)
        o_ref[part, :] = total
        return carry
    lax.fori_loop(0, 8, add_part, 0)
    for copy in copies:
        copy.wait_send()


def reduce_frames(n_t, partial):
    dma = pltpu.SemaphoreType.DMA
    vmem = pl.BlockSpec(memory_space=pltpu.VMEM)
    return pl.pallas_call(
        functools.partial(reduce_frames_body, n_t),
        name="reduce_frames",
        out_shape=jax.ShapeDtypeStruct(partial.shape[1:], jnp.float32),
        in_specs=[vmem],
        out_specs=vmem,
        scratch_shapes=[pltpu.VMEM((n_t - 1,) + partial.shape[1:], partial.dtype), dma((n_t - 1,)), dma((n_t - 1,))],
        compiler_params=pltpu.CompilerParams(collective_id=3, has_side_effects=True),
    )(partial)


EDGE = 16


def edge_pieces(n_t, source, edges, send, recv):
    d = lax.axis_index("dp")
    t = lax.axis_index("tensor")
    before = (d, lax.rem(t + n_t - 1, n_t))
    after = (d, lax.rem(t + 1, n_t))
    rows = source.shape[1]
    return [remote(source.at[:, pl.ds(0, EDGE), :], edges.at[1], send.at[0], recv.at[0], before),
            remote(source.at[:, pl.ds(rows - EDGE, EDGE), :], edges.at[0], send.at[1], recv.at[1], after)]


def edges_body(n_t, x_ref, e_ref, send, recv):
    d = lax.axis_index("dp")
    t = lax.axis_index("tensor")
    greet([(d, lax.rem(t + n_t - 1, n_t)), (d, lax.rem(t + 1, n_t))])
    copies = edge_pieces(n_t, x_ref, e_ref, send, recv)
    for copy in copies:
        copy.start()
    for copy in copies:
        copy.wait()


def swap_edges(n_t, x):
    dma = pltpu.SemaphoreType.DMA
    vmem = pl.BlockSpec(memory_space=pltpu.VMEM)
    return pl.pallas_call(
        functools.partial(edges_body, n_t),
        name="swap_edges",
        out_shape=jax.ShapeDtypeStruct((2, x.shape[0], EDGE, x.shape[2]), x.dtype),
        in_specs=[vmem],
        out_specs=vmem,
        scratch_shapes=[dma((2,)), dma((2,))],
        compiler_params=pltpu.CompilerParams(collective_id=4, has_side_effects=True),
    )(x)


def totals_body(n_dp, n_t, with_edges, *refs):
    if with_edges:
        s_ref, x_ref, o_ref, e_ref, mine, dp_buf, mid, z_buf, d_send, d_recv, z_send, z_recv, e_send, e_recv = refs
    else:
        s_ref, o_ref, mine, dp_buf, mid, z_buf, d_send, d_recv, z_send, z_recv = refs
    d = lax.axis_index("dp")
    t = lax.axis_index("tensor")
    z_peers = tensor_peers(d, t, n_t)
    d_peers = [(flip(d, mask), t) for mask in range(1, n_dp)]
    greet(z_peers + d_peers)
    if with_edges:
        edge_copies = edge_pieces(n_t, x_ref, e_ref, e_send, e_recv)
    d_copies = [remote(s_ref, dp_buf.at[k], d_send.at[k], d_recv.at[k], d_peers[k]) for k in range(n_dp - 1)]
    for copy in d_copies:
        copy.start()
    if with_edges:
        for copy in edge_copies:
            copy.start()
    total = s_ref[...]
    for k in range(n_dp - 1):
        d_copies[k].wait_recv()
        total = total + dp_buf[k]
    mid[...] = total
    z_copies = [remote(mid, z_buf.at[k], z_send.at[k], z_recv.at[k], z_peers[k]) for k in range(n_t - 1)]
    for copy in z_copies:
        copy.start()
    for k in range(n_t - 1):
        z_copies[k].wait_recv()
        total = total + z_buf[k]
    o_ref[...] = total
    for copy in d_copies + z_copies:
        copy.wait_send()
    if with_edges:
        for copy in edge_copies:
            copy.wait()


def whole_totals(n_dp, n_t, sums, collective_id, edge_rows=None):
    dma = pltpu.SemaphoreType.DMA
    vmem = pl.BlockSpec(memory_space=pltpu.VMEM)
    shape = jax.ShapeDtypeStruct(sums.shape, jnp.float32)
    scratch = [pltpu.VMEM(sums.shape, jnp.float32), pltpu.VMEM((n_dp - 1,) + sums.shape, jnp.float32),
               pltpu.VMEM(sums.shape, jnp.float32), pltpu.VMEM((n_t - 1,) + sums.shape, jnp.float32),
               dma((n_dp - 1,)), dma((n_dp - 1,)), dma((n_t - 1,)), dma((n_t - 1,))]
    args = [sums]
    outs = [shape]
    if edge_rows is not None:
        args.append(edge_rows)
        outs.append(jax.ShapeDtypeStruct((2, edge_rows.shape[0], EDGE, edge_rows.shape[2]), jnp.float32))
        scratch += [dma((2,)), dma((2,))]
    return pl.pallas_call(
        functools.partial(totals_body, n_dp, n_t, edge_rows is not None),
        name="whole_totals",
        out_shape=tuple(outs),
        in_specs=[vmem] * len(args),
        out_specs=tuple([vmem] * len(outs)),
        scratch_shapes=scratch,
        compiler_params=pltpu.CompilerParams(collective_id=collective_id, has_side_effects=True),
    )(*args)


KERNEL = 31
HALF = KERNEL // 2
norm_eps = 1e-05
f32 = jnp.float32
bf16 = jnp.bfloat16


def norm_rows(values):
    centred = values - jnp.mean(values, axis=-1, keepdims=True)
    inverse = lax.rsqrt(jnp.mean(centred * centred, axis=-1, keepdims=True) + norm_eps)
    return centred * inverse, inverse


def norm_back(incoming, gain_row, saved):
    scaled, inverse = saved
    grad_scaled = incoming * gain_row
    inner = jnp.mean(grad_scaled * scaled, axis=-1, keepdims=True)
    grad_in = inverse * (grad_scaled - jnp.mean(grad_scaled, axis=-1, keepdims=True) - scaled * inner)
    return grad_in, jnp.sum(incoming * scaled, axis=0)


def swish_grad(pre_act):
    sigmoid_val = jax.nn.sigmoid(pre_act)
    return sigmoid_val * (1.0 + pre_act * (1.0 - sigmoid_val))


def dot(left, right, left_dim, right_dim):
    return lax.dot_general(left, right, (((left_dim,), (right_dim,)), ((), ())), preferred_element_type=f32)


def feed_forward(residual, gain_row, up, down_t):
    saved = norm_rows(residual)
    normed = (saved[0] * gain_row).astype(bf16)
    pre_act = dot(normed, up, 1, 0)
    hidden = (pre_act * jax.nn.sigmoid(pre_act)).astype(bf16)
    return residual + 0.5 * dot(hidden, down_t, 1, 1), (saved, normed, pre_act, hidden)


def feed_backward(incoming, gain_row, up, down_t, stored):
    saved, normed, pre_act, hidden = stored
    grad_branch = (0.5 * incoming).astype(bf16)
    grad_down_t = dot(grad_branch, hidden, 0, 0)
    grad_pre = (dot(grad_branch, down_t, 1, 0) * swish_grad(pre_act)).astype(bf16)
    grad_up = dot(normed, grad_pre, 0, 0)
    grad_resid, gain_grad = norm_back(dot(grad_pre, up, 1, 1), gain_row, saved)
    return incoming + grad_resid, gain_grad, grad_up, grad_down_t


def angle_tables(frames, width):
    step = 32
    frequency = jnp.exp(jnp.arange(width // 2, dtype=f32) * (-2.0 * math.log(10000.0) / width))
    coarse = (jnp.arange(frames // step, dtype=f32) * step)[:, None] * frequency
    fine = jnp.arange(step, dtype=f32)[:, None] * frequency
    cs, cc = jnp.sin(coarse)[:, None], jnp.cos(coarse)[:, None]
    fs, fc = jnp.sin(fine)[None], jnp.cos(fine)[None]
    sines = (cs * fc + cc * fs).reshape(frames, width // 2)
    cosines = (cc * fc - cs * fs).reshape(frames, width // 2)
    return sines, cosines


def shifted(whole, taps, rows, reverse):
    total = None
    for tap in range(KERNEL):
        first = EDGE - HALF + (KERNEL - 1 - tap if reverse else tap)
        term = taps[tap] * whole[first:first + rows]
        total = term if total is None else total + term
    return total


def with_edges(block, edges, t, n_t):
    before = jnp.where(t > 0, edges[0], 0.0)
    after = jnp.where(t < n_t - 1, edges[1], 0.0)
    return jnp.concatenate([before, block, after], axis=0)


def per_device(n_dp, n_t, inputs, out_grad, norm_gains, first_up, first_down, attend_in, attend_out, position_bias,
               convolve_in, depth_kernel, batch_norm, convolve_out, second_up, second_down):
    d = lax.axis_index("dp")
    t = lax.axis_index("tensor")
    rows, D = inputs.shape
    w = attend_in.shape[2]
    R = attend_in.shape[1]
    F = first_up.shape[1]
    head_dim = position_bias.shape[2] * n_dp
    heads = D // head_dim
    local_heads = position_bias.shape[1]
    frames = rows * n_t
    n_gain = norm_gains.shape[1]
    n_bias = position_bias.shape[2]

    packed = jnp.stack([
        first_up, first_down.T, attend_in.transpose(1, 0, 2).reshape(R, 4 * w),
        jnp.concatenate([convolve_in.reshape(R, 2 * w), attend_out.T, convolve_out.T], axis=1),
        second_up, second_down.T])
    small = jnp.zeros((16, 128), f32)
    small = small.at[:n_gain, :5].set(norm_gains.T)
    small = small.at[:n_bias, 8:8 + 2 * local_heads].set(position_bias.astype(f32).reshape(2 * local_heads, n_bias).T)
    taps = jnp.concatenate([depth_kernel.T, batch_norm, jnp.zeros((7, w), f32)], axis=0)
    weights, small_all, taps_all = gather_weights(n_dp, n_t, packed, small, taps)
    small_all = small_all.reshape(n_t, n_dp, 16, 128)
    gains = small_all[:, :, :n_gain, :5].transpose(3, 1, 0, 2).reshape(5, D)
    bias = small_all[:, :, :n_bias, 8:8 + 2 * local_heads].reshape(n_t, n_dp, n_bias, 2, local_heads)
    bias = bias.transpose(3, 0, 4, 1, 2).reshape(2, D)
    taps_all = taps_all.transpose(1, 0, 2).reshape(40, D)
    tap_rows = taps_all[:KERNEL]
    bn_gain, bn_shift = taps_all[KERNEL], taps_all[KERNEL + 1]
    attend_w = weights[2].reshape(D, n_t, 4, w).transpose(2, 0, 1, 3).reshape(4, D, D)
    mixed_w = weights[3].reshape(D, n_t, 4, w).transpose(2, 0, 1, 3).reshape(4, D, D)

    x0 = inputs.astype(f32)
    x1, stored_one = feed_forward(x0, gains[0], weights[0], weights[1])

    saved_two = norm_rows(x1)
    a2 = (saved_two[0] * gains[1]).astype(bf16)
    a2_all = spread_frames(n_t, a2).reshape(frames, D)
    q = dot(a2, attend_w[0], 1, 0)
    content_q = (q + bias[0]).astype(bf16).reshape(rows, heads, head_dim)
    position_q = (q + bias[1]).astype(bf16).reshape(rows, heads, head_dim)
    keys = dot(a2_all, attend_w[1], 1, 0).astype(bf16).reshape(frames, heads, head_dim)
    values = dot(a2_all, attend_w[2], 1, 0).astype(bf16).reshape(frames, heads, head_dim)
    sines, cosines = angle_tables(frames, D)
    phases = jnp.concatenate([sines, cosines], axis=1).astype(bf16)
    own_sin = lax.dynamic_slice_in_dim(sines, t * rows, rows, 0)
    own_cos = lax.dynamic_slice_in_dim(cosines, t * rows, rows, 0)
    pos_w = attend_w[3].reshape(D, heads, head_dim)
    scale = head_dim ** -0.5
    turned = jnp.einsum("rhe,che->hrc", position_q, pos_w, preferred_element_type=f32)
    rs, rc = turned[..., :D // 2], turned[..., D // 2:]
    turned = jnp.concatenate([rc * own_sin - rs * own_cos, rs * own_sin + rc * own_cos], axis=-1).astype(bf16)
    scores = (jnp.einsum("rhe,fhe->hrf", content_q, keys, preferred_element_type=f32)
              + jnp.einsum("hrc,fc->hrf", turned, phases, preferred_element_type=f32)) * scale
    exponent = jnp.exp(scores - jnp.max(scores, axis=-1, keepdims=True))
    softmax_w = (exponent / jnp.sum(exponent, axis=-1, keepdims=True)).astype(bf16)
    mixture = jnp.einsum("hrf,fhe->rhe", softmax_w, values, preferred_element_type=f32).astype(bf16).reshape(rows, D)
    x2 = x1 + dot(mixture, mixed_w[2], 1, 1)

    saved_three = norm_rows(x2)
    a3 = (saved_three[0] * gains[2]).astype(bf16)
    value_half = dot(a3, mixed_w[0], 1, 0)
    sigmoid_gate = jax.nn.sigmoid(dot(a3, mixed_w[1], 1, 0))
    gated = value_half * sigmoid_gate
    edges = swap_edges(n_t, gated[None])
    gated_all = with_edges(gated, edges[:, 0], t, n_t)
    convolved = shifted(gated_all, tap_rows, rows, False)
    row_count = frames * n_dp
    sums = jnp.concatenate([jnp.stack([jnp.sum(convolved, axis=0), jnp.sum(convolved * convolved, axis=0)]),
                            jnp.zeros((6, D), f32)])
    sums, = whole_totals(n_dp, n_t, sums, 5)
    batch_mean = sums[0] / row_count
    inverse = lax.rsqrt(sums[1] / row_count - batch_mean * batch_mean + norm_eps)
    scaled = (convolved - batch_mean) * inverse
    normal_out = scaled * bn_gain + bn_shift
    activated = (normal_out * jax.nn.sigmoid(normal_out)).astype(bf16)
    x3 = x2 + dot(activated, mixed_w[3], 1, 1)

    x4, stored_four = feed_forward(x3, gains[3], weights[4], weights[5])
    saved_five = norm_rows(x4)
    output_rows = saved_five[0] * gains[4]

    dx4, gain_four = norm_back(out_grad.astype(f32), gains[4], saved_five)
    dx3, gain_three, grad_second_up, grad_second_down = feed_backward(dx4, gains[3], weights[4], weights[5],
                                                                      stored_four)
    dz3 = dx3.astype(bf16)
    grad_convolve_out = dot(dz3, activated, 0, 0)
    dbn = dot(dz3, mixed_w[3], 1, 0) * swish_grad(normal_out)
    sums = jnp.concatenate([jnp.stack([jnp.sum(dbn * scaled, axis=0), jnp.sum(dbn, axis=0)]), jnp.zeros((6, D), f32)])
    sums, edges = whole_totals(n_dp, n_t, sums, 6, jnp.stack([dbn, scaled]))
    grad_bn = sums[:2]
    norm_scale = bn_gain * inverse

    def conv_grad(dbn_rows, scaled_rows):
        return norm_scale * (dbn_rows - grad_bn[1] / row_count - scaled_rows * (grad_bn[0] / row_count))
    dcv = conv_grad(dbn, scaled)
    dcv_all = with_edges(dcv, conv_grad(edges[:, 0], edges[:, 1]), t, n_t)
    first = EDGE - HALF
    grad_taps = jnp.stack([jnp.sum(dcv * gated_all[first + tap:first + tap + rows], axis=0) for tap in range(KERNEL)])
    dglu = shifted(dcv_all, tap_rows, rows, True)
    de_value = (dglu * sigmoid_gate).astype(bf16)
    de_gate = (dglu * value_half * sigmoid_gate * (1.0 - sigmoid_gate)).astype(bf16)
    grad_value = dot(a3, de_value, 0, 0)
    grad_gate = dot(a3, de_gate, 0, 0)
    grad_normed = dot(de_value, mixed_w[0], 1, 1) + dot(de_gate, mixed_w[1], 1, 1)
    grad_resid, gain_two = norm_back(grad_normed, gains[2], saved_three)
    dx2 = dx3 + grad_resid

    dz2 = dx2.astype(bf16)
    grad_attend_out = dot(dz2, mixture, 0, 0)
    dmix = dot(dz2, mixed_w[2], 1, 0).astype(bf16).reshape(rows, heads, head_dim)
    dpl = jnp.einsum("rhe,fhe->hrf", dmix, values, preferred_element_type=f32)
    p = softmax_w.astype(f32)
    ds = (p * (dpl - jnp.sum(dpl * p, axis=-1, keepdims=True))).astype(bf16)
    dvalues = jnp.einsum("hrf,rhe->fhe", softmax_w, dmix, preferred_element_type=f32).astype(bf16).reshape(frames, D)
    dkeys = (jnp.einsum("hrf,rhe->fhe", ds, content_q, preferred_element_type=f32) * scale).astype(bf16)
    dkeys = dkeys.reshape(frames, D)
    dcq = jnp.einsum("hrf,fhe->rhe", ds, keys, preferred_element_type=f32).reshape(rows, D) * scale
    turned = jnp.einsum("hrf,fc->hrc", ds, phases, preferred_element_type=f32)
    ts, tc = turned[..., :D // 2], turned[..., D // 2:]
    turned = jnp.concatenate([tc * own_sin - ts * own_cos, ts * own_sin + tc * own_cos], axis=-1).astype(bf16)
    dpq = jnp.einsum("hrc,che->rhe", turned, pos_w, preferred_element_type=f32).reshape(rows, D) * scale
    grad_pos = (jnp.einsum("hrc,rhe->che", turned, position_q, preferred_element_type=f32) * scale).reshape(D, D)
    dq = (dcq + dpq).astype(bf16)
    grad_attend = jnp.stack([dot(a2, dq, 0, 0), dot(a2_all, dkeys, 0, 0), dot(a2_all, dvalues, 0, 0), grad_pos])
    part = dot(dkeys, attend_w[1], 1, 1) + dot(dvalues, attend_w[2], 1, 1)
    part = reduce_frames(n_t, part.astype(bf16).reshape(n_t, rows, D))
    grad_resid, gain_one = norm_back(part + dot(dq, attend_w[0], 1, 1), gains[1], saved_two)
    dx1 = dx2 + grad_resid
    dx0, gain_zero, grad_first_up, grad_first_down = feed_backward(dx1, gains[0], weights[0], weights[1], stored_one)

    def by_tensor(stacked):
        return stacked.reshape(4, D, n_t, w).transpose(1, 2, 0, 3).reshape(D, 4 * D)
    grads = jnp.stack([
        grad_first_up, grad_first_down, by_tensor(grad_attend),
        by_tensor(jnp.stack([grad_value, grad_gate, grad_attend_out, grad_convolve_out])),
        grad_second_up, grad_second_down]).astype(bf16)
    gain_rows = jnp.stack([gain_zero, gain_one, gain_two, gain_three, gain_four])
    gain_rows = gain_rows.reshape(5, n_dp, n_t, n_gain).transpose(2, 0, 1, 3).reshape(n_t, 5, w)
    wide_rows = jnp.concatenate([grad_taps, jnp.sum(dcq, axis=0)[None], jnp.sum(dpq, axis=0)[None],
                                 jnp.zeros((2, D), f32)])
    wide_rows = wide_rows.reshape(35, n_t, w).transpose(1, 0, 2)
    small = jnp.concatenate([wide_rows, gain_rows], axis=1)
    shards, small = fold_weights(n_dp, n_t, grads, small)
    grad_gains = lax.dynamic_slice_in_dim(small[35:], d * n_gain, n_gain, 1)
    grad_bias = small[KERNEL:KERNEL + 2].reshape(2, local_heads, head_dim)
    grad_bias = lax.dynamic_slice_in_dim(grad_bias, d * n_bias, n_bias, 2)
    return (
        output_rows, dx0, grad_gains,
        shards[0], shards[1].T, shards[2].reshape(R, 4, w).transpose(1, 0, 2), shards[3][:, 2 * w:3 * w].T, grad_bias,
        shards[3][:, :2 * w].reshape(R, 2, w), small[:KERNEL].T, lax.dynamic_slice_in_dim(grad_bn, t * w, w, 1),
        shards[3][:, 3 * w:].T, shards[4], shards[5].T)


def solution(mesh):
    n_dp, n_t = mesh.shape["dp"], mesh.shape["tensor"]
    row = P(("dp", "tensor"), None)
    gain = P(None, ("dp", "tensor"))
    up = P("dp", "tensor")
    down = P("tensor", "dp")
    weights = (up, down, P(None, "dp", "tensor"), down, P(None, "tensor", "dp"), P("dp", None, "tensor"),
               P("tensor", None), P(None, "tensor"), down, up, down)
    return jax.shard_map(
        functools.partial(per_device, n_dp, n_t), mesh=mesh,
        in_specs=(row, row, gain) + weights,
        out_specs=(row, row, gain) + weights,
        check_vma=False)
```

time: 1570 us -> 480 us (0.31)
  waiting for transfers between devices: 873 us -> 0 us
  Pallas kernels: 0 us -> 246 us
  blocking collectives: 206 us -> 0 us
  local copies, waits for them, and re-layouts: 243 us -> 80.3 us
  matrix products: 126 us -> 89 us
  loops' own time: 30 us -> 0 us
    reduce_scatter x15 -> x0, waiting for transfers between devices: 608 us -> none  [the longest x8 340 us: fold_rows(): lax.psum_scatter(lax.dot_general(source, weight, (((1,), (contract,)), ((...]
    pallas_call x0 -> x7, Pallas kernels: none -> 246 us  [the longest x1 86.8 us: fold_weights(): pl.pallas_call(functools.partial(fold_body, n_dp, n_t), name='fold_weight...]
    all_gather x10 -> x0, blocking collectives: 156 us -> none  [the longest x1 70.9 us: per_device(): gain_rows = lax.all_gather(norm_gains, ('dp', 'tensor'), axis=1, tiled=True)]
    unnamed x27 -> x0, waiting for transfers between devices: 137 us -> none
    reshape x14 -> x4, local copies, waits for them, and re-layouts: 134 us -> 0.84 us  [the longest x1 0.66 us: per_device(): shards[3][:, :2 * w].reshape(R, 2, w)]
    all_gather x8 -> x0, waiting for transfers between devices: 129 us -> none  [spread_rows(): return lax.all_gather(row_block, 'tensor', axis=0, tiled=True)]
    dot_general x47 -> x43, matrix products: 124 us -> 79.4 us  [the longest x33 59.6 us: dot(): lax.dot_general(left, right, (((left_dim,), (right_dim,)), ((), ())), pre...]
    slice x11 -> x12, local copies, waits for them, and re-layouts: 42.2 us -> 8.72 us  [the longest x1 4.12 us: per_device(): weights[3].reshape(D, n_t, 4, w).transpose(2, 0, 1, 3).reshape(4, D, D)]
  transfers between devices with their start and end apart: 25 -> 0, of which waited for: 24 -> 0; matrix products, arithmetic and copies ran while one was open for 3% -> 0% of each run, Pallas kernels for 0% -> 0%
where the time goes in v1:
time: 480 us; the launch traced here: 471 us
  Pallas kernels  246 us (51%)
  matrix products  89 us (19%)
  local copies, waits for them, and re-layouts  80.3 us (17%)
  other arithmetic  52.3 us (11%)
    pallas_call x1, Pallas kernels, fold_weights(): pl.pallas_call(functools.partial(fold_body, n_dp, n_t), name='fold_weight...  86.8 us
    pallas_call x1, Pallas kernels, gather_weights(): pl.pallas_call(functools.partial(gather_body, n_dp, n_t), name='gather_we...  76.6 us
    dot_general x33, matrix products, dot(): lax.dot_general(left, right, (((left_dim,), (right_dim,)), ((), ())), pre...  59.6 us
    pallas_call x1, Pallas kernels, spread_frames(): pl.pallas_call(functools.partial(spread_body, n_t), name='spread_frames',...  25.8 us
    pallas_call x2, Pallas kernels, whole_totals(): pl.pallas_call(functools.partial(totals_body, n_dp, n_t, edge_rows is not...  23.4 us
    pallas_call x1, Pallas kernels, reduce_frames(): pl.pallas_call(functools.partial(reduce_frames_body, n_t), name='reduce_f...  23.1 us
    unnamed x426, local copies, waits for them, and re-layouts  21.5 us
    reduce_sum x1, other arithmetic, per_device(): jnp.sum(convolved, axis=0)  11.3 us

profile of v1, /device:TPU:0, one launch (start us, length us, event | category | flops | bytes accessed | tf_op | source)
XLA Modules:
  0.0 471.4 jit_solution(6249075332291011391)
XLA Ops:
  20.8 76.6 %gather_weights.1 = (bf16[6,512,2048]{2,1,0:T(8,128)(2,1)S(1)}, f32[4,128,128]{2,1,0:T(8,128)S(1)}, f32[4,40,128]{2,1,0:T(8,128)S(1)}) custom-call(bf16[6,64,512]{2,1,0:T(8,128)(2,1)S(1)} %bitcast_dynamic-update-slice_fusion.p_ref, f32[16,128]{1,0:T(8,128)S(1)} %scatter.9.e_ref, f32[40,128]{1,0:T(8,128)S(1)} %maximum_maximum_fusion.f_ref), custom_call_target="tpu_custom_call" | custom-call | tf_op jit(solution)/shard_map/gather_weights/pallas_call | solution.py:143
  97.4 4.6 copy-done
  108.2 3.2 fusion.237
  112.5 25.8 %spread_frames.1 = bf16[4,256,512]{2,1,0:T(8,128)(2,1)} custom-call(bf16[256,512]{1,0:T(8,128)(2,1)} %multiply_convert_fusion.11.x_ref), custom_call_target="tpu_custom_call" | custom-call | tf_op jit(solution)/shard_map/spread_frames/pallas_call | solution.py:337
  138.3 4.1 fusion.229
  149.3 4.6 reshape_squeeze.12
  168.2 5.7 %fusion.13 = f32[8,256,1024]{2,1,0:T(8,128)} fusion(bf16[8,256,256]{2,1,0:T(8,128)(2,1)S(1)} %get-tuple-element.113, bf16[8,256,256]{2,1,0:T(8,128)(2,1)S(1)} %get-tuple-element.112, bf16[1024,256]{1,0:T(8,128)(2,1)S(1)} %copy-done.57, bf16[1024,256]{1,0:T(8,128)(2,1)S(1)} %copy-done.59), kind=kOutput, calls=%fused_computation.80 | convolution fusion | flops 2153775104 | bytes 11534336 | tf_op jit(solution)/shard_map/hrc,fc->hrf/dot_general | solution.py:617
  173.9 9.6 %fusion.238 = (f32[8,256]{1,0:T(8,128)S(1)}, f32[8,256,1024]{2,1,0:T(8,128)}) fusion(f32[8,256,1024]{2,1,0:T(8,128)} %fusion.13, bf16[256,8,64]{0,2,1:T(8,128)(2,1)} %bitcast.399, bf16[1024,8,64]{0,2,1:T(8,128)(2,1)S(1)} %bitcast.390), kind=kOutput, calls=%fused_computation.508 | convolution fusion | flops 276825088 | bytes 18096128 | tf_op jit(solution)/shard_map/sub | solution.py:618
  183.6 4.0 divide_convert_fusion
  193.8 10.3 %swap_edges.1 = f32[2,1,16,512]{3,2,1,0:T(8,128)} custom-call(f32[1,256,512]{2,1,0:T(8,128)} %bitcast.378), custom_call_target="tpu_custom_call" | custom-call | tf_op jit(solution)/shard_map/swap_edges/pallas_call | solution.py:415
  205.2 11.3 %fusion.227 = (f32[512]{0:T(512)S(1)}, f32[512]{0:T(512)S(1)}, f32[256,512]{1,0:T(8,128)S(1)}) fusion(f32[16,512]{1,0:T(8,128)S(1)} %get-tuple-element.181, f32[256,512]{1,0:T(8,128)} %get-tuple-element.199, f32[512]{0:T(512)S(1)} %bitcast.469, f32[512]{0:T(512)S(1)} %bitcast.471, f32[512]{0:T(512)S(1)} %bitcast.473, f32[512]{0:T(512)S(1)} %bitcast.475, ...), kind=kLoop, calls=%fused_computation.498 | loop fusion | flops 12319744 | bytes 1181696 | tf_op jit(solution)/shard_map/reduce_sum | solution.py:632
  217.2 11.8 %whole_totals.2 = f32[8,512]{1,0:T(8,128)} custom-call(f32[8,512]{1,0:T(8,128)} %maximum_maximum_fusion.1.refs_0_), custom_call_target="tpu_custom_call" | custom-call | tf_op jit(solution)/shard_map/whole_totals/pallas_call | solution.py:476
  233.6 3.2 fusion.242
  238.1 3.4 fusion.11
  241.5 3.6 multiply_reduce_fusion
  252.9 11.6 %whole_totals.3 = (f32[8,512]{1,0:T(8,128)}, f32[2,2,16,512]{3,2,1,0:T(8,128)}) custom-call(f32[8,512]{1,0:T(8,128)} %maximum_maximum_fusion.2.refs_0_, f32[2,256,512]{2,1,0:T(8,128)} %pad_maximum_fusion.5.refs_1_), custom_call_target="tpu_custom_call" | custom-call | tf_op jit(solution)/shard_map/whole_totals/pallas_call | solution.py:476
  284.3 4.5 copy.56
  288.8 4.5 stack_reshape.14
  317.4 4.5 copy.55
  322.2 4.5 stack_reshape.13
  332.3 23.1 %reduce_frames.1 = f32[256,512]{1,0:T(8,128)} custom-call(bf16[4,256,512]{2,1,0:T(8,128)(2,1)} %bitcast.396), custom_call_target="tpu_custom_call" | custom-call | tf_op jit(solution)/shard_map/reduce_frames/pallas_call | solution.py:377
  357.4 3.3 fusion.12
  365.0 3.6 fusion.4
  379.6 86.8 %fold_weights.1 = (f32[6,64,512]{2,1,0:T(8,128)S(1)}, f32[40,128]{1,0:T(8,128)S(1)}) custom-call(bf16[6,512,2048]{2,1,0:T(8,128)(2,1)} %fusion.10.x_ref, f32[4,40,128]{2,1,0:T(8,128)S(1)} %pad_maximum_fusion.10.s_ref), custom_call_target="tpu_custom_call" | custom-call | tf_op jit(solution)/shard_map/fold_weights/pallas_call | solution.py:295
  (587 shorter events, 139.3 us)
Async XLA Ops:
  3.1 102.7 %copy-start.155 = (f32[256]{0:T(256)}, f32[256]{0:T(256)S(1)}, u32[]{:S(2)}) copy-start(f32[256]{0:T(256)S(1)} %broadcast_multiply_fusion.14) | copy-start | bytes 3076
  4.2 101.5 %copy-start.161 = (f32[256]{0:T(256)}, f32[256]{0:T(256)S(1)}, u32[]{:S(2)}) copy-start(f32[256]{0:T(256)S(1)} %add_rsqrt_fusion.5) | copy-start | bytes 3076
  19.7 86.0 %copy-start.21 = (bf16[256,512]{1,0:T(8,128)(2,1)S(1)}, bf16[256,512]{1,0:T(8,128)(2,1)}, u32[]{:S(2)}) copy-start(bf16[256,512]{1,0:T(8,128)(2,1)} %param.18) | copy-start | bytes 786436
  105.1 85.2 %copy-start.71 = (f32[512]{0:T(512)}, f32[512]{0:T(512)S(1)}, u32[]{:S(2)}) copy-start(f32[512]{0:T(512)S(1)} %mul.1309) | copy-start | bytes 6148
  111.4 26.9 %copy-start.77 = (f32[256]{0:T(256)}, f32[256]{0:T(256)S(1)}, u32[]{:S(2)}) copy-start(f32[256]{0:T(256)S(1)} %broadcast_multiply_fusion.13) | copy-start | bytes 3076
  111.6 26.7 %copy-start.151 = (f32[256]{0:T(256)}, f32[256]{0:T(256)S(1)}, u32[]{:S(2)}) copy-start(f32[256]{0:T(256)S(1)} %add_rsqrt_fusion.4) | copy-start | bytes 3076
  149.3 40.3 %copy-start.7 = (bf16[1,512,4,128]{1,3,2,0:T(8,128)(2,1)}, bf16[1,512,4,128]{1,3,2,0:T(8,128)(2,1)S(1)}, u32[]{:S(2)}) copy-start(bf16[1,512,4,128]{1,3,2,0:T(8,128)(2,1)S(1)} %get-tuple-element.117) | copy-start | bytes 1572868
  165.6 22.0 %copy-start.18 = (bf16[1024,512]{0,1:T(8,128)(2,1)}, bf16[1024,512]{0,1:T(8,128)(2,1)S(1)}, u32[]{:S(2)}) copy-start(bf16[1024,512]{0,1:T(8,128)(2,1)S(1)} %convolution_convert_fusion.6) | copy-start | bytes 3145732
  192.0 12.8 %copy-start.93 = (f32[1,4,128]{2,0,1:T(1,128)S(1)}, f32[1,4,128]{2,0,1:T(1,128)}, u32[]{:S(2)}) copy-start(f32[1,4,128]{2,0,1:T(1,128)} %get-tuple-element.167) | copy-start | bytes 6148
  192.1 12.8 %copy-start.95 = (f32[1,4,128]{2,0,1:T(1,128)S(1)}, f32[1,4,128]{2,0,1:T(1,128)}, u32[]{:S(2)}) copy-start(f32[1,4,128]{2,0,1:T(1,128)} %get-tuple-element.168) | copy-start | bytes 6148
  192.1 12.8 %copy-start.97 = (f32[1,4,128]{2,0,1:T(1,128)S(1)}, f32[1,4,128]{2,0,1:T(1,128)}, u32[]{:S(2)}) copy-start(f32[1,4,128]{2,0,1:T(1,128)} %get-tuple-element.169) | copy-start | bytes 6148
  192.3 24.2 %copy-start.201 = (f32[8]{0:T(128)S(1)}, f32[8]{0:T(128)}, u32[]{:S(2)}) copy-start(f32[8]{0:T(128)} %pad.30.clone) | copy-start | bytes 100
  192.3 38.1 %copy-start.183 = (f32[1,4,128]{2,0,1:T(1,128)S(1)}, f32[1,4,128]{2,0,1:T(1,128)}, u32[]{:S(2)}) copy-start(f32[1,4,128]{2,0,1:T(1,128)} %get-tuple-element.145) | copy-start | bytes 6148
  192.4 38.1 %copy-start.62 = (bf16[1,512,4,128]{1,3,2,0:T(8,128)(2,1)S(1)}, bf16[1,512,4,128]{1,3,2,0:T(8,128)(2,1)}, u32[]{:S(2)}) copy-start(bf16[1,512,4,128]{1,3,2,0:T(8,128)(2,1)} %get-tuple-element.115) | copy-start | bytes 1572868
  192.4 38.1 %copy-start.199 = (f32[1,4,128]{2,0,1:T(1,128)S(1)}, f32[1,4,128]{2,0,1:T(1,128)}, u32[]{:S(2)}) copy-start(f32[1,4,128]{2,0,1:T(1,128)} %get-tuple-element.146) | copy-start | bytes 6148
  230.9 14.9 %copy-start.81 = (f32[256]{0:T(256)}, f32[256]{0:T(256)S(1)}, u32[]{:S(2)}) copy-start(f32[256]{0:T(256)S(1)} %broadcast_multiply_fusion.11) | copy-start | bytes 3076
  231.2 14.7 %copy-start.159 = (f32[256]{0:T(256)}, f32[256]{0:T(256)S(1)}, u32[]{:S(2)}) copy-start(f32[256]{0:T(256)S(1)} %add_rsqrt_fusion.2) | copy-start | bytes 3076
  251.0 15.5 %copy-start.3 = (f32[256,512]{1,0:T(8,128)S(1)}, f32[256,512]{1,0:T(8,128)}, u32[]{:S(2)}) copy-start(f32[256,512]{1,0:T(8,128)} %get-tuple-element.199) | copy-start | bytes 1572868
  251.0 15.5 %copy-start.194 = (f32[1,512]{1,0:T(1,128)S(1)}, f32[1,512]{1,0:T(1,128)}, u32[]{:S(2)}) copy-start(f32[1,512]{1,0:T(1,128)} %get-tuple-element.105) | copy-start | bytes 6148
  329.3 26.2 %copy-start.12 = (bf16[1,512,4,128]{1,3,2,0:T(8,128)(2,1)S(1)}, bf16[1,512,4,128]{1,3,2,0:T(8,128)(2,1)}, u32[]{:S(2)}) copy-start(bf16[1,512,4,128]{1,3,2,0:T(8,128)(2,1)} %copy-done.11) | copy-start | bytes 1572868
  329.3 26.2 %copy-start.63 = (bf16[256,8,64]{0,2,1:T(8,128)(2,1)S(1)}, bf16[256,8,64]{0,2,1:T(8,128)(2,1)}, u32[]{:S(2)}) copy-start(bf16[256,8,64]{0,2,1:T(8,128)(2,1)} %get-tuple-element.132) | copy-start | bytes 786436
  329.3 26.2 %copy-start.70 = (f32[512]{0:T(512)S(1)}, f32[512]{0:T(512)}, u32[]{:S(2)}) copy-start(f32[512]{0:T(512)} %copy-done.69) | copy-start | bytes 6148
  329.3 26.2 %copy-start.78 = (f32[256]{0:T(256)S(1)}, f32[256]{0:T(256)}, u32[]{:S(2)}) copy-start(f32[256]{0:T(256)} %copy-done.77) | copy-start | bytes 3076
  329.3 26.2 %copy-start.152 = (f32[256]{0:T(256)S(1)}, f32[256]{0:T(256)}, u32[]{:S(2)}) copy-start(f32[256]{0:T(256)} %copy-done.151) | copy-start | bytes 3076
  (182 other events, 879.9 us)

commit v2 on v1

--- a/solution.py
+++ b/solution.py
@@ -3,6 +3,7 @@
 
 import jax
 import jax.numpy as jnp
+import numpy as np
 from jax import lax
 from jax.experimental import pallas as pl
 from jax.experimental.pallas import tpu as pltpu
@@ -534,14 +535,10 @@
 
 def angle_tables(frames, width):
     step = 32
-    frequency = jnp.exp(jnp.arange(width // 2, dtype=f32) * (-2.0 * math.log(10000.0) / width))
-    coarse = (jnp.arange(frames // step, dtype=f32) * step)[:, None] * frequency
-    fine = jnp.arange(step, dtype=f32)[:, None] * frequency
-    cs, cc = jnp.sin(coarse)[:, None], jnp.cos(coarse)[:, None]
-    fs, fc = jnp.sin(fine)[None], jnp.cos(fine)[None]
-    sines = (cs * fc + cc * fs).reshape(frames, width // 2)
-    cosines = (cc * fc - cs * fs).reshape(frames, width // 2)
-    return sines, cosines
+    frequency = np.exp(np.arange(width // 2) * (-2.0 * math.log(10000.0) / width))
+    coarse = np.arange(frames // step)[:, None] * step * frequency
+    fine = np.arange(step)[:, None] * frequency
+    return jnp.asarray(np.stack([np.sin(coarse), np.cos(coarse), np.sin(fine), np.cos(fine)]), f32)
 
 
 def shifted(whole, taps, rows, reverse):
@@ -574,51 +571,32 @@
     n_gain = norm_gains.shape[1]
     n_bias = position_bias.shape[2]
 
-    packed = jnp.stack([
-        first_up, first_down.T, attend_in.transpose(1, 0, 2).reshape(R, 4 * w),
-        jnp.concatenate([convolve_in.reshape(R, 2 * w), attend_out.T, convolve_out.T], axis=1),
-        second_up, second_down.T])
-    small = jnp.zeros((16, 128), f32)
-    small = small.at[:n_gain, :5].set(norm_gains.T)
-    small = small.at[:n_bias, 8:8 + 2 * local_heads].set(position_bias.astype(f32).reshape(2 * local_heads, n_bias).T)
+    gain_pack = jnp.concatenate([norm_gains, position_bias.astype(f32).reshape(2, local_heads * n_bias),
+                                 jnp.zeros((1, n_gain), f32)])
     taps = jnp.concatenate([depth_kernel.T, batch_norm, jnp.zeros((7, w), f32)], axis=0)
-    weights, small_all, taps_all = gather_weights(n_dp, n_t, packed, small, taps)
-    small_all = small_all.reshape(n_t, n_dp, 16, 128)
-    gains = small_all[:, :, :n_gain, :5].transpose(3, 1, 0, 2).reshape(5, D)
-    bias = small_all[:, :, :n_bias, 8:8 + 2 * local_heads].reshape(n_t, n_dp, n_bias, 2, local_heads)
-    bias = bias.transpose(3, 0, 4, 1, 2).reshape(2, D)
+    weights, gains, taps_all, x1, x2, a2_all, kv, content_q, position_q, softmax_w, mixture, phases, turns = forward_kernel(
+        n_dp, n_t, head_dim,
+        (first_up, first_down, attend_in, convolve_in.reshape(R, 2 * w), attend_out, convolve_out, second_up,
+         second_down), gain_pack, taps, inputs, angle_tables(frames, D))
+    a2_all = a2_all.reshape(frames, D)
+    a2 = lax.dynamic_slice_in_dim(a2_all, t * rows, rows, 0)
     taps_all = taps_all.transpose(1, 0, 2).reshape(40, D)
     tap_rows = taps_all[:KERNEL]
     bn_gain, bn_shift = taps_all[KERNEL], taps_all[KERNEL + 1]
     attend_w = weights[2].reshape(D, n_t, 4, w).transpose(2, 0, 1, 3).reshape(4, D, D)
     mixed_w = weights[3].reshape(D, n_t, 4, w).transpose(2, 0, 1, 3).reshape(4, D, D)
-
     x0 = inputs.astype(f32)
-    x1, stored_one = feed_forward(x0, gains[0], weights[0], weights[1])
-
+    _, stored_one = feed_forward(x0, gains[0], weights[0], weights[1])
     saved_two = norm_rows(x1)
-    a2 = (saved_two[0] * gains[1]).astype(bf16)
-    a2_all = spread_frames(n_t, a2).reshape(frames, D)
-    q = dot(a2, attend_w[0], 1, 0)
-    content_q = (q + bias[0]).astype(bf16).reshape(rows, heads, head_dim)
-    position_q = (q + bias[1]).astype(bf16).reshape(rows, heads, head_dim)
-    keys = dot(a2_all, attend_w[1], 1, 0).astype(bf16).reshape(frames, heads, head_dim)
-    values = dot(a2_all, attend_w[2], 1, 0).astype(bf16).reshape(frames, heads, head_dim)
-    sines, cosines = angle_tables(frames, D)
-    phases = jnp.concatenate([sines, cosines], axis=1).astype(bf16)
-    own_sin = lax.dynamic_slice_in_dim(sines, t * rows, rows, 0)
-    own_cos = lax.dynamic_slice_in_dim(cosines, t * rows, rows, 0)
     pos_w = attend_w[3].reshape(D, heads, head_dim)
     scale = head_dim ** -0.5
-    turned = jnp.einsum("rhe,che->hrc", position_q, pos_w, preferred_element_type=f32)
-    rs, rc = turned[..., :D // 2], turned[..., D // 2:]
-    turned = jnp.concatenate([rc * own_sin - rs * own_cos, rs * own_sin + rc * own_cos], axis=-1).astype(bf16)
-    scores = (jnp.einsum("rhe,fhe->hrf", content_q, keys, preferred_element_type=f32)
-              + jnp.einsum("hrc,fc->hrf", turned, phases, preferred_element_type=f32)) * scale
-    exponent = jnp.exp(scores - jnp.max(scores, axis=-1, keepdims=True))
-    softmax_w = (exponent / jnp.sum(exponent, axis=-1, keepdims=True)).astype(bf16)
-    mixture = jnp.einsum("hrf,fhe->rhe", softmax_w, values, preferred_element_type=f32).astype(bf16).reshape(rows, D)
-    x2 = x1 + dot(mixture, mixed_w[2], 1, 1)
+    own_sin, own_cos = turns[0], turns[1]
+    flat = lambda part: part.transpose(1, 0, 2).reshape(part.shape[1], D)
+    keys = flat(kv[:, :, :w]).reshape(frames, heads, head_dim)
+    values = flat(kv[:, :, w:]).reshape(frames, heads, head_dim)
+    content_q = flat(content_q).reshape(rows, heads, head_dim)
+    position_q = flat(position_q).reshape(rows, heads, head_dim)
+    mixture = flat(mixture)
 
     saved_three = norm_rows(x2)
     a3 = (saved_three[0] * gains[2]).astype(bf16)
@@ -728,3 +706,322 @@
         in_specs=(row, row, gain) + weights,
         out_specs=(row, row, gain) + weights,
         check_vma=False)
+
+
+def lane_head(shape, head_dim, head):
+    lanes = lax.broadcasted_iota(jnp.int32, shape, 1)
+    return (lanes >= head * head_dim) & (lanes < (head + 1) * head_dim)
+
+
+def row_head(shape, head_dim, head):
+    lanes = lax.broadcasted_iota(jnp.int32, shape, 0)
+    return (lanes >= head * head_dim) & (lanes < (head + 1) * head_dim)
+
+
+def keep(mask, value):
+    return jnp.where(mask, value, jnp.zeros_like(value))
+
+
+def row_loop(rows, size, body):
+    def step(k, carry):
+        body(pl.ds(pl.multiple_of(k * size, size), size))
+        return carry
+    lax.fori_loop(0, rows // size, step, 0)
+
+
+def sigmoid(values):
+    return 1.0 / (1.0 + jnp.exp(-values))
+
+
+def norm_parts(values):
+    centred = values - jnp.mean(values, axis=-1, keepdims=True)
+    inverse = lax.rsqrt(jnp.mean(centred * centred, axis=-1, keepdims=True) + norm_eps)
+    return centred * inverse, inverse
+
+
+def block_of(k, size):
+    return pl.ds(pl.multiple_of(k * size, size), size)
+
+
+def feed_rows(a_ref, up, down_t, z_ref):
+    rows = a_ref.shape[0]
+    width = 512
+
+    def step(k, carry):
+        cols = block_of(k, width)
+        pre = dot(a_ref[...], up[:, cols], 1, 0)
+        hidden = (pre * sigmoid(pre)).astype(bf16)
+        z_ref[...] = z_ref[...] + dot(hidden, down_t[:, cols], 1, 1)
+        return carry
+    z_ref[...] = jnp.zeros_like(z_ref)
+    lax.fori_loop(0, up.shape[1] // width, step, 0)
+
+
+def forward_body(n_dp, n_t, head_dim, fu, fd, at, cw, ao, co, su, sd, gain_ref, f_ref, x_ref, tab_ref,
+                 g_ref, gains_out, gf_ref, x1_ref, x2_ref, a2_ref, kv_ref, cq_ref, pq_ref, p_ref, mix_ref, phase_ref,
+                 turn_ref,
+                 pack, wbuf, a_s, z_s, s_s, u_s, e_acc, e_buf,
+                 local_sem, z_send, z_recv, d_send, d_recv, fz_send, fz_recv, e_send, e_recv, a_send, a_recv):
+    d = lax.axis_index("dp")
+    t = lax.axis_index("tensor")
+    rows_w, width = pack.shape[1], pack.shape[2]
+    rows, D = x_ref.shape
+    w = D // n_t
+    half = n_t * width // 2
+    frames = rows * n_t
+    local_heads = w // head_dim
+    n_gain = gain_ref.shape[1]
+    n_bias = n_gain // local_heads
+    orders = [order + [CORE] for order in link_orders(n_dp)]
+    stages = len(orders[0])
+    z_peers = tensor_peers(d, t, n_t)
+    greet(z_peers + [(flip(d, bit), t) for bit in orders[0]])
+
+    eye = (lax.broadcasted_iota(jnp.int32, (rows_w, rows_w), 0)
+           == lax.broadcasted_iota(jnp.int32, (rows_w, rows_w), 1)).astype(bf16)
+
+    def turn(ref):
+        return dot(eye, ref[...], 1, 1).astype(bf16)
+
+    def window(c, mask, start, size):
+        first = pl.multiple_of(flip(d, mask) * rows_w, rows_w)
+        return wbuf.at[c, pl.ds(first, rows_w), pl.ds(start, size)]
+
+    def own(c):
+        return window(c, 0, pl.multiple_of(t * width, width), width)
+
+    def z_copy(c, step):
+        return remote(pack.at[c], own(c), z_send.at[c, step], z_recv.at[c, step], z_peers[step])
+
+    def local_copy(c):
+        return pltpu.make_async_copy(pack.at[c], own(c), local_sem.at[c])
+
+    def out_copy(c):
+        return pltpu.make_async_copy(wbuf.at[c], g_ref.at[c], local_sem.at[CHUNKS + c])
+
+    def f_copy(step):
+        return remote(f_ref, gf_ref.at[t], fz_send.at[step], fz_recv.at[step], z_peers[step])
+
+    def a_copy(step):
+        return remote(a_s, a2_ref.at[t], a_send.at[step], a_recv.at[step], z_peers[step])
+
+    def dp_copies(c, stage):
+        copies = []
+        for h in range(2):
+            bit = orders[h][stage]
+            masks = span(orders[h][:stage])
+            for j, mask in enumerate(masks):
+                slot = len(masks) - 1 + j
+                part = window(c, mask, h * half, half)
+                copies.append(remote(part, part, d_send.at[c, h, slot], d_recv.at[c, h, slot], (flip(d, bit), t)))
+        return copies
+
+    def send_own(c):
+        local_copy(c).start()
+        for step in range(n_t - 1):
+            z_copy(c, step).start()
+
+    def e_copy(k):
+        if k < n_t - 1:
+            return remote(e_acc.at[0], e_buf.at[k], e_send.at[k], e_recv.at[k], z_peers[k])
+        return remote(e_acc.at[k - n_t + 2], e_buf.at[k], e_send.at[k], e_recv.at[k],
+                      (flip(d, orders[0][k - n_t + 1]), t))
+
+    pack[0] = fu[...]
+    send_own(0)
+    pack[1] = turn(fd)
+    send_own(1)
+    entry = lax.broadcasted_iota(jnp.int32, (n_gain, D), 0)
+    lane = lax.broadcasted_iota(jnp.int32, (n_gain, D), 1)
+    gain_spot = (lane == (d * n_t + t) * n_gain + entry).astype(f32)
+    spot = lax.rem(entry, n_bias) + d * n_bias + (entry // n_bias + t * local_heads) * head_dim
+    bias_spot = (lane == spot).astype(f32)
+    high = lax.Precision.HIGHEST
+    is_gain = lax.broadcasted_iota(jnp.int32, (8, D), 0) < 5
+    e_acc[0] = jnp.where(is_gain, jnp.dot(gain_ref[...], gain_spot, precision=high, preferred_element_type=f32),
+                         jnp.dot(gain_ref[...], bias_spot, precision=high, preferred_element_type=f32))
+    for k in range(n_t - 1):
+        e_copy(k).start()
+    for k in range(4):
+        pack[2, :, k * w:(k + 1) * w] = at[k]
+    send_own(2)
+    pack[3, :, 0:2 * w] = cw[...]
+    pack[3, :, 2 * w:3 * w] = turn(ao)
+    pack[3, :, 3 * w:4 * w] = turn(co)
+    send_own(3)
+    for step in range(n_t - 1):
+        f_copy(step).start()
+    own_f = pltpu.make_async_copy(f_ref, gf_ref.at[t], local_sem.at[2 * CHUNKS])
+    own_f.start()
+    pack[4] = su[...]
+    send_own(4)
+    pack[5] = turn(sd)
+    send_own(5)
+    total = e_acc[0]
+    for k in range(n_t - 1):
+        e_copy(k).wait_recv()
+        total = total + e_buf[k]
+    e_acc[1] = total
+
+    def relay(stage, c):
+        if stage == 0:
+            local_copy(c).wait()
+            for step in range(n_t - 1):
+                z_copy(c, step).wait_recv()
+        else:
+            for copy in dp_copies(c, stage - 1):
+                copy.wait_recv()
+        if stage < stages:
+            for copy in dp_copies(c, stage):
+                copy.start()
+        else:
+            out_copy(c).start()
+
+    def chain(number):
+        if 0 < number <= len(orders[0]):
+            e_copy(n_t - 2 + number).wait_recv()
+            e_acc[number + 1] = e_acc[number] + e_buf[n_t - 2 + number]
+        if number < len(orders[0]):
+            e_copy(n_t - 1 + number).start()
+
+    def step_all(number):
+        chain(number)
+        for stage in range(stages + 1):
+            if 0 <= number - stage < CHUNKS:
+                relay(stage, number - stage)
+
+    step_t = tab_ref.shape[1]
+
+    def table(k, carry):
+        cs, cc = tab_ref[0, pl.ds(k, 1), :], tab_ref[1, pl.ds(k, 1), :]
+        part = block_of(k, step_t)
+        phase_ref[part, 0:D // 2] = (cs * tab_ref[3] + cc * tab_ref[2]).astype(bf16)
+        phase_ref[part, D // 2:D] = (cc * tab_ref[3] - cs * tab_ref[2]).astype(bf16)
+        return carry
+    lax.fori_loop(0, frames // step_t, table, 0)
+
+    def own_table(k, carry):
+        at_k = t * (rows // step_t) + k
+        cs, cc = tab_ref[0, pl.ds(at_k, 1), :], tab_ref[1, pl.ds(at_k, 1), :]
+        part = block_of(k, step_t)
+        turn_ref[0, part, :] = cs * tab_ref[3] + cc * tab_ref[2]
+        turn_ref[1, part, :] = cc * tab_ref[3] - cs * tab_ref[2]
+        return carry
+    lax.fori_loop(0, rows // step_t, own_table, 0)
+
+    last = len(orders[0]) + 1
+    for number in range(stages + 2):
+        step_all(number)
+    gains_out[...] = e_acc[last]
+
+    def norm_one(part):
+        a_s[part, :] = (norm_parts(x_ref[part, :].astype(f32))[0] * gains_out[0:1, :]).astype(bf16)
+    row_loop(rows, 64, norm_one)
+    feed_rows(a_s, wbuf.at[0], wbuf.at[1], z_s)
+
+    def norm_two(part):
+        value = x_ref[part, :].astype(f32) + 0.5 * z_s[part, :]
+        x1_ref[part, :] = value
+        a_s[part, :] = (norm_parts(value)[0] * gains_out[1:2, :]).astype(bf16)
+    row_loop(rows, 64, norm_two)
+    for step in range(n_t - 1):
+        a_copy(step).start()
+    a2_ref[t] = a_s[...]
+    for number in range(stages + 2, CHUNKS + stages):
+        step_all(number)
+    for step in range(n_t - 1):
+        a_copy(step).wait_recv()
+
+    scale = head_dim ** -0.5
+    z_s[...] = jnp.zeros_like(z_s)
+
+    def head_group(j, carry):
+        cols = block_of(j, width)
+        block = wbuf[2, :, cols]
+        kv_cols = block[:, w:3 * w]
+        for part in range(n_t):
+            kv_ref[j, part * rows:(part + 1) * rows, :] = dot(a2_ref[part], kv_cols, 1, 0).astype(bf16)
+        q = dot(a_s[...], block[:, 0:w], 1, 0)
+        if w % 128 == 0:
+            bias = gains_out[5:7, pl.ds(pl.multiple_of(j * w, w), w)]
+        else:
+            bias = keep(lax.broadcasted_iota(jnp.int32, (2, w), 0) >= 0, gains_out[5:7, 0:w])
+            for other in range(1, n_t):
+                bias = jnp.where(j == other, gains_out[5:7, other * w:(other + 1) * w], bias)
+        cq = (q + bias[0:1]).astype(bf16)
+        pq = (q + bias[1:2]).astype(bf16)
+        cq_ref[j] = cq
+        pq_ref[j] = pq
+        for h in range(local_heads):
+            mask = lane_head((rows, w), head_dim, h)
+            turned = dot(keep(mask, pq), block[:, 3 * w:4 * w], 1, 1)
+            rs, rc = turned[:, :D // 2], turned[:, D // 2:]
+            u_s[:, 0:D // 2] = (rc * turn_ref[0] - rs * turn_ref[1]).astype(bf16)
+            u_s[:, D // 2:D] = (rs * turn_ref[0] + rc * turn_ref[1]).astype(bf16)
+            s_s[...] = (dot(u_s[...], phase_ref[...], 1, 1)
+                        + dot(keep(mask, cq), kv_ref[j, :, 0:w], 1, 1))
+            head = j * local_heads + h
+
+            def soften(part):
+                s = s_s[part, :] * scale
+                e = jnp.exp(s - jnp.max(s, axis=-1, keepdims=True))
+                p_ref[head, part, :] = (e * (1.0 / jnp.sum(e, axis=-1, keepdims=True))).astype(bf16)
+            row_loop(rows, 32, soften)
+            mixed = dot(p_ref[head], kv_ref[j, :, w:2 * w], 1, 0).astype(bf16)
+            mixture = mixed if h == 0 else jnp.where(mask, mixed, mixture)
+        mix_ref[j] = mixture
+        block = wbuf[3, :, cols]
+        z_s[...] = z_s[...] + dot(mixture, block[:, 2 * w:3 * w], 1, 1)
+        return carry
+    lax.fori_loop(0, n_t, head_group, 0)
+    x2_ref[...] = x1_ref[...] + z_s[...]
+
+    for step in range(n_t - 1):
+        f_copy(step).wait()
+        a_copy(step).wait_send()
+    own_f.wait()
+    for k in range(n_t - 1 + len(orders[0])):
+        e_copy(k).wait_send()
+    for c in range(CHUNKS):
+        out_copy(c).wait()
+        for step in range(n_t - 1):
+            z_copy(c, step).wait_send()
+        for stage in range(stages):
+            for copy in dp_copies(c, stage):
+                copy.wait_send()
+
+
+def forward_kernel(n_dp, n_t, head_dim, args, gains, taps, x, tables):
+    rows, D = x.shape
+    rows_w, width = args[0].shape
+    w = D // n_t
+    frames = rows * n_t
+    heads = D // head_dim
+    n_e = n_t - 1 + n_dp.bit_length() - 1
+    dma = pltpu.SemaphoreType.DMA
+    vmem = pl.BlockSpec(memory_space=pltpu.VMEM)
+    hbm = pl.BlockSpec(memory_space=pl.ANY)
+
+    def shape(*dims, kind=bf16):
+        return jax.ShapeDtypeStruct(dims, kind)
+    inputs = list(args) + [gains, taps, x, tables]
+    outs = (shape(CHUNKS, n_dp * rows_w, n_t * width), shape(8, D, kind=f32), shape(n_t, *taps.shape, kind=f32),
+            shape(rows, D, kind=f32), shape(rows, D, kind=f32), shape(n_t, rows, D), shape(n_t, frames, 2 * w),
+            shape(n_t, rows, w), shape(n_t, rows, w), shape(heads, rows, frames), shape(n_t, rows, w),
+            shape(frames, D), shape(2, rows, D // 2, kind=f32))
+    return pl.pallas_call(
+        functools.partial(forward_body, n_dp, n_t, head_dim),
+        name="forward",
+        out_shape=outs,
+        in_specs=[vmem] * len(inputs),
+        out_specs=(hbm,) + (vmem,) * (len(outs) - 1),
+        scratch_shapes=[
+            pltpu.VMEM((CHUNKS, rows_w, width), bf16), pltpu.VMEM((CHUNKS, n_dp * rows_w, n_t * width), bf16),
+            pltpu.VMEM((rows, D), bf16), pltpu.VMEM((rows, D), f32), pltpu.VMEM((rows, frames), f32),
+            pltpu.VMEM((rows, D), bf16),
+            pltpu.VMEM((n_dp.bit_length() + 1, 8, D), f32), pltpu.VMEM((n_e, 8, D), f32),
+            dma((2 * CHUNKS + 1,)), dma((CHUNKS, n_t - 1)), dma((CHUNKS, n_t - 1)),
+            dma((CHUNKS, 2, n_dp - 1)), dma((CHUNKS, 2, n_dp - 1)),
+            dma((n_t - 1,)), dma((n_t - 1,)), dma((n_e,)), dma((n_e,)), dma((n_t - 1,)), dma((n_t - 1,))],
+        compiler_params=pltpu.CompilerParams(collective_id=0, has_side_effects=True, vmem_limit_bytes=60 << 20),
+    )(*inputs)

time: 480 us -> 439 us (0.915)
  matrix products: 89 us -> 66 us
  local copies, waits for them, and re-layouts: 80.3 us -> 67.2 us
  other arithmetic: 52.3 us -> 45.1 us
    dot_general x33 -> x28, matrix products: 59.6 us -> 47.4 us  [dot(): lax.dot_general(left, right, (((left_dim,), (right_dim,)), ((), ())), pre...]
    sub x1 -> x0, matrix products: 9.63 us -> none  [per_device(): exponent = jnp.exp(scores - jnp.max(scores, axis=-1, keepdims=True))]
    unnamed x426 -> x205, local copies, waits for them, and re-layouts: 21.5 us -> 12.6 us
    dot_general x3 -> x0, matrix products: 7.84 us -> none  [the longest x1 5.69 us: per_device(): jnp.einsum('hrc,fc->hrf', turned, phases, preferred_element_type=f32)]
    transpose x1 -> x6, local copies, waits for them, and re-layouts: 0.89 us -> 7.48 us  [per_device(): flat = lambda part: part.transpose(1, 0, 2).reshape(part.shape[1], D)]
    pallas_call x2 -> x1, Pallas kernels: 102 us -> 107 us  [forward_kernel(): pl.pallas_call(functools.partial(forward_body, n_dp, n_t, head_dim), name...]
    convert_element_type x2 -> x0, other arithmetic: 4.87 us -> none  [the longest x1 4.01 us: per_device(): (exponent / jnp.sum(exponent, axis=-1, keepdims=True)).astype(bf16)]
where the time goes in v2:
time: 439 us; the launch traced here: 431 us
  Pallas kernels  250 us (57%)
  local copies, waits for them, and re-layouts  67.2 us (15%)
  matrix products  66 us (15%)
  other arithmetic  45.1 us (10%)
    pallas_call x1, Pallas kernels, forward_kernel(): pl.pallas_call(functools.partial(forward_body, n_dp, n_t, head_dim), name...  107 us
    pallas_call x1, Pallas kernels, fold_weights(): pl.pallas_call(functools.partial(fold_body, n_dp, n_t), name='fold_weight...  86.5 us
    dot_general x28, matrix products, dot(): lax.dot_general(left, right, (((left_dim,), (right_dim,)), ((), ())), pre...  47.4 us
    pallas_call x1, Pallas kernels, reduce_frames(): pl.pallas_call(functools.partial(reduce_frames_body, n_t), name='reduce_f...  23.4 us
    pallas_call x2, Pallas kernels, whole_totals(): pl.pallas_call(functools.partial(totals_body, n_dp, n_t, edge_rows is not...  23 us
    reduce_sum x1, other arithmetic, per_device(): jnp.sum(convolved, axis=0)  14.2 us
    unnamed x205, local copies, waits for them, and re-layouts  12.6 us
    pallas_call x1, Pallas kernels, swap_edges(): pl.pallas_call(functools.partial(edges_body, n_t), name='swap_edges', out...  10 us

profile of v2, /device:TPU:0, one launch (start us, length us, event | category | flops | bytes accessed | tf_op | source)
XLA Modules:
  0.0 430.9 jit_solution(6875218573626559308)
XLA Ops:
  11.8 107.4 %forward.1 = (bf16[6,512,2048]{2,1,0:T(8,128)(2,1)}, f32[8,512]{1,0:T(8,128)}, f32[4,40,128]{2,1,0:T(8,128)}, f32[256,512]{1,0:T(8,128)}, f32[256,512]{1,0:T(8,1...) custom-call(bf16[64,512]{1,0:T(8,128)(2,1)} %fu.1, ...), custom_call_target="tpu_custom_call" | custom-call | tf_op jit(solution)/shard_map/forward/pallas_call | solution.py:1012
  123.7 4.1 fusion.216
  130.5 3.0 copy.45
  136.8 10.0 %swap_edges.1 = f32[2,1,16,512]{3,2,1,0:T(8,128)} custom-call(f32[1,256,512]{2,1,0:T(8,128)} %bitcast.319), custom_call_target="tpu_custom_call" | custom-call | tf_op jit(solution)/shard_map/swap_edges/pallas_call | solution.py:416
  147.7 14.2 %fusion.214 = (f32[512]{0:T(512)S(1)}, f32[512]{0:T(512)S(1)}, f32[256,512]{1,0:T(8,128)S(1)}) fusion(f32[16,512]{1,0:T(8,128)S(1)} %get-tuple-element.170, f32[256,512]{1,0:T(8,128)} %get-tuple-element.179, f32[512]{0:T(512)S(1)} %bitcast.388, f32[512]{0:T(512)S(1)} %bitcast.390, f32[512]{0:T(512)S(1)} %bitcast.392, f32[512]{0:T(512)S(1)} %bitcast.394, ...), kind=kLoop, calls=%fused_computation.459 | loop fusion | flops 12319744 | bytes 1181696 | tf_op jit(solution)/shard_map/reduce_sum | solution.py:610
  162.6 11.8 %whole_totals.2 = f32[8,512]{1,0:T(8,128)} custom-call(f32[8,512]{1,0:T(8,128)} %maximum_maximum_fusion.1.refs_0_), custom_call_target="tpu_custom_call" | custom-call | tf_op jit(solution)/shard_map/whole_totals/pallas_call | solution.py:477
  178.3 3.2 fusion.224
  185.4 3.5 multiply_reduce_fusion
  192.6 11.2 %whole_totals.3 = (f32[8,512]{1,0:T(8,128)}, f32[2,2,16,512]{3,2,1,0:T(8,128)}) custom-call(f32[8,512]{1,0:T(8,128)} %maximum_maximum_fusion.2.refs_0_, f32[2,256,512]{2,1,0:T(8,128)} %pad_maximum_fusion.5.refs_1_), custom_call_target="tpu_custom_call" | custom-call | tf_op jit(solution)/shard_map/whole_totals/pallas_call | solution.py:477
  215.7 3.0 slice_bitcast_fusion
  220.5 3.7 fusion
  231.2 4.7 %fusion.227 = f32[8,64,256]{2,1,0:T(8,128)} fusion(bf16[1024,8,64]{0,2,1:T(8,128)(2,1)} %bitcast.329, bf16[8,256,1024]{2,1,0:T(8,128)(2,1)} %copy-done.2), kind=kOutput, calls=%fused_computation.471 | convolution fusion | flops 268435456 | bytes 5767168 | tf_op jit(solution)/shard_map/hrf,fhe->rhe/dot_general | solution.py:659
  235.9 4.5 %reshape_squeeze.13 = bf16[512,4,4,128]{3,2,1,0:T(4,128)(2,1)} reshape(bf16[1,512,2048]{2,1,0:T(8,128)(2,1)} %get-tuple-element.104) | data formatting | bytes 4194304 | tf_op jit(solution)/shard_map/reshape;squeeze | solution.py:586
  240.4 4.3 copy.51
  250.0 3.2 multiply_convert_fusion.1
  256.7 23.4 %reduce_frames.1 = f32[256,512]{1,0:T(8,128)} custom-call(bf16[4,256,512]{2,1,0:T(8,128)(2,1)} %bitcast.328), custom_call_target="tpu_custom_call" | custom-call | tf_op jit(solution)/shard_map/reduce_frames/pallas_call | solution.py:378
  284.7 3.4 fusion.11
  288.2 3.6 fusion.63
  298.1 3.1 copy.56
  301.2 3.4 stack_reshape.10
  313.8 4.5 %copy.54 = bf16[512,4,4,128]{3,2,1,0:T(4,128)(2,1)} copy(bf16[512,4,4,128]{0,3,1,2:T(8,128)(2,1)} %maximum_bitcast_fusion) | data formatting | bytes 4194304 | tf_op jit(solution)/shard_map/transpose | solution.py:674
  318.3 4.6 %stack_reshape.9 = bf16[1,512,2048]{2,1,0:T(8,128)(2,1)} reshape(bf16[512,4,4,128]{3,2,1,0:T(4,128)(2,1)} %copy.54) | data formatting | bytes 4194304 | tf_op jit(solution)/shard_map/stack;reshape | solution.py:675
  323.0 3.6 fusion.3
  337.0 86.5 %fold_weights.1 = (f32[6,64,512]{2,1,0:T(8,128)S(1)}, f32[40,128]{1,0:T(8,128)S(1)}) custom-call(bf16[6,512,2048]{2,1,0:T(8,128)(2,1)} %fusion.9.x_ref, f32[4,40,128]{2,1,0:T(8,128)S(1)} %pad_maximum_fusion.10.s_ref), custom_call_target="tpu_custom_call" | custom-call | tf_op jit(solution)/shard_map/fold_weights/pallas_call | solution.py:296
  (334 shorter events, 100.8 us)
Async XLA Ops:
  123.7 11.8 %copy-start.16 = (bf16[256,512]{1,0:T(8,128)(2,1)}, bf16[256,512]{1,0:T(8,128)(2,1)S(1)}, u32[]{:S(2)}) copy-start(bf16[256,512]{1,0:T(8,128)(2,1)S(1)} %multiply_convert_fusion.11) | copy-start | bytes 786436
  135.1 12.5 %copy-start.55 = (f32[4,40,128]{2,1,0:T(8,128)S(1)}, f32[4,40,128]{2,1,0:T(8,128)}, u32[]{:S(2)}) copy-start(f32[4,40,128]{2,1,0:T(8,128)} %get-tuple-element.32) | copy-start | bytes 245764
  135.5 39.7 %copy-start.4 = (f32[256,512]{1,0:T(8,128)S(1)}, f32[256,512]{1,0:T(8,128)}, u32[]{:S(2)}) copy-start(f32[256,512]{1,0:T(8,128)} %get-tuple-element.31) | copy-start | bytes 1572868
  135.5 39.8 %copy-start.49 = (bf16[1,512,4,128]{1,3,2,0:T(8,128)(2,1)S(1)}, bf16[1,512,4,128]{1,3,2,0:T(8,128)(2,1)}, u32[]{:S(2)}) copy-start(bf16[1,512,4,128]{1,3,2,0:T(8,128)(2,1)} %get-tuple-element.115) | copy-start | bytes 1572868
  147.6 42.4 %copy-start.92 = (f32[1,4,128]{2,0,1:T(1,128)}, f32[1,4,128]{2,0,1:T(1,128)S(1)}, u32[]{:S(2)}) copy-start(f32[1,4,128]{2,0,1:T(1,128)S(1)} %get-tuple-element.135) | copy-start | bytes 6148
  147.6 61.5 %copy-start.76 = (f32[1,4,128]{2,0,1:T(1,128)}, f32[1,4,128]{2,0,1:T(1,128)S(1)}, u32[]{:S(2)}) copy-start(f32[1,4,128]{2,0,1:T(1,128)S(1)} %get-tuple-element.134) | copy-start | bytes 6148
  175.7 13.2 %copy-start.7 = (f32[256,512]{1,0:T(8,128)}, f32[256,512]{1,0:T(8,128)S(1)}, u32[]{:S(2)}) copy-start(f32[256,512]{1,0:T(8,128)S(1)} %get-tuple-element.182) | copy-start | bytes 1572868
  178.3 4.3 copy-start.33
  181.5 7.3 %copy-start.10 = (f32[256,512]{1,0:T(8,128)}, f32[256,512]{1,0:T(8,128)S(1)}, u32[]{:S(2)}) copy-start(f32[256,512]{1,0:T(8,128)S(1)} %get-tuple-element.184) | copy-start | bytes 1572868
  182.6 6.3 %copy-start.88 = (f32[256]{0:T(256)}, f32[256]{0:T(256)S(1)}, u32[]{:S(2)}) copy-start(f32[256]{0:T(256)S(1)} %broadcast_multiply_fusion.10) | copy-start | bytes 3076
  182.6 6.3 %copy-start.90 = (f32[256]{0:T(256)}, f32[256]{0:T(256)S(1)}, u32[]{:S(2)}) copy-start(f32[256]{0:T(256)S(1)} %broadcast_multiply_fusion.11) | copy-start | bytes 3076
  190.5 14.1 %copy-start.3 = (f32[256,512]{1,0:T(8,128)S(1)}, f32[256,512]{1,0:T(8,128)}, u32[]{:S(2)}) copy-start(f32[256,512]{1,0:T(8,128)} %get-tuple-element.179) | copy-start | bytes 1572868
  250.0 4.0 copy-start.1
  254.9 25.1 %copy-start.87 = (f32[256]{0:T(256)S(1)}, f32[256]{0:T(256)}, u32[]{:S(2)}) copy-start(f32[256]{0:T(256)} %get-tuple-element.192) | copy-start | bytes 3076
  254.9 25.2 %copy-start.40 = (bf16[1,512,4,128]{1,3,2,0:T(8,128)(2,1)S(1)}, bf16[1,512,4,128]{1,3,2,0:T(8,128)(2,1)}, u32[]{:S(2)}) copy-start(bf16[1,512,4,128]{1,3,2,0:T(8,128)(2,1)} %get-tuple-element.108) | copy-start | bytes 1572868
  254.9 25.2 %copy-start.50 = (bf16[256,8,64]{0,2,1:T(8,128)(2,1)S(1)}, bf16[256,8,64]{0,2,1:T(8,128)(2,1)}, u32[]{:S(2)}) copy-start(bf16[256,8,64]{0,2,1:T(8,128)(2,1)} %get-tuple-element.128) | copy-start | bytes 786436
  288.1 3.8 copy-start.75
  288.1 3.9 copy-start.94
  288.2 4.0 copy-start.74
  288.2 4.3 copy-start.29
  288.2 4.3 copy-start.77
  288.2 4.3 copy-start.93
  423.5 4.9 %copy-start.32 = (f32[256,512]{1,0:T(8,128)S(1)}, f32[256,512]{1,0:T(8,128)}, u32[]{:S(2)}) copy-start(f32[256,512]{1,0:T(8,128)} %copy-done.30) | copy-start | bytes 1572868
  423.5 4.9 %copy-start.48 = (f32[256,512]{1,0:T(8,128)S(1)}, f32[256,512]{1,0:T(8,128)}, u32[]{:S(2)}) copy-start(f32[256,512]{1,0:T(8,128)} %get-tuple-element.191) | copy-start | bytes 1572868
  (73 other events, 165.6 us)

commit v3 on v0

v3 whole, which is shorter than its diff:
```python
import functools
import math
from types import SimpleNamespace

import jax
import jax.numpy as jnp
import numpy as np
from jax import lax
from jax.experimental import pallas as pl
from jax.experimental.pallas import tpu as pltpu
from jax.sharding import PartitionSpec as P

MESH = pl.DeviceIdType.MESH
CHUNKS = 6
CORE = 1
EDGE = 16
KERNEL = 31
HALF = KERNEL // 2
norm_eps = 1e-05
f32 = jnp.float32
bf16 = jnp.bfloat16
high = lax.Precision.HIGHEST


def flip(index, mask):
    result = index
    bit = 1
    while bit <= mask:
        if mask & bit:
            result = result + bit - 2 * bit * ((index // bit) % 2)
        bit *= 2
    return result


def span(bits):
    masks = [0]
    for bit in bits:
        masks = masks + [mask ^ bit for mask in masks]
    return masks


def link_orders(n_dp):
    bits = [1 << k for k in range(1, n_dp.bit_length() - 1)]
    return (bits, bits[::-1])


def greet(peers):
    barrier = pltpu.get_barrier_semaphore()
    for peer in peers:
        pl.semaphore_signal(barrier, inc=1, device_id=peer, device_id_type=MESH)
    pl.semaphore_wait(barrier, len(peers))


def remote(src, dst, send_sem, recv_sem, peer):
    return pltpu.make_async_remote_copy(
        src_ref=src, dst_ref=dst, send_sem=send_sem, recv_sem=recv_sem,
        device_id=peer, device_id_type=MESH)


def start_all(copies):
    for copy in copies:
        copy.start()


def arrive_all(copies):
    for copy in copies:
        copy.wait_recv()


def sent_all(copies):
    for copy in copies:
        copy.wait_send()


def dot(left, right, left_dim, right_dim):
    return lax.dot_general(left, right, (((left_dim,), (right_dim,)), ((), ())), preferred_element_type=f32)


def turned(value):
    return value.astype(f32).T.astype(bf16)


def head_mask(shape, axis, head_dim, head):
    place = lax.broadcasted_iota(jnp.int32, shape, axis)
    return (place >= head * head_dim) & (place < (head + 1) * head_dim)


def keep(mask, value):
    return jnp.where(mask, value, jnp.zeros_like(value))


def block_of(k, size):
    return pl.ds(pl.multiple_of(k * size, size), size)


def loop(count, body):
    def step(k, carry):
        body(k)
        return carry
    lax.fori_loop(0, count, step, 0)


def row_loop(rows, size, body):
    loop(rows // size, lambda k: body(block_of(k, size)))


def sigmoid(values):
    return 1.0 / (1.0 + jnp.exp(-values))


def norm_parts(values):
    centred = values - jnp.mean(values, axis=-1, keepdims=True)
    inverse = lax.rsqrt(jnp.mean(centred * centred, axis=-1, keepdims=True) + norm_eps)
    return centred * inverse, inverse


def norm_back(value, incoming, gain_row):
    scaled, inverse = norm_parts(value)
    grad_scaled = incoming * gain_row
    inner = jnp.mean(grad_scaled * scaled, axis=-1, keepdims=True)
    grad_in = inverse * (grad_scaled - jnp.mean(grad_scaled, axis=-1, keepdims=True) - scaled * inner)
    return scaled, grad_in, jnp.sum(incoming * scaled, axis=0, keepdims=True)


SLAB = 512


def feed_rows(a_ref, up, down_t, z_ref, hidden, slope):
    z_ref[...] = jnp.zeros_like(z_ref)

    def step(k):
        cols = block_of(k, SLAB)
        pre = dot(a_ref[...], up[:, cols], 1, 0)
        sig = sigmoid(pre)
        hidden[:, cols] = (pre * sig).astype(bf16)
        slope[:, cols] = (sig * (1.0 + pre * (1.0 - sig))).astype(bf16)
        z_ref[...] = z_ref[...] + dot(hidden[:, cols], down_t[:, cols], 1, 1)
    loop(up.shape[1] // SLAB, step)


def feed_back(dz_ref, dz_turn, a_turn, up, down_t, z_ref, hidden, slope, g_up, g_down):
    z_ref[...] = jnp.zeros_like(z_ref)

    def step(k):
        cols = block_of(k, SLAB)
        g_down[:, cols] = dot(dz_turn[...], hidden[:, cols], 1, 0).astype(bf16)
        grad_pre = (dot(dz_ref[...], down_t[:, cols], 1, 0) * slope[:, cols].astype(f32)).astype(bf16)
        g_up[:, cols] = dot(a_turn[...], grad_pre, 1, 0).astype(bf16)
        z_ref[...] = z_ref[...] + dot(grad_pre, up[:, cols], 1, 1)
    loop(up.shape[1] // SLAB, step)


def layer_body(names, n_dp, n_t, head_dim, *all_refs):
    r = SimpleNamespace(**dict(zip(names, all_refs)))
    d = lax.axis_index("dp")
    t = lax.axis_index("tensor")
    pack, wbuf, gbuf = r.pack, r.wbuf, r.gbuf
    x_ref, gains, taps = r.x, r.gains, r.taps
    rows_w, width = pack.shape[1], pack.shape[2]
    rows, D = x_ref.shape
    w = D // n_t
    half = n_t * width // 2
    frames = rows * n_t
    local_heads = w // head_dim
    n_gain = r.gain_in.shape[1]
    n_bias = n_gain // local_heads
    row_count = frames * n_dp
    scale = head_dim ** -0.5
    links = link_orders(n_dp)
    orders = [order + [CORE] for order in links]
    stages = len(orders[0])
    n_link = len(links[0])
    z_peers = [(d, lax.rem(t + step, n_t)) for step in range(1, n_t)]
    d_peers = [(flip(d, mask), t) for mask in range(1, n_dp)]
    before = (d, lax.rem(t + n_t - 1, n_t))
    after = (d, lax.rem(t + 1, n_t))
    z_range = range(n_t - 1)
    greet(z_peers + d_peers)

    eye = (lax.broadcasted_iota(jnp.int32, (rows_w, rows_w), 0)
           == lax.broadcasted_iota(jnp.int32, (rows_w, rows_w), 1)).astype(bf16)

    def turn(ref):
        return dot(eye, ref[...], 1, 1).astype(bf16)

    def window(c, mask, start, size):
        first = pl.multiple_of(flip(d, mask) * rows_w, rows_w)
        return wbuf.at[c, pl.ds(first, rows_w), pl.ds(start, size)]

    def own(c):
        return window(c, 0, pl.multiple_of(t * width, width), width)

    def z_copies(c):
        return [remote(pack.at[c], own(c), r.z_send.at[c, k], r.z_recv.at[c, k], z_peers[k]) for k in z_range]

    def local_copy(c):
        return pltpu.make_async_copy(pack.at[c], own(c), r.local_sem.at[c])

    def dp_copies(c, stage):
        copies = []
        for h in range(2):
            bit = orders[h][stage]
            masks = span(orders[h][:stage])
            for j, mask in enumerate(masks):
                slot = len(masks) - 1 + j
                part = window(c, mask, h * half, half)
                copies.append(remote(part, part, r.d_send.at[c, h, slot], r.d_recv.at[c, h, slot],
                                     (flip(d, bit), t)))
        return copies

    def send_own(c):
        local_copy(c).start()
        start_all(z_copies(c))

    e_acc, e_buf = r.e_acc, r.e_buf

    def e_copies(first, stop):
        copies = []
        for k in range(first, stop):
            if k < n_t - 1:
                source, peer = e_acc.at[0], z_peers[k]
            else:
                source, peer = e_acc.at[k - n_t + 2], (flip(d, orders[0][k - n_t + 1]), t)
            copies.append(remote(source, e_buf.at[k], r.e_send.at[k], r.e_recv.at[k], peer))
        return copies

    tap_copies = [remote(r.tap_in, taps.at[t], r.f_send.at[k], r.f_recv.at[k], z_peers[k]) for k in z_range]

    pack[0] = r.fu[...]
    send_own(0)
    pack[1] = turn(r.fd)
    send_own(1)
    entry = lax.broadcasted_iota(jnp.int32, (n_gain, D), 0)
    lane = lax.broadcasted_iota(jnp.int32, (n_gain, D), 1)
    gain_spot = (lane == (d * n_t + t) * n_gain + entry).astype(f32)
    bias_spot = (lane == lax.rem(entry, n_bias) + d * n_bias
                 + (entry // n_bias + t * local_heads) * head_dim).astype(f32)
    is_gain = lax.broadcasted_iota(jnp.int32, (8, D), 0) < 5
    e_acc[0] = jnp.where(is_gain, jnp.dot(r.gain_in[...], gain_spot, precision=high, preferred_element_type=f32),
                         jnp.dot(r.gain_in[...], bias_spot, precision=high, preferred_element_type=f32))
    start_all(e_copies(0, n_t - 1))
    for k in range(4):
        pack[2, :, k * w:(k + 1) * w] = r.at[k]
    send_own(2)
    pack[3, :, 0:2 * w] = r.cw[...]
    pack[3, :, 2 * w:3 * w] = turn(r.ao)
    pack[3, :, 3 * w:4 * w] = turn(r.co)
    send_own(3)
    start_all(tap_copies)
    taps[t] = r.tap_in[...]
    pack[4] = r.su[...]
    send_own(4)
    pack[5] = turn(r.sd)
    send_own(5)
    arrive_all(e_copies(0, n_t - 1))
    total = e_acc[0]
    for k in z_range:
        total = total + e_buf[k]
    e_acc[1] = total

    def tick(number):
        if 0 < number <= n_link + 1:
            arrive_all(e_copies(n_t - 2 + number, n_t - 1 + number))
            e_acc[number + 1] = e_acc[number] + e_buf[n_t - 2 + number]
        if number <= n_link:
            start_all(e_copies(n_t - 1 + number, n_t + number))
        for stage in range(stages + 1):
            c = number - stage
            if not 0 <= c < CHUNKS:
                continue
            if stage == 0:
                local_copy(c).wait()
                arrive_all(z_copies(c))
            else:
                arrive_all(dp_copies(c, stage - 1))
            if stage < stages:
                start_all(dp_copies(c, stage))

    tab, phase, spin = r.tab, r.phase, r.spin
    step_t = tab.shape[1]

    def table(k):
        cs, cc = tab[0, pl.ds(k, 1), :], tab[1, pl.ds(k, 1), :]
        part = block_of(k, step_t)
        phase[part, 0:D // 2] = (cs * tab[3] + cc * tab[2]).astype(bf16)
        phase[part, D // 2:D] = (cc * tab[3] - cs * tab[2]).astype(bf16)
    loop(frames // step_t, table)

    def own_table(k):
        place = t * (rows // step_t) + k
        cs, cc = tab[0, pl.ds(place, 1), :], tab[1, pl.ds(place, 1), :]
        part = block_of(k, step_t)
        spin[0, part, :] = cs * tab[3] + cc * tab[2]
        spin[1, part, :] = cc * tab[3] - cs * tab[2]
    loop(rows // step_t, own_table)

    def spun(sines, cosines):
        u_s = r.u_s
        u_s[:, 0:D // 2] = (cosines * spin[0] - sines * spin[1]).astype(bf16)
        u_s[:, D // 2:D] = (sines * spin[0] + cosines * spin[1]).astype(bf16)

    z_s, a1, a2, a2_all = r.z_s, r.a1, r.a2, r.a2_all
    x1, x2, x3 = r.x1, r.x2, r.x3
    for number in range(stages + 2):
        tick(number)
    gains[...] = e_acc[n_link + 2]

    def norm_one(part):
        a1[part, :] = (norm_parts(x_ref[part, :].astype(f32))[0] * gains[0:1, :]).astype(bf16)
    row_loop(rows, 64, norm_one)
    feed_rows(a1, wbuf.at[0], wbuf.at[1], z_s, r.hid1, r.slope1)

    def norm_two(part):
        value = x_ref[part, :].astype(f32) + 0.5 * z_s[part, :]
        x1[part, :] = value
        a2[part, :] = (norm_parts(value)[0] * gains[1:2, :]).astype(bf16)
    row_loop(rows, 64, norm_two)

    a_copies = [remote(a2, a2_all.at[t], r.a_send.at[k], r.a_recv.at[k], z_peers[k]) for k in z_range]
    start_all(a_copies)
    a2_all[t] = a2[...]
    for number in range(stages + 2, CHUNKS + stages):
        tick(number)
    arrive_all(a_copies)
    kv, cq, pq, probs, mix, s_s, u_s = r.kv, r.cq, r.pq, r.probs, r.mix, r.s_s, r.u_s
    z_s[...] = jnp.zeros_like(z_s)

    def head_group(j):
        cols = block_of(j, width)
        block = wbuf[2, :, cols]
        for part in range(n_t):
            kv[j, part * rows:(part + 1) * rows, :] = dot(a2_all[part], block[:, w:3 * w], 1, 0).astype(bf16)
        q = dot(a2[...], block[:, 0:w], 1, 0)
        if w % 128 == 0:
            bias = gains[5:7, block_of(j, w)]
        else:
            bias = gains[5:7, 0:w]
            for other in range(1, n_t):
                bias = jnp.where(j == other, gains[5:7, other * w:(other + 1) * w], bias)
        cq_j = (q + bias[0:1]).astype(bf16)
        pq_j = (q + bias[1:2]).astype(bf16)
        cq[j] = cq_j
        pq[j] = pq_j
        for h in range(local_heads):
            mask = head_mask((rows, w), 1, head_dim, h)
            spread = dot(keep(mask, pq_j), block[:, 3 * w:4 * w], 1, 1)
            spun(spread[:, :D // 2], spread[:, D // 2:])
            s_s[...] = dot(u_s[...], phase[...], 1, 1) + dot(keep(mask, cq_j), kv[j, :, 0:w], 1, 1)
            head = j * local_heads + h

            def soften(part):
                s = s_s[part, :] * scale
                e = jnp.exp(s - jnp.max(s, axis=-1, keepdims=True))
                probs[head, part, :] = (e * (1.0 / jnp.sum(e, axis=-1, keepdims=True))).astype(bf16)
            row_loop(rows, 32, soften)
            mixed = dot(probs[head], kv[j, :, w:2 * w], 1, 0).astype(bf16)
            mixture = mixed if h == 0 else jnp.where(mask, mixed, mixture)
        mix[j] = mixture
        z_s[...] = z_s[...] + dot(mixture, wbuf[3, :, cols][:, 2 * w:3 * w], 1, 1)
    loop(n_t, head_group)

    a3, glu, bhat, val, sig, act = r.a3, r.glu, r.bhat, r.val, r.sig, r.act
    dbn, sums, sum_buf, sum_mid, sum_z = r.dbn, r.sums, r.sum_buf, r.sum_mid, r.sum_z
    inner = pl.ds(EDGE, rows)

    def norm_three(part):
        value = x1[part, :] + z_s[part, :]
        x2[part, :] = value
        a3[part, :] = (norm_parts(value)[0] * gains[2:3, :]).astype(bf16)
    row_loop(rows, 64, norm_three)

    def gate(j):
        block = wbuf[3, :, block_of(j, width)]
        e = dot(a3[...], block[:, 0:2 * w], 1, 0)
        sig_j = sigmoid(e[:, w:2 * w])
        val[j] = e[:, 0:w]
        sig[j] = sig_j
        glu[j, inner, :] = e[:, 0:w] * sig_j
    loop(n_t, gate)

    def edge_copies(ref, k):
        first, last = pl.ds(EDGE, EDGE), pl.ds(rows, EDGE)
        return [remote(ref.at[:, first, :], ref.at[:, pl.ds(EDGE + rows, EDGE), :], r.edge_send.at[k, 0],
                       r.edge_recv.at[k, 0], before),
                remote(ref.at[:, last, :], ref.at[:, pl.ds(0, EDGE), :], r.edge_send.at[k, 1],
                       r.edge_recv.at[k, 1], after)]

    def close_edges(ref):
        ref[:, pl.ds(0, EDGE), :] = jnp.where(t > 0, ref[:, pl.ds(0, EDGE), :], 0.0)
        tail = pl.ds(EDGE + rows, EDGE)
        ref[:, tail, :] = jnp.where(t < n_t - 1, ref[:, tail, :], 0.0)

    def sum_copies(k):
        return [remote(sums.at[k], sum_buf.at[k, i], r.sum_send.at[k, i], r.sum_recv.at[k, i], d_peers[i])
                for i in range(n_dp - 1)]

    def sum_z_copies(k):
        return [remote(sum_mid.at[k], sum_z.at[k, i], r.sumz_send.at[k, i], r.sumz_recv.at[k, i], z_peers[i])
                for i in z_range]

    def sum_middle(k):
        arrive_all(sum_copies(k))
        total = sums[k]
        for i in range(n_dp - 1):
            total = total + sum_buf[k, i]
        sum_mid[k] = total
        start_all(sum_z_copies(k))

    def sum_end(k):
        arrive_all(sum_z_copies(k))
        total = sum_mid[k]
        for i in z_range:
            total = total + sum_z[k, i]
        sum_mid_out = r.sum_out
        sum_mid_out[k] = total

    start_all(edge_copies(glu, 0))
    arrive_all(tap_copies)
    arrive_all(edge_copies(glu, 0))
    sent_all(edge_copies(glu, 0))
    close_edges(glu)
    size = 64

    def sweep(ref, j, first, backward):
        total = None
        for k in range(KERNEL):
            offset = EDGE - HALF + (KERNEL - 1 - k if backward else k)
            term = taps[j, k:k + 1, :] * ref[j, pl.ds(first + offset, size), :]
            total = term if total is None else total + term
        return total

    def convolve(j):
        def part_step(k, carry):
            first = pl.multiple_of(k * size, size)
            value = sweep(glu, j, first, False)
            bhat[j, pl.ds(first + EDGE, size), :] = value
            return (carry[0] + jnp.sum(value, axis=0, keepdims=True),
                    carry[1] + jnp.sum(value * value, axis=0, keepdims=True))
        zero = jnp.zeros((1, w), f32)
        one, two = lax.fori_loop(0, rows // size, part_step, (zero, zero))
        sums[0, pl.ds(2 * j, 1), :] = one
        sums[0, pl.ds(2 * j + 1, 1), :] = two
    loop(n_t, convolve)
    start_all(sum_copies(0))
    sum_middle(0)
    sum_end(0)

    def bn_parts(j):
        mean = r.sum_out[0, pl.ds(2 * j, 1), :] / row_count
        square = r.sum_out[0, pl.ds(2 * j + 1, 1), :] / row_count
        return mean, lax.rsqrt(square - mean * mean + norm_eps), taps[j, KERNEL:KERNEL + 1, :], taps[
            j, KERNEL + 1:KERNEL + 2, :]

    z_s[...] = jnp.zeros_like(z_s)

    def activate(j):
        mean, inverse, bn_gain, bn_shift = bn_parts(j)
        scaled = (bhat[j, inner, :] - mean) * inverse
        bhat[j, inner, :] = scaled
        normal = scaled * bn_gain + bn_shift
        act[j] = (normal * sigmoid(normal)).astype(bf16)
        z_s[...] = z_s[...] + dot(act[j], wbuf[3, :, block_of(j, width)][:, 3 * w:4 * w], 1, 1)
    loop(n_t, activate)
    start_all(edge_copies(bhat, 1))

    a4, dx = r.a4, r.dx0

    def norm_four(part):
        value = x2[part, :] + z_s[part, :]
        x3[part, :] = value
        a4[part, :] = (norm_parts(value)[0] * gains[3:4, :]).astype(bf16)
    row_loop(rows, 64, norm_four)
    feed_rows(a4, wbuf.at[4], wbuf.at[5], z_s, r.hid2, r.slope2)
    gsum = r.gsum
    gsum[0] = jnp.zeros_like(gsum[0])
    dz, dz_turn, a_turn = r.dz, r.dz_turn, r.a_turn

    def add_gain(row, part_sum):
        gsum[0, row:row + 1, :] = gsum[0, row:row + 1, :] + part_sum

    def norm_five(part):
        value = x3[part, :] + 0.5 * z_s[part, :]
        scaled, grad_in, part_sum = norm_back(value, r.og[part, :].astype(f32), gains[4:5, :])
        r.out[part, :] = scaled * gains[4:5, :]
        dx[part, :] = grad_in
        dz[part, :] = (0.5 * grad_in).astype(bf16)
        add_gain(4, part_sum)
    row_loop(rows, 64, norm_five)

    def grad_chunk(c):
        return gbuf.at[c - 2] if c >= 2 else wbuf.at[c + 4]

    def join_norm(row, x_of, factor):
        def step(part):
            _, grad_in, part_sum = norm_back(x_of(part), z_s[part, :], gains[row:row + 1, :])
            value = dx[part, :] + grad_in
            dx[part, :] = value
            dz[part, :] = (factor * value).astype(bf16)
            add_gain(row, part_sum)
        row_loop(rows, 64, step)

    folds = [order[::-1] for order in links]
    groups = span(links[0])
    core_buf, dp_buf, z_buf = r.core_buf, r.dp_buf, r.z_buf

    def grad_rows(c, mask):
        return grad_chunk(c).at[pl.ds(pl.multiple_of(flip(d, mask) * rows_w, rows_w), rows_w), :]

    def core_copies(c):
        return [remote(grad_rows(c, mask ^ CORE), core_buf.at[c, k], r.core_send.at[c, k], r.core_recv.at[c, k],
                       (flip(d, CORE), t)) for k, mask in enumerate(groups)]

    def fold_moves(c, stage):
        moves = []
        for h in range(2):
            bit = folds[h][stage]
            masks = span(folds[h][stage + 1:])
            base = len(groups) - 2 * len(masks)
            for j, mask in enumerate(masks):
                slot = base + j
                copy = remote(grad_rows(c, mask ^ bit).at[:, pl.ds(h * half, half)], dp_buf.at[c, h, slot],
                              r.fd_send.at[c, h, slot], r.fd_recv.at[c, h, slot], (flip(d, bit), t))
                moves.append((copy, mask, h, slot))
        return moves

    def fold_copies(c, stage):
        return [move[0] for move in fold_moves(c, stage)]

    def fold_z_copies(c):
        copies = []
        for k in z_range:
            target = lax.rem(t + k + 1, n_t)
            source = grad_rows(c, 0).at[:, pl.ds(pl.multiple_of(target * width, width), width)]
            copies.append(remote(source, z_buf.at[c, k], r.fz_send.at[c, k], r.fz_recv.at[c, k], z_peers[k]))
        return copies

    piece = 16

    def fold_start(c):
        start_all(core_copies(c))

    def fold_next(c, stage):
        if stage < n_link:
            start_all(fold_copies(c, stage))
        else:
            start_all(fold_z_copies(c))

    def fold_step(c, stage):
        ref = grad_chunk(c)
        if stage == 0:
            arrive_all(core_copies(c))
            for k, mask in enumerate(groups):
                base = flip(d, mask) * rows_w

                def add_core(step, k=k, base=base):
                    part = pl.ds(pl.multiple_of(base + step * piece, piece), piece)
                    ref[part, :] = (ref[part, :].astype(f32)
                                    + core_buf[c, k, block_of(step, piece), :].astype(f32)).astype(bf16)
                loop(rows_w // piece, add_core)
            fold_next(c, 0)
        elif stage <= n_link:
            for copy, mask, h, slot in fold_moves(c, stage - 1):
                copy.wait_recv()
                base = flip(d, mask) * rows_w
                cols = pl.ds(h * half, half)

                def add_dp(step, base=base, cols=cols, h=h, slot=slot):
                    part = pl.ds(pl.multiple_of(base + step * piece, piece), piece)
                    ref[part, cols] = (ref[part, cols].astype(f32)
                                       + dp_buf[c, h, slot, block_of(step, piece), :].astype(f32)).astype(bf16)
                loop(rows_w // piece, add_dp)
            fold_next(c, stage)
        else:
            arrive_all(fold_z_copies(c))

            def finish(step):
                part = pl.ds(pl.multiple_of(d * rows_w + step * piece, piece), piece)
                total = ref[part, block_of(t, width)].astype(f32)
                for k in z_range:
                    total = total + z_buf[c, k, block_of(step, piece), :].astype(f32)
                r.shards[c, block_of(step, piece), :] = total
            loop(rows_w // piece, finish)

    final = n_link + 1

    dz_turn[...] = turned(dz[...])
    a_turn[...] = turned(a4[...])
    sent_all([copy for c in range(CHUNKS) for copy in z_copies(c)])
    sent_all([copy for c in range(CHUNKS) for stage in range(stages) for copy in dp_copies(c, stage)])
    feed_back(dz, dz_turn, a_turn, wbuf.at[4], wbuf.at[5], z_s, r.hid2, r.slope2, grad_chunk(4), grad_chunk(5))
    fold_start(4)
    fold_start(5)
    join_norm(3, lambda part: x3[part, :], 1.0)

    dz_turn[...] = turned(dz[...])

    def act_back(j):
        mean, inverse, bn_gain, bn_shift = bn_parts(j)
        grad_act = dot(dz[...], wbuf[3, :, block_of(j, width)][:, 3 * w:4 * w], 1, 0)
        scaled = bhat[j, inner, :]
        normal = scaled * bn_gain + bn_shift
        sig_n = sigmoid(normal)
        value = grad_act * (sig_n * (1.0 + normal * (1.0 - sig_n)))
        dbn[j, inner, :] = value
        sums[1, pl.ds(2 * j, 1), :] = jnp.sum(value * scaled, axis=0, keepdims=True)
        sums[1, pl.ds(2 * j + 1, 1), :] = jnp.sum(value, axis=0, keepdims=True)
    loop(n_t, act_back)
    start_all(sum_copies(1))
    start_all(edge_copies(dbn, 2))
    fold_step(4, 0)
    sum_middle(1)
    fold_step(5, 0)
    a_turn[...] = turned(a3[...])
    sum_end(1)
    for k, ref in ((1, bhat), (2, dbn)):
        arrive_all(edge_copies(ref, k))
        sent_all(edge_copies(ref, k))
    r.bn_out[...] = r.sum_out[1, pl.ds(2 * t, 2), :]
    small = r.small
    z_s[...] = jnp.zeros_like(z_s)

    def put_grad(c, j, first, value):
        if w % 128 == 0:
            grad_chunk(c)[:, pl.ds(pl.multiple_of(j * width + first, 128), value.shape[1])] = value
        else:
            old = grad_chunk(c)[:, block_of(j, width)]
            pieces = [old[:, :first], value, old[:, first + value.shape[1]:]]
            grad_chunk(c)[:, block_of(j, width)] = jnp.concatenate([p for p in pieces if p.shape[1] > 0], axis=1)

    def conv_back(j):
        mean, inverse, bn_gain, bn_shift = bn_parts(j)
        gamma = r.sum_out[1, pl.ds(2 * j, 1), :] / row_count
        beta = r.sum_out[1, pl.ds(2 * j + 1, 1), :] / row_count
        dbn[j] = bn_gain * inverse * (dbn[j] - beta - bhat[j] * gamma)
        dbn[j, pl.ds(0, EDGE), :] = jnp.where(t > 0, dbn[j, pl.ds(0, EDGE), :], 0.0)
        tail = pl.ds(EDGE + rows, EDGE)
        dbn[j, tail, :] = jnp.where(t < n_t - 1, dbn[j, tail, :], 0.0)

        def tap_step(k, carry):
            first = pl.multiple_of(k * size, size)
            own_part = dbn[j, pl.ds(first + EDGE, size), :]
            result = []
            for tap in range(KERNEL):
                term = own_part * glu[j, pl.ds(first + EDGE - HALF + tap, size), :]
                result.append(carry[tap] + jnp.sum(term.reshape(size // 8, 8, w), axis=0))
            return tuple(result)
        tap_sums = lax.fori_loop(0, rows // size, tap_step, tuple(jnp.zeros((8, w), f32) for _ in range(KERNEL)))
        for tap in range(KERNEL):
            small[0, j, tap:tap + 1, :] = jnp.sum(tap_sums[tap], axis=0, keepdims=True)

        def spread_step(k):
            first = pl.multiple_of(k * size, size)
            part = pl.ds(first, size)
            dglu = sweep(dbn, j, first, True)
            sig_p = sig[j, part, :]
            grad_val = dglu * sig_p
            r.de[part, 0:w] = grad_val.astype(bf16)
            r.de[part, w:2 * w] = (grad_val * val[j, part, :] * (1.0 - sig_p)).astype(bf16)
        loop(rows // size, spread_step)
        put_grad(3, j, 0, dot(a_turn[...], r.de[...], 1, 0).astype(bf16))
        put_grad(3, j, 3 * w, dot(dz_turn[...], act[j], 1, 0).astype(bf16))
        z_s[...] = z_s[...] + dot(r.de[...], wbuf[3, :, block_of(j, width)][:, 0:2 * w], 1, 1)
    loop(n_t, conv_back)
    fold_step(4, 1)
    fold_step(5, 1)
    join_norm(2, lambda part: x2[part, :], 1.0)

    dz_turn[...] = turned(dz[...])
    loop(n_t, lambda j: put_grad(3, j, 2 * w, dot(dz_turn[...], mix[j], 1, 0).astype(bf16)))
    fold_start(3)
    a2_turn, ds_s, rf_acc, rf_buf = r.a2_turn, r.ds_s, r.rf_acc, r.rf_buf
    for part in range(n_t):
        a2_turn[:, part * rows:(part + 1) * rows] = turned(a2_all[part])
    z_s[...] = jnp.zeros_like(z_s)
    rf_acc[...] = jnp.zeros_like(rf_acc)
    for stage in range(2, final + 1):
        fold_step(4, stage)
        fold_step(5, stage)

    def head_back(j):
        cols = block_of(j, width)
        block = wbuf[2, :, cols]
        dmix = dot(dz[...], wbuf[3, :, cols][:, 2 * w:3 * w], 1, 0)
        dmix_turn = dmix.T.astype(bf16)
        dmix = dmix.astype(bf16)
        cq_turn, pq_turn = turned(cq[j]), turned(pq[j])
        for h in range(local_heads):
            mask = head_mask((rows, w), 1, head_dim, h)
            turn_mask = head_mask((w, rows), 0, head_dim, h)
            head = j * local_heads + h
            s_s[...] = dot(keep(mask, dmix), kv[j, :, w:2 * w], 1, 1)

            def soft_back(part):
                p = probs[head, part, :].astype(f32)
                g = s_s[part, :]
                ds_s[part, :] = (p * (g - jnp.sum(p * g, axis=-1, keepdims=True))).astype(bf16)
            row_loop(rows, 32, soft_back)
            dv_h = dot(keep(turn_mask, dmix_turn), probs[head], 1, 0)
            dk_h = dot(keep(turn_mask, cq_turn), ds_s[...], 1, 0)
            dcq_h = keep(mask, dot(ds_s[...], kv[j, :, 0:w], 1, 0))
            back = dot(ds_s[...], phase[...], 1, 0)
            spun(back[:, :D // 2], back[:, D // 2:])
            dpq_h = keep(mask, dot(u_s[...], block[:, 3 * w:4 * w], 1, 0))
            pos_h = dot(keep(turn_mask, pq_turn), u_s[...], 1, 0)
            if h == 0:
                dv, dk, dcq, dpq, pos = dv_h, dk_h, dcq_h, dpq_h, pos_h
            else:
                dv, dk, dcq, dpq, pos = dv + dv_h, dk + dk_h, dcq + dcq_h, dpq + dpq_h, pos + pos_h
        dcq = dcq * scale
        dpq = dpq * scale
        small[0, j, KERNEL:KERNEL + 1, :] = jnp.sum(dcq, axis=0, keepdims=True)
        small[0, j, KERNEL + 1:KERNEL + 2, :] = jnp.sum(dpq, axis=0, keepdims=True)
        dq = (dcq + dpq).astype(bf16)
        dkv_turn = r.dkv_turn
        dkv_turn[0:w, :] = (dk * scale).astype(bf16)
        dkv_turn[w:2 * w, :] = dv.astype(bf16)
        for part in range(n_t):
            dkv = turned(dkv_turn[:, part * rows:(part + 1) * rows])
            rf_acc[part] = rf_acc[part] + dot(dkv, block[:, w:3 * w], 1, 1)
        z_s[...] = z_s[...] + dot(dq, block[:, 0:w], 1, 1)
        put_grad(2, j, 0, dot(a2_turn[:, block_of(t, rows)], dq, 1, 0).astype(bf16))
        put_grad(2, j, w, dot(a2_turn[...], dkv_turn[...], 1, 1).astype(bf16))
        put_grad(2, j, 3 * w, (pos.T * scale).astype(bf16))
    loop(n_t, head_back)

    for part in range(n_t):
        probs[part, :, 0:D] = rf_acc[part].astype(bf16)
    rf_copies = [remote(probs.at[lax.rem(t + k + 1, n_t), :, pl.ds(0, D)], rf_buf.at[k], r.rf_ss.at[k], r.rf_rs.at[k],
                        z_peers[k]) for k in z_range]
    start_all(rf_copies)
    fold_start(2)
    small_buf, small_z = r.small_buf, r.small_z
    all_bits = [CORE] + links[0]

    def small_copy(k):
        return remote(small.at[k], small_buf.at[k], r.s_send.at[k], r.s_recv.at[k], (flip(d, all_bits[k]), t))

    small_z_copies = [remote(small.at[len(all_bits), lax.rem(t + k + 1, n_t)], small_z.at[k], r.sz_send.at[k],
                             r.sz_recv.at[k], z_peers[k]) for k in z_range]
    small_copy(0).start()
    fold_step(3, 0)
    fold_step(2, 0)
    for k in range(1, len(all_bits) + 1):
        small_copy(k - 1).wait_recv()
        small[k] = small[k - 1] + small_buf[k - 1]
        if k < len(all_bits):
            small_copy(k).start()
    start_all(small_z_copies)
    a_turn[...] = turned(a1[...])
    fold_step(3, 1)
    fold_step(2, 1)
    arrive_all(rf_copies)

    def join_rows(part):
        total = z_s[part, :] + rf_acc[t, part, :]
        for k in z_range:
            total = total + rf_buf[k, part, :].astype(f32)
        z_s[part, :] = total
    row_loop(rows, 64, join_rows)
    join_norm(1, lambda part: x1[part, :], 0.5)

    dz_turn[...] = turned(dz[...])
    feed_back(dz, dz_turn, a_turn, wbuf.at[0], wbuf.at[1], z_s, r.hid1, r.slope1, grad_chunk(0), grad_chunk(1))
    fold_start(0)
    fold_start(1)
    join_norm(0, lambda part: x_ref[part, :].astype(f32), 1.0)

    def gsum_copy(k):
        return remote(gsum.at[k], r.gsum_buf.at[k], r.g_send.at[k], r.g_recv.at[k], (flip(d, all_bits[k]), t))

    gsum_z_copies = [remote(gsum.at[len(all_bits)], r.gsum_z.at[k], r.gz_send.at[k], r.gz_recv.at[k],
                            z_peers[k]) for k in z_range]
    gsum_copy(0).start()
    for stage in range(2, final + 1):
        fold_step(3, stage)
        fold_step(2, stage)
    for k in range(1, len(all_bits) + 1):
        gsum_copy(k - 1).wait_recv()
        gsum[k] = gsum[k - 1] + r.gsum_buf[k - 1]
        if k < len(all_bits):
            gsum_copy(k).start()
    start_all(gsum_z_copies)
    for stage in range(final + 1):
        fold_step(0, stage)
        fold_step(1, stage)
    arrive_all(small_z_copies)
    total = small[len(all_bits), t]
    for k in z_range:
        total = total + small_z[k]
    r.small_out[...] = total
    arrive_all(gsum_z_copies)
    total_g = gsum[len(all_bits)]
    for k in z_range:
        total_g = total_g + r.gsum_z[k]
    spot_g = lax.dot_general(total_g, gain_spot, (((1,), (1,)), ((), ())), precision=high, preferred_element_type=f32)
    r.gain_out[...] = spot_g

    sent_all(tap_copies + a_copies + rf_copies + small_z_copies + gsum_z_copies)
    sent_all(e_copies(0, n_t + n_link))
    for k in range(2):
        sent_all(sum_copies(k) + sum_z_copies(k))
    for k in range(len(all_bits)):
        small_copy(k).wait_send()
        gsum_copy(k).wait_send()
    for c in range(CHUNKS):
        sent_all(core_copies(c) + fold_z_copies(c))
        for stage in range(n_link):
            sent_all(fold_copies(c, stage))


def layer_kernel(n_dp, n_t, head_dim, inputs):
    given = SimpleNamespace(**inputs)
    rows, D = given.x.shape
    rows_w, width = given.fu.shape
    w = D // n_t
    frames = rows * n_t
    heads = D // head_dim
    hidden = n_t * width
    n_bits = n_dp.bit_length() - 1
    n_e = n_t - 1 + n_bits
    n_gain = given.gain_in.shape[1]
    tap_rows = given.tap_in.shape[0]
    groups = n_dp // 2
    z = n_t - 1
    sem = pltpu.SemaphoreType.DMA
    vm = pltpu.VMEM
    outs = dict(
        out=((rows, D), f32), dx0=((rows, D), f32), gain_out=((8, n_gain), f32),
        shards=((CHUNKS, rows_w, width), f32), small_out=((tap_rows, w), f32), bn_out=((2, w), f32))
    edge_shape = (n_t, rows + 2 * EDGE, w)
    scratch = dict(
        pack=vm((CHUNKS, rows_w, width), bf16), wbuf=vm((CHUNKS, n_dp * rows_w, hidden), bf16),
        gbuf=vm((CHUNKS - 2, n_dp * rows_w, hidden), bf16), gains=vm((8, D), f32),
        taps=vm((n_t, tap_rows, w), f32), e_acc=vm((n_bits + 2, 8, D), f32), e_buf=vm((n_e, 8, D), f32),
        phase=vm((frames, D), bf16), spin=vm((2, rows, D // 2), f32), u_s=vm((rows, D), bf16),
        z_s=vm((rows, D), f32), x1=vm((rows, D), f32), x2=vm((rows, D), f32),
        x3=vm((rows, D), f32), a1=vm((rows, D), bf16), a2=vm((rows, D), bf16), a3=vm((rows, D), bf16),
        a4=vm((rows, D), bf16), dz=vm((rows, D), bf16), dz_turn=vm((D, rows), bf16),
        a_turn=vm((D, rows), bf16), a2_all=vm((n_t, rows, D), bf16), a2_turn=vm((D, frames), bf16),
        hid1=vm((rows, hidden), bf16), slope1=vm((rows, hidden), bf16), hid2=vm((rows, hidden), bf16),
        slope2=vm((rows, hidden), bf16), kv=vm((n_t, frames, 2 * w), bf16), cq=vm((n_t, rows, w), bf16),
        pq=vm((n_t, rows, w), bf16), mix=vm((n_t, rows, w), bf16), probs=vm((heads, rows, frames), bf16),
        s_s=vm((rows, frames), f32), ds_s=vm((rows, frames), bf16), dkv_turn=vm((2 * w, frames), bf16),
        rf_acc=vm((n_t, rows, D), f32), rf_buf=vm((z, rows, D), bf16),
        glu=vm(edge_shape, f32), bhat=vm(edge_shape, f32), dbn=vm(edge_shape, f32),
        val=vm((n_t, rows, w), f32), sig=vm((n_t, rows, w), f32), act=vm((n_t, rows, w), bf16),
        de=vm((rows, 2 * w), bf16), sums=vm((2, 2 * n_t, w), f32), sum_mid=vm((2, 2 * n_t, w), f32),
        sum_out=vm((2, 2 * n_t, w), f32), sum_buf=vm((2, n_dp - 1, 2 * n_t, w), f32),
        sum_z=vm((2, z, 2 * n_t, w), f32), core_buf=vm((CHUNKS, groups, rows_w, hidden), bf16),
        dp_buf=vm((CHUNKS, 2, groups - 1, rows_w, hidden // 2), bf16), z_buf=vm((CHUNKS, z, rows_w, width), bf16),
        small=vm((n_bits + 1, n_t, tap_rows, w), f32), small_buf=vm((n_bits, n_t, tap_rows, w), f32),
        small_z=vm((z, tap_rows, w), f32), gsum=vm((n_bits + 1, 8, D), f32), gsum_buf=vm((n_bits, 8, D), f32),
        gsum_z=vm((z, 8, D), f32), local_sem=sem((CHUNKS,)))
    scratch.update(
        z_send=sem((CHUNKS, z)), z_recv=sem((CHUNKS, z)),
        d_send=sem((CHUNKS, 2, n_dp - 1)), d_recv=sem((CHUNKS, 2, n_dp - 1)),
        f_send=sem((z,)), f_recv=sem((z,)),
        e_send=sem((n_e,)), e_recv=sem((n_e,)),
        a_send=sem((z,)), a_recv=sem((z,)),
        edge_send=sem((3, 2)), edge_recv=sem((3, 2)),
        sum_send=sem((2, n_dp - 1)), sum_recv=sem((2, n_dp - 1)),
        sumz_send=sem((2, z)), sumz_recv=sem((2, z)),
        core_send=sem((CHUNKS, groups)), core_recv=sem((CHUNKS, groups)),
        fd_send=sem((CHUNKS, 2, groups - 1)), fd_recv=sem((CHUNKS, 2, groups - 1)),
        fz_send=sem((CHUNKS, z)), fz_recv=sem((CHUNKS, z)),
        rf_ss=sem((z,)), rf_rs=sem((z,)),
        s_send=sem((n_bits,)), s_recv=sem((n_bits,)),
        sz_send=sem((z,)), sz_recv=sem((z,)),
        g_send=sem((n_bits,)), g_recv=sem((n_bits,)),
        gz_send=sem((z,)), gz_recv=sem((z,)))
    names = list(inputs) + list(outs) + list(scratch)
    vmem = pl.BlockSpec(memory_space=pltpu.VMEM)
    result = pl.pallas_call(
        functools.partial(layer_body, names, n_dp, n_t, head_dim),
        name="layer",
        out_shape=tuple(jax.ShapeDtypeStruct(dims, kind) for dims, kind in outs.values()),
        in_specs=[vmem] * len(inputs),
        out_specs=(vmem,) * len(outs),
        scratch_shapes=list(scratch.values()),
        compiler_params=pltpu.CompilerParams(collective_id=0, has_side_effects=True, vmem_limit_bytes=67043328),
    )(*inputs.values())
    return SimpleNamespace(**dict(zip(outs, result)))


def angle_tables(frames, width):
    step = 32
    frequency = np.exp(np.arange(width // 2) * (-2.0 * math.log(10000.0) / width))
    coarse = np.arange(frames // step)[:, None] * step * frequency
    fine = np.arange(step)[:, None] * frequency
    return jnp.asarray(np.stack([np.sin(coarse), np.cos(coarse), np.sin(fine), np.cos(fine)]), f32)


def per_device(n_dp, n_t, inputs, out_grad, norm_gains, first_up, first_down, attend_in, attend_out, position_bias,
               convolve_in, depth_kernel, batch_norm, convolve_out, second_up, second_down):
    rows, D = inputs.shape
    w = attend_in.shape[2]
    R = attend_in.shape[1]
    n_bias = position_bias.shape[2]
    local_heads = position_bias.shape[1]
    head_dim = n_bias * n_dp
    n_gain = norm_gains.shape[1]
    d = lax.axis_index("dp")
    gain_in = jnp.concatenate([norm_gains, position_bias.astype(f32).reshape(2, local_heads * n_bias),
                               jnp.zeros((1, n_gain), f32)])
    tap_in = jnp.concatenate([depth_kernel.T, batch_norm, jnp.zeros((7, w), f32)], axis=0)
    got = layer_kernel(n_dp, n_t, head_dim, dict(
        fu=first_up, fd=first_down, at=attend_in, cw=convolve_in.reshape(R, 2 * w), ao=attend_out,
        co=convolve_out, su=second_up, sd=second_down, gain_in=gain_in, tap_in=tap_in, x=inputs,
        og=out_grad, tab=angle_tables(rows * n_t, D)))
    shards, small = got.shards, got.small_out
    grad_bias = small[KERNEL:KERNEL + 2].reshape(2, local_heads, head_dim)
    grad_bias = lax.dynamic_slice_in_dim(grad_bias, d * n_bias, n_bias, 2)
    return (
        got.out, got.dx0, got.gain_out[:5],
        shards[0], shards[1].T, shards[2].reshape(R, 4, w).transpose(1, 0, 2), shards[3][:, 2 * w:3 * w].T, grad_bias,
        shards[3][:, :2 * w].reshape(R, 2, w), small[:KERNEL].T, got.bn_out,
        shards[3][:, 3 * w:].T, shards[4], shards[5].T)


def solution(mesh):
    n_dp, n_t = mesh.shape["dp"], mesh.shape["tensor"]
    row = P(("dp", "tensor"), None)
    gain = P(None, ("dp", "tensor"))
    up = P("dp", "tensor")
    down = P("tensor", "dp")
    weights = (up, down, P(None, "dp", "tensor"), down, P(None, "tensor", "dp"), P("dp", None, "tensor"),
               P("tensor", None), P(None, "tensor"), down, up, down)
    return jax.shard_map(
        functools.partial(per_device, n_dp, n_t), mesh=mesh,
        in_specs=(row, row, gain) + weights,
        out_specs=(row, row, gain) + weights,
        check_vma=False)
```

time: 1570 us -> 271 us (0.17)
  waiting for transfers between devices: 873 us -> 0 us
  Pallas kernels: 0 us -> 254 us
  local copies, waits for them, and re-layouts: 243 us -> 14.5 us
  blocking collectives: 206 us -> 0 us
  matrix products: 126 us -> 0 us
  other arithmetic: 58.3 us -> 1.34 us
  loops' own time: 30 us -> 0 us
  between operations: 17.8 us -> 0.71 us
    reduce_scatter x15 -> x0, waiting for transfers between devices: 608 us -> none  [the longest x8 340 us: fold_rows(): lax.psum_scatter(lax.dot_general(source, weight, (((1,), (contract,)), ((...]
    pallas_call x0 -> x1, Pallas kernels: none -> 254 us  [layer_kernel(): pl.pallas_call(functools.partial(layer_body, names, n_dp, n_t, head_dim),...]
    all_gather x10 -> x0, blocking collectives: 156 us -> none  [the longest x1 70.9 us: per_device(): gain_rows = lax.all_gather(norm_gains, ('dp', 'tensor'), axis=1, tiled=True)]
    unnamed x27 -> x0, waiting for transfers between devices: 137 us -> none
    reshape x14 -> x3, local copies, waits for them, and re-layouts: 134 us -> 0.83 us  [the longest x1 0.66 us: per_device(): shards[3][:, :2 * w].reshape(R, 2, w)]
    all_gather x8 -> x0, waiting for transfers between devices: 129 us -> none  [spread_rows(): return lax.all_gather(row_block, 'tensor', axis=0, tiled=True)]
    dot_general x47 -> x0, matrix products: 124 us -> none  [the longest x8 19.4 us: contract_rows(): lax.dot_general(left, right, (((0,), (0,)), ((), ())), preferred_element_...]
    slice x11 -> x2, local copies, waits for them, and re-layouts: 42.2 us -> 0.71 us  [the longest x1 0.7 us: per_device(): grad_bias = small[KERNEL:KERNEL + 2].reshape(2, local_heads, head_dim)]
  transfers between devices with their start and end apart: 25 -> 0, of which waited for: 24 -> 0; matrix products, arithmetic and copies ran while one was open for 3% -> 0% of each run, Pallas kernels for 0% -> 0%
where the time goes in v3:
time: 271 us; the launch traced here: 270 us
  Pallas kernels  254 us (94%)
  local copies, waits for them, and re-layouts  14.5 us (5%)
    pallas_call x1, Pallas kernels, layer_kernel(): pl.pallas_call(functools.partial(layer_body, names, n_dp, n_t, head_dim),...  254 us
    unnamed x35, local copies, waits for them, and re-layouts  7.48 us

profile of v3, /device:TPU:0, one launch (start us, length us, event | category | flops | bytes accessed | tf_op | source)
XLA Modules:
  0.0 270.3 jit_solution(2594751083121085434)
XLA Ops:
  0.8 0.5 copy-done.11
  1.3 0.1 reshape.49
  1.4 0.7 maximum_maximum_fusion.1.all_refs_8_
  2.1 0.7 maximum_maximum_fusion.all_refs_9_
  2.8 0.7 copy.30.all_refs_4_
  3.6 0.6 copy.38
  4.2 0.7 copy.31.all_refs_5_
  4.9 0.8 copy.29.all_refs_1_
  5.7 0.1 copy-done.3
  5.8 0.8 copy.32.all_refs_7_
  6.5 253.7 %layer.1 = (f32[256,512]{1,0:T(8,128)}, f32[256,512]{1,0:T(8,128)}, f32[8,16]{1,0:T(8,128)}, f32[6,64,512]{2,1,0:T(8,128)}, f32[40,128]{1,0:T(8,128)}, /*index=5*/f32[2,128]{1,0:T(2,128)}) custom-call(bf16[64,512]{1,0:T(8,128)(2,1)} %all_refs_0_.1, bf16[512,64]{1,0:T(8,128)(2,1)} %copy.29.all_refs_1_, bf16[4,64,128]{2,1,0:T(8,128)(2,1)} %all_refs_2_.1, ...), custom_call_target="tpu_custom_call" | custom-call | tf_op jit(solution)/shard_map/layer/pallas_call | solution.py:873
  260.3 0.7 slice.44
  261.0 1.3 slice_bitcast_fusion.7
  262.3 0.1 reshape.46
  262.4 0.7 constant_dynamic-slice_fusion
  263.0 2.0 slice_bitcast_fusion
  265.0 0.6 slice_bitcast_fusion.5
  265.7 0.7 reshape.47
  266.4 0.7 copy.37
  267.1 0.8 copy.43
  267.9 0.4 copy-done
  268.3 0.8 copy.44
  269.1 0.6 copy.45
  269.7 0.6 copy.46
  (28 shorter events, 0.3 us)
Async XLA Ops:
  0.7 1.4 copy-start.7
  0.7 0.7 copy-start.11
  0.7 0.8 copy-start.8
  1.4 0.7 copy-start.10
  2.1 0.7 copy-start.5
  2.8 0.8 copy-start.4
  2.8 1.4 copy-start.6
  3.6 1.4 copy-start.2
  4.9 0.8 copy-start.3
  265.0 2.0 copy-start.1
  267.1 1.2 copy-start
  268.3 0.8 copy-start.9
  269.1 0.6 copy-start.12

commit v4 on v3

v4 whole, which is shorter than its diff:
```python
import functools
import math
from types import SimpleNamespace

import jax
import jax.numpy as jnp
import numpy as np
from jax import lax
from jax.experimental import pallas as pl
from jax.experimental.pallas import tpu as pltpu
from jax.sharding import PartitionSpec as P

MESH = pl.DeviceIdType.MESH
CHUNKS = 6
CUTS = 2
AHEAD = 2
CORE = 1
EDGE = 16
KERNEL = 31
HALF = KERNEL // 2
norm_eps = 1e-05
f32 = jnp.float32
bf16 = jnp.bfloat16
high = lax.Precision.HIGHEST


def flip(index, mask):
    result = index
    bit = 1
    while bit <= mask:
        if mask & bit:
            result = result + bit - 2 * bit * ((index // bit) % 2)
        bit *= 2
    return result


def span(bits):
    masks = [0]
    for bit in bits:
        masks = masks + [mask ^ bit for mask in masks]
    return masks


def link_orders(n_dp):
    bits = [1 << k for k in range(1, n_dp.bit_length() - 1)]
    return (bits, bits[::-1])


def greet(peers):
    barrier = pltpu.get_barrier_semaphore()
    for peer in peers:
        pl.semaphore_signal(barrier, inc=1, device_id=peer, device_id_type=MESH)
    pl.semaphore_wait(barrier, len(peers))


def remote(src, dst, send_sem, recv_sem, peer):
    return pltpu.make_async_remote_copy(
        src_ref=src, dst_ref=dst, send_sem=send_sem, recv_sem=recv_sem,
        device_id=peer, device_id_type=MESH)


def start_all(copies):
    for copy in copies:
        copy.start()


def settled(ref, sem, peer):
    remote(ref, ref, sem, sem, peer).wait_recv()


def arrive_all(copies):
    for copy in copies:
        copy.wait_recv()


def sent_all(copies):
    for copy in copies:
        copy.wait_send()


def dot(left, right, left_dim, right_dim):
    return lax.dot_general(left, right, (((left_dim,), (right_dim,)), ((), ())), preferred_element_type=f32)


def turned(value):
    return value.astype(f32).T.astype(bf16)


def head_mask(shape, axis, head_dim, head):
    place = lax.broadcasted_iota(jnp.int32, shape, axis)
    return (place >= head * head_dim) & (place < (head + 1) * head_dim)


def keep(mask, value):
    return jnp.where(mask, value, jnp.zeros_like(value))


def block_of(k, size):
    return pl.ds(pl.multiple_of(k * size, size), size)


def loop(count, body):
    def step(k, carry):
        body(k)
        return carry
    lax.fori_loop(0, count, step, 0)


def row_loop(rows, size, body):
    loop(rows // size, lambda k: body(block_of(k, size)))


def sigmoid(values):
    return 1.0 / (1.0 + jnp.exp(-values))


def norm_parts(values):
    centred = values - jnp.mean(values, axis=-1, keepdims=True)
    inverse = lax.rsqrt(jnp.mean(centred * centred, axis=-1, keepdims=True) + norm_eps)
    return centred * inverse, inverse


def norm_back(value, incoming, gain_row):
    scaled, inverse = norm_parts(value)
    grad_scaled = incoming * gain_row
    inner = jnp.mean(grad_scaled * scaled, axis=-1, keepdims=True)
    grad_in = inverse * (grad_scaled - jnp.mean(grad_scaled, axis=-1, keepdims=True) - scaled * inner)
    return scaled, grad_in, jnp.sum(incoming * scaled, axis=0, keepdims=True)


def tail_plan(final):
    parts = range(CUTS)
    plan = [((2, part), 1) for part in parts] + [((0, part), 0) for part in parts]
    for stage in range(1, final):
        plan += [((1, part), stage) for part in parts]
        if stage + 1 < final:
            plan += [((2, part), stage + 1) for part in parts]
        plan += [((0, part), stage) for part in parts]
    return plan + [((c, part), final) for c in (4, 5, 3, 2, 1, 0) for part in parts]


def relay_order(stages):
    hop, link_free, order = 1.5, 0.0, []
    units = [(c, part) for c in range(CHUNKS) for part in range(CUTS)]
    waiting = [(7.0 + 6.5 / CUTS * (k + 1), 0, u) for k, u in enumerate(units)]
    while waiting:
        waiting.sort()
        now, stage, u = waiting.pop(0)
        order.append((now, stage, u))
        if stage < stages - 1:
            link_free = max(now, link_free) + 3.1 / CUTS * 2 ** stage
            waiting.append((link_free + hop, stage + 1, u))
        elif stage == stages - 1:
            waiting.append((now + hop + 2.0 / CUTS, stages, u))
    return order


SLAB = 512
HBM = "_hbm"


def feed_rows(a_ref, up, down_t, z_ref, hidden, slope):
    z_ref[...] = jnp.zeros_like(z_ref)

    def step(k):
        cols = block_of(k, SLAB)
        pre = dot(a_ref[...], up[:, cols], 1, 0)
        sig = sigmoid(pre)
        hidden[:, cols] = (pre * sig).astype(bf16)
        slope[:, cols] = (sig * (1.0 + pre * (1.0 - sig))).astype(bf16)
        z_ref[...] = z_ref[...] + dot(hidden[:, cols], down_t[:, cols], 1, 1)
    loop(up.shape[1] // SLAB, step)


def feed_back(dz_ref, dz_turn, a_turn, up, down_t, z_ref, hidden, slope, g_up, g_down, start_down, middle):
    z_ref[...] = jnp.zeros_like(z_ref)

    def first_step(k):
        cols = block_of(k, SLAB)
        g_down[:, cols] = dot(dz_turn[...], hidden[:, cols], 1, 0).astype(bf16)
    loop(up.shape[1] // SLAB, first_step)
    start_down()
    slabs = up.shape[1] // SLAB

    def step(k):
        cols = block_of(k, SLAB)
        grad_pre = (dot(dz_ref[...], down_t[:, cols], 1, 0) * slope[:, cols].astype(f32)).astype(bf16)
        g_up[:, cols] = dot(a_turn[...], grad_pre, 1, 0).astype(bf16)
        z_ref[...] = z_ref[...] + dot(grad_pre, up[:, cols], 1, 1)
    loop(slabs - 1, step)
    middle()
    step(slabs - 1)


def layer_body(names, n_dp, n_t, head_dim, *all_refs):
    r = SimpleNamespace(**dict(zip(names, all_refs)))
    d = lax.axis_index("dp")
    t = lax.axis_index("tensor")
    pack, wbuf, gbuf = r.pack, r.wbuf, r.gbuf
    x_ref, gains, taps = r.x, r.gains, r.taps
    rows_w, width = pack.shape[1], pack.shape[2]
    rows, D = x_ref.shape
    w = D // n_t
    half = n_t * width // 2
    frames = rows * n_t
    local_heads = w // head_dim
    n_gain = r.gain_in.shape[1]
    n_bias = n_gain // local_heads
    row_count = frames * n_dp
    scale = head_dim ** -0.5
    links = link_orders(n_dp)
    orders = [order + [CORE] for order in links]
    stages = len(orders[0])
    n_link = len(links[0])
    z_peers = [(d, lax.rem(t + step, n_t)) for step in range(1, n_t)]
    d_peers = [(flip(d, mask), t) for mask in range(1, n_dp)]
    before = (d, lax.rem(t + n_t - 1, n_t))
    after = (d, lax.rem(t + 1, n_t))
    z_range = range(n_t - 1)
    leaving = [name for name in names if name.endswith(HBM)]

    def leave(*chosen):
        for ref in chosen:
            name = [one for one in leaving if getattr(r, one[:-len(HBM)]) is ref][0]
            k = leaving.index(name)
            pltpu.make_async_copy(ref, getattr(r, name), r.out_sem.at[k]).start()

    greet(z_peers + d_peers)

    def window(u, mask, start, size):
        c, part = u
        count = rows_w // CUTS
        first = pl.multiple_of(flip(d, mask) * rows_w + part * count, count)
        return wbuf.at[c, pl.ds(first, count), pl.ds(start, size)]

    def own(u):
        return window(u, 0, pl.multiple_of(t * width, width), width)

    def source(u):
        count = rows_w // CUTS
        return sources[u[0]].at[pl.ds(u[1] * count, count), :]

    sources = (r.fu, r.fd, pack.at[0], pack.at[1], r.su, r.sd)

    def z_copies(u):
        return [remote(source(u), own(u), r.z_send.at[0], r.z_recv.at[u[0], u[1]], z_peers[k])
                for k in z_range]

    def local_copy(u):
        return pltpu.make_async_copy(source(u), own(u), r.local_sem.at[u[0], u[1]])

    def dp_copies(u, stage):
        copies = []
        for h in range(2):
            bit = orders[h][stage]
            masks = span(orders[h][:stage])
            for mask in masks:
                part = window(u, mask, h * half, half)
                copies.append(remote(part, part, r.d_send.at[u[0]], r.d_recv.at[u[0], u[1], stage],
                                     (flip(d, bit), t)))
        return copies

    def send_unit(u):
        local_copy(u).start()
        start_all(z_copies(u))

    def allowed(done):
        return AHEAD + done + max(0, done - 3)

    queue = [(c, part) for c in range(CHUNKS) for part in range(CUTS)]

    e_acc, e_buf = r.e_acc, r.e_buf

    def e_copies(first, stop):
        copies = []
        for k in range(first, stop):
            if k < n_t - 1:
                source, peer = e_acc.at[0], z_peers[k]
            else:
                source, peer = e_acc.at[k - n_t + 2], (flip(d, orders[0][k - n_t + 1]), t)
            sem = max(0, k - n_t + 2)
            copies.append(remote(source, e_buf.at[k], r.e_send.at[sem], r.e_recv.at[sem], peer))
        return copies

    taps_own = r.taps_own
    tap_copies = [remote(taps_own, taps.at[t], r.f_send.at[0], r.f_recv.at[0], z_peers[k]) for k in z_range]

    entry = lax.broadcasted_iota(jnp.int32, (n_gain, D), 0)
    lane = lax.broadcasted_iota(jnp.int32, (n_gain, D), 1)
    gain_spot = (lane == (d * n_t + t) * n_gain + entry).astype(f32)
    e_acc[0] = jnp.zeros_like(e_acc[0])
    e_acc[0, 0:5, :] = jnp.dot(r.gain_in[...], gain_spot, precision=high, preferred_element_type=f32)
    entry_b = lax.broadcasted_iota(jnp.int32, (n_bias, D), 0)
    lane_b = lax.broadcasted_iota(jnp.int32, (n_bias, D), 1)
    bias_spots = [(lane_b == entry_b + d * n_bias + (h + t * local_heads) * head_dim).astype(f32)
                  for h in range(local_heads)]
    for pair in range(2):
        row = None
        for h in range(local_heads):
            term = jnp.dot(r.bias_in[pair, h:h + 1, :].astype(f32), bias_spots[h], precision=high,
                           preferred_element_type=f32)
            row = term if row is None else row + term
        e_acc[0, 5 + pair:6 + pair, :] = row
    start_all(e_copies(0, n_t - 1))
    for u in queue[:AHEAD]:
        send_unit(u)
    for k in range(4):
        pack[0, :, k * w:(k + 1) * w] = r.at[k]
    for k in range(2):
        pack[1, :, k * w:(k + 1) * w] = r.cw[:, k, :]
    pack[1, :, 2 * w:3 * w] = r.ao[...]
    pack[1, :, 3 * w:4 * w] = r.co[...]
    taps_own[...] = jnp.zeros_like(taps_own)
    taps_own[0:KERNEL, :] = r.tap_in[...]
    taps_own[KERNEL:KERNEL + 2, :] = r.bn_in[...]
    start_all(tap_copies)
    taps[t] = taps_own[...]

    def relay(stage, u):
        count = rows_w // CUTS
        if stage == 0:
            local_copy(u).wait()
            settled(wbuf.at[0, pl.ds(0, count), pl.ds(0, (n_t - 1) * width)], r.z_recv.at[u[0], u[1]], before)
            place = queue.index(u)
            for other in queue[allowed(place):allowed(place + 1)]:
                send_unit(other)
        else:
            settled(wbuf.at[0, pl.ds(0, count * 2 ** (stage - 1)), :], r.d_recv.at[u[0], u[1], stage - 1], before)
        if stage < stages:
            start_all(dp_copies(u, stage))

    def ready_after(order, chunks):
        places = [k + 1 for k, (_, stage, u) in enumerate(order) if stage == stages and u[0] in chunks]
        return max(places, default=0)

    e_step = [0]

    def e_next():
        k = e_step[0]
        if k == 0:
            settled(e_buf.at[pl.ds(0, n_t - 1)], r.e_recv.at[0], before)
            total = e_acc[0]
            for i in z_range:
                total = total + e_buf[i]
            e_acc[1] = total
        elif k <= n_link + 1:
            arrive_all(e_copies(n_t - 2 + k, n_t - 1 + k))
            e_acc[k + 1] = e_acc[k] + e_buf[n_t - 2 + k]
        if k <= n_link:
            start_all(e_copies(n_t - 1 + k, n_t + k))
        e_step[0] = k + 1

    tab, phase, spin = r.tab, r.phase, r.spin
    step_t = tab.shape[1]

    def table(k):
        cs, cc = tab[0, pl.ds(k, 1), :], tab[1, pl.ds(k, 1), :]
        part = block_of(k, step_t)
        phase[part, 0:D // 2] = (cs * tab[3] + cc * tab[2]).astype(bf16)
        phase[part, D // 2:D] = (cc * tab[3] - cs * tab[2]).astype(bf16)
    loop(frames // step_t, table)

    def own_table(k):
        place = t * (rows // step_t) + k
        cs, cc = tab[0, pl.ds(place, 1), :], tab[1, pl.ds(place, 1), :]
        part = block_of(k, step_t)
        spin[0, part, :] = cs * tab[3] + cc * tab[2]
        spin[1, part, :] = cc * tab[3] - cs * tab[2]
    loop(rows // step_t, own_table)

    def spun(sines, cosines):
        u_s = r.u_s
        u_s[:, 0:D // 2] = (cosines * spin[0] - sines * spin[1]).astype(bf16)
        u_s[:, D // 2:D] = (sines * spin[0] + cosines * spin[1]).astype(bf16)

    z_s, a1, a2, a2_all = r.z_s, r.a1, r.a2, r.a2_all
    x1, x2, x3 = r.x1, r.x2, r.x3
    events = relay_order(stages)
    ready = ready_after(events, (0, 1))
    for k, (_, stage, u) in enumerate(events[:ready]):
        relay(stage, u)
        if k % 4 == 3 and e_step[0] < n_link + 2:
            e_next()
    while e_step[0] < n_link + 2:
        e_next()
    gains[...] = e_acc[n_link + 2]

    def norm_one(part):
        a1[part, :] = (norm_parts(x_ref[part, :].astype(f32))[0] * gains[0:1, :]).astype(bf16)
    row_loop(rows, 64, norm_one)
    feed_rows(a1, wbuf.at[0], wbuf.at[1], z_s, r.hid1, r.slope1)

    def norm_two(part):
        value = x_ref[part, :].astype(f32) + 0.5 * z_s[part, :]
        x1[part, :] = value
        a2[part, :] = (norm_parts(value)[0] * gains[1:2, :]).astype(bf16)
    row_loop(rows, 64, norm_two)

    a_copies = [remote(a2, a2_all.at[t], r.a_send.at[0], r.a_recv.at[0], z_peers[k]) for k in z_range]
    start_all(a_copies)
    a2_all[t] = a2[...]
    for _, stage, u in events[ready:]:
        relay(stage, u)
    settled(a2_all.at[pl.ds(0, n_t - 1)], r.a_recv.at[0], before)
    kv, cq, pq, probs, mix, s_s, u_s = r.kv, r.cq, r.pq, r.probs, r.mix, r.s_s, r.u_s
    z_s[...] = jnp.zeros_like(z_s)
    inv_s = r.inv_s
    scale_low = jnp.asarray(scale, bf16)

    def head_group(j):
        cols = block_of(j, width)
        block = wbuf[2, :, cols]
        for part in range(n_t):
            kv[j, part * rows:(part + 1) * rows, :] = dot(a2_all[part], block[:, w:3 * w], 1, 0).astype(bf16)
        q = dot(a2[...], block[:, 0:w], 1, 0)
        if w % 128 == 0:
            bias = gains[5:7, block_of(j, w)]
        else:
            bias = gains[5:7, 0:w]
            for other in range(1, n_t):
                bias = jnp.where(j == other, gains[5:7, other * w:(other + 1) * w], bias)
        cq_j = (q + bias[0:1]).astype(bf16)
        pq_j = (q + bias[1:2]).astype(bf16)
        cq[j] = cq_j
        pq[j] = pq_j
        for h in range(local_heads):
            mask = head_mask((rows, w), 1, head_dim, h)
            spread = dot(keep(mask, pq_j), block[:, 3 * w:4 * w], 1, 1)
            spun(spread[:, :D // 2] * scale, spread[:, D // 2:] * scale)
            s_s[...] = dot(u_s[...], phase[...], 1, 1) + dot(keep(mask, cq_j) * scale_low, kv[j, :, 0:w], 1, 1)
            head = j * local_heads + h

            s = s_s[...]
            e = jnp.exp(s - jnp.max(s, axis=-1, keepdims=True))
            inv = 1.0 / jnp.sum(e, axis=-1, keepdims=True)
            probs[head] = e.astype(bf16)
            mixed = dot(probs[head], kv[j, :, w:2 * w], 1, 0) * inv
            inv = jnp.broadcast_to(inv, (rows, w))
            inverse = inv if h == 0 else jnp.where(mask, inv, inverse)
            mixture = mixed if h == 0 else jnp.where(mask, mixed, mixture)
        mix[j] = mixture
        inv_s[j] = inverse
        z_s[...] = z_s[...] + dot(mixture.astype(bf16), wbuf[3, :, cols][:, 2 * w:3 * w], 1, 1)
    loop(n_t, head_group)

    a3, glu, bhat, val, sig, act = r.a3, r.glu, r.bhat, r.val, r.sig, r.act
    dbn, sums, sum_buf, sum_mid, sum_z = r.dbn, r.sums, r.sum_buf, r.sum_mid, r.sum_z
    inner = pl.ds(EDGE, rows)

    def norm_three(part):
        value = x1[part, :] + z_s[part, :]
        x2[part, :] = value
        a3[part, :] = (norm_parts(value)[0] * gains[2:3, :]).astype(bf16)
    row_loop(rows, 64, norm_three)

    def gate(j):
        block = wbuf[3, :, block_of(j, width)]
        e = dot(a3[...], block[:, 0:2 * w], 1, 0)
        sig_j = sigmoid(e[:, w:2 * w])
        val[j] = e[:, 0:w]
        sig[j] = sig_j
        glu[j, inner, :] = e[:, 0:w] * sig_j
    loop(n_t, gate)

    def edge_copies(ref, k):
        first, last = pl.ds(EDGE, EDGE), pl.ds(rows, EDGE)
        return [remote(ref.at[:, first, :], ref.at[:, pl.ds(EDGE + rows, EDGE), :], r.edge_send.at[k, 0],
                       r.edge_recv.at[k, 0], before),
                remote(ref.at[:, last, :], ref.at[:, pl.ds(0, EDGE), :], r.edge_send.at[k, 1],
                       r.edge_recv.at[k, 1], after)]

    def edge_start(ref, k):
        back, ahead = edge_copies(ref, k)

        @pl.when(t > 0)
        def _():
            back.start()

        @pl.when(t < n_t - 1)
        def _():
            ahead.start()

        @pl.when(t == 0)
        def _():
            ref[:, pl.ds(0, EDGE), :] = jnp.zeros((n_t, EDGE, w), f32)

        @pl.when(t == n_t - 1)
        def _():
            ref[:, pl.ds(EDGE + rows, EDGE), :] = jnp.zeros((n_t, EDGE, w), f32)

    def edge_wait(ref, k):
        back, ahead = edge_copies(ref, k)

        @pl.when(t > 0)
        def _():
            ahead.wait_recv()
            back.wait_send()

        @pl.when(t < n_t - 1)
        def _():
            back.wait_recv()
            ahead.wait_send()

    def sum_copies(k):
        return [remote(sums.at[k], sum_buf.at[k, i], r.sum_send.at[k], r.sum_recv.at[k], d_peers[i])
                for i in range(n_dp - 1)]

    def sum_z_copies(k):
        return [remote(sum_mid.at[k], sum_z.at[k, i], r.sumz_send.at[k], r.sumz_recv.at[k], z_peers[i])
                for i in z_range]

    def sum_middle(k):
        settled(sum_buf.at[k], r.sum_recv.at[k], before)
        total = sums[k]
        for i in range(n_dp - 1):
            total = total + sum_buf[k, i]
        sum_mid[k] = total
        start_all(sum_z_copies(k))

    def sum_end(k):
        settled(sum_z.at[k], r.sumz_recv.at[k], before)
        total = sum_mid[k]
        for i in z_range:
            total = total + sum_z[k, i]
        sum_mid_out = r.sum_out
        sum_mid_out[k] = total

    edge_start(glu, 0)
    settled(taps.at[pl.ds(0, n_t - 1)], r.f_recv.at[0], before)
    edge_wait(glu, 0)
    size = 64

    def sweep(ref, j, first, backward):
        total = None
        for k in range(KERNEL):
            offset = EDGE - HALF + (KERNEL - 1 - k if backward else k)
            term = taps[j, k:k + 1, :] * ref[j, pl.ds(first + offset, size), :]
            total = term if total is None else total + term
        return total

    def convolve(j):
        def part_step(k, carry):
            first = pl.multiple_of(k * size, size)
            value = sweep(glu, j, first, False)
            bhat[j, pl.ds(first + EDGE, size), :] = value
            return (carry[0] + jnp.sum(value, axis=0, keepdims=True),
                    carry[1] + jnp.sum(value * value, axis=0, keepdims=True))
        zero = jnp.zeros((1, w), f32)
        one, two = lax.fori_loop(0, rows // size, part_step, (zero, zero))
        sums[0, pl.ds(2 * j, 1), :] = one
        sums[0, pl.ds(2 * j + 1, 1), :] = two
    loop(n_t, convolve)
    start_all(sum_copies(0))
    sum_middle(0)
    sum_end(0)

    def bn_parts(j):
        mean = r.sum_out[0, pl.ds(2 * j, 1), :] / row_count
        square = r.sum_out[0, pl.ds(2 * j + 1, 1), :] / row_count
        return mean, lax.rsqrt(square - mean * mean + norm_eps), taps[j, KERNEL:KERNEL + 1, :], taps[
            j, KERNEL + 1:KERNEL + 2, :]

    z_s[...] = jnp.zeros_like(z_s)

    def activate(j):
        mean, inverse, bn_gain, bn_shift = bn_parts(j)
        scaled = (bhat[j, inner, :] - mean) * inverse
        bhat[j, inner, :] = scaled
        normal = scaled * bn_gain + bn_shift
        act[j] = (normal * sigmoid(normal)).astype(bf16)
        z_s[...] = z_s[...] + dot(act[j], wbuf[3, :, block_of(j, width)][:, 3 * w:4 * w], 1, 1)
    loop(n_t, activate)
    edge_start(bhat, 1)

    a4, dx = r.a4, r.dx0

    def norm_four(part):
        value = x2[part, :] + z_s[part, :]
        x3[part, :] = value
        a4[part, :] = (norm_parts(value)[0] * gains[3:4, :]).astype(bf16)
    row_loop(rows, 64, norm_four)
    feed_rows(a4, wbuf.at[4], wbuf.at[5], z_s, r.hid2, r.slope2)
    gsum = r.gsum
    gsum[0] = jnp.zeros_like(gsum[0])
    dz, dz_turn, a_turn = r.dz, r.dz_turn, r.a_turn

    def add_gain(row, part_sum):
        gsum[0, row:row + 1, :] = gsum[0, row:row + 1, :] + part_sum

    def norm_five(part):
        value = x3[part, :] + 0.5 * z_s[part, :]
        scaled, grad_in, part_sum = norm_back(value, r.og[part, :].astype(f32), gains[4:5, :])
        r.out[part, :] = scaled * gains[4:5, :]
        dx[part, :] = grad_in
        dz[part, :] = (0.5 * grad_in).astype(bf16)
        add_gain(4, part_sum)
    row_loop(rows, 64, norm_five)
    leave(r.out)

    def grad_chunk(c):
        return gbuf.at[c - 2] if c >= 2 else wbuf.at[c + 4]

    def join_norm(row, x_of, factor):
        def step(part):
            _, grad_in, part_sum = norm_back(x_of(part), z_s[part, :], gains[row:row + 1, :])
            value = dx[part, :] + grad_in
            dx[part, :] = value
            dz[part, :] = (factor * value).astype(bf16)
            add_gain(row, part_sum)
        row_loop(rows, 64, step)

    folds = [order[::-1] for order in links]
    groups = span(links[0])
    core_buf, dp_buf, z_buf = r.core_buf, r.dp_buf, r.z_buf

    def grad_rows(u, mask):
        c, part = u
        count = rows_w // CUTS
        return grad_chunk(c).at[pl.ds(pl.multiple_of(flip(d, mask) * rows_w + part * count, count), count), :]

    def part_rows(part):
        return pl.ds(part * (rows_w // CUTS), rows_w // CUTS)

    def core_copies(u):
        return [remote(grad_rows(u, mask ^ CORE), core_buf.at[u[0], k, part_rows(u[1])],
                       r.core_send.at[0], r.core_recv.at[u[0], u[1]],
                       (flip(d, CORE), t)) for k, mask in enumerate(groups)]

    def fold_places(stage):
        places = []
        for h in range(2):
            masks = span(folds[h][stage + 1:])
            base = len(groups) - 2 * len(masks)
            places += [(mask, h, base + j) for j, mask in enumerate(masks)]
        return places

    def fold_copies(u, stage):
        c, part = u
        return [remote(grad_rows(u, mask ^ folds[h][stage]).at[:, pl.ds(h * half, half)],
                       dp_buf.at[c, h, slot, part_rows(part)],
                       r.fd_send.at[c], r.fd_recv.at[c, part, stage], (flip(d, folds[h][stage]), t))
                for mask, h, slot in fold_places(stage)]

    def fold_z_copies(u):
        c, part = u
        copies = []
        for k in z_range:
            target = lax.rem(t + k + 1, n_t)
            place = grad_rows(u, 0).at[:, pl.ds(pl.multiple_of(target * width, width), width)]
            copies.append(remote(place, z_buf.at[c, k, part_rows(part)], r.fz_send.at[0],
                                 r.fz_recv.at[c, part], z_peers[k]))
        return copies

    piece = 16
    per_part = rows_w // CUTS // piece

    def fold_start(c):
        for part in range(CUTS):
            start_all(core_copies((c, part)))

    def fold_step(c, stage, go=True):
        for part in range(CUTS):
            fold_unit((c, part), stage, go)

    def fold_send(c):
        for part in range(CUTS):
            start_all(fold_z_copies((c, part)))

    def fold_unit(u, stage, go=True):
        c, cut = u
        ref = grad_chunk(c)
        if stage == 0:
            settled(core_buf.at[c, :, part_rows(cut)], r.core_recv.at[c, cut], before)
            for k, mask in enumerate(groups):
                base = flip(d, mask) * rows_w

                def add_core(step, k=k, base=base):
                    step = step + cut * per_part
                    part = pl.ds(pl.multiple_of(base + step * piece, piece), piece)
                    ref[part, :] = (ref[part, :].astype(f32)
                                    + core_buf[c, k, block_of(step, piece), :].astype(f32)).astype(bf16)
                loop(per_part, add_core)
        elif stage <= n_link:
            places = fold_places(stage - 1)
            first_slot, count = places[0][2], len(places) // 2
            settled(dp_buf.at[c, :, pl.ds(first_slot, count), part_rows(cut)], r.fd_recv.at[c, cut, stage - 1], before)
            for mask, h, slot in places:
                base = flip(d, mask) * rows_w
                cols = pl.ds(h * half, half)

                def add_dp(step, base=base, cols=cols, h=h, slot=slot):
                    step = step + cut * per_part
                    part = pl.ds(pl.multiple_of(base + step * piece, piece), piece)
                    ref[part, cols] = (ref[part, cols].astype(f32)
                                       + dp_buf[c, h, slot, block_of(step, piece), :].astype(f32)).astype(bf16)
                loop(per_part, add_dp)
        else:
            settled(z_buf.at[c, :, part_rows(cut)], r.fz_recv.at[c, cut], before)

            def finish(step):
                step = step + cut * per_part
                part = pl.ds(pl.multiple_of(d * rows_w + step * piece, piece), piece)
                total = ref[part, block_of(t, width)].astype(f32)
                for k in z_range:
                    total = total + z_buf[c, k, block_of(step, piece), :].astype(f32)
                here = block_of(step, piece)
                if c == 2:
                    for k in range(4):
                        r.g_at[k, here, :] = total[:, k * w:(k + 1) * w]
                elif c == 3:
                    for k in range(2):
                        r.g_cw[here, k, :] = total[:, k * w:(k + 1) * w]
                    r.g_ao[here, :] = total[:, 2 * w:3 * w]
                    r.g_co[here, :] = total[:, 3 * w:4 * w]
                else:
                    grads[c][here, :] = total
            loop(per_part, finish)
            if cut == CUTS - 1:
                leave(*((r.g_at,) if c == 2 else (r.g_cw, r.g_ao, r.g_co) if c == 3 else (grads[c],)))
        if stage < n_link and go:
            start_all(fold_copies(u, stage))
        elif stage == n_link and go:
            start_all(fold_z_copies(u))

    grads = {0: r.g_fu, 1: r.g_fd, 4: r.g_su, 5: r.g_sd}
    final = n_link + 1
    fold_plan_one = [[(4, 1)], [], [(3, 0)]]
    fold_plan_two = []
    for stage in range(2, n_link + 1):
        fold_plan_two += [[(4, stage)], [(3, stage - 1)]]
    fold_plan_two += [[], [(3, n_link)]]

    dz_turn[...] = turned(dz[...])
    a_turn[...] = turned(a4[...])
    units = [(c, part) for c in range(CHUNKS) for part in range(CUTS)]
    settled(wbuf.at[0, pl.ds(0, CHUNKS * rows_w), pl.ds(0, (n_t - 1) * width)], r.z_send.at[0], before)
    for c in range(CHUNKS):
        settled(wbuf.at[0, pl.ds(0, (n_dp - 1) * rows_w), :], r.d_send.at[c], before)
    feed_back(dz, dz_turn, a_turn, wbuf.at[4], wbuf.at[5], z_s, r.hid2, r.slope2, grad_chunk(4), grad_chunk(5),
              lambda: fold_start(5), lambda: None)
    fold_start(4)
    join_norm(3, lambda part: x3[part, :], 1.0)

    dz_turn[...] = turned(dz[...])

    def act_back(j):
        mean, inverse, bn_gain, bn_shift = bn_parts(j)
        grad_act = dot(dz[...], wbuf[3, :, block_of(j, width)][:, 3 * w:4 * w], 1, 0)
        scaled = bhat[j, inner, :]
        normal = scaled * bn_gain + bn_shift
        sig_n = sigmoid(normal)
        value = grad_act * (sig_n * (1.0 + normal * (1.0 - sig_n)))
        dbn[j, inner, :] = value
        sums[1, pl.ds(2 * j, 1), :] = jnp.sum(value * scaled, axis=0, keepdims=True)
        sums[1, pl.ds(2 * j + 1, 1), :] = jnp.sum(value, axis=0, keepdims=True)
    loop(n_t, act_back)
    start_all(sum_copies(1))
    edge_start(dbn, 2)
    fold_step(5, 0)
    sum_middle(1)
    fold_step(4, 0, False)
    a_turn[...] = turned(a3[...])
    sum_end(1)
    for k, ref in ((1, bhat), (2, dbn)):
        edge_wait(ref, k)
    r.g_bn[...] = r.sum_out[1, pl.ds(2 * t, 2), :]
    leave(r.g_bn)
    small = r.small
    z_s[...] = jnp.zeros_like(z_s)

    def put_grad(c, j, first, value):
        if w % 128 == 0:
            grad_chunk(c)[:, pl.ds(pl.multiple_of(j * width + first, 128), value.shape[1])] = value
        else:
            old = grad_chunk(c)[:, block_of(j, width)]
            pieces = [old[:, :first], value, old[:, first + value.shape[1]:]]
            grad_chunk(c)[:, block_of(j, width)] = jnp.concatenate([p for p in pieces if p.shape[1] > 0], axis=1)

    def conv_back(j):
        mean, inverse, bn_gain, bn_shift = bn_parts(j)
        gamma = r.sum_out[1, pl.ds(2 * j, 1), :] / row_count
        beta = r.sum_out[1, pl.ds(2 * j + 1, 1), :] / row_count
        dbn[j] = bn_gain * inverse * (dbn[j] - beta - bhat[j] * gamma)
        dbn[j, pl.ds(0, EDGE), :] = jnp.where(t > 0, dbn[j, pl.ds(0, EDGE), :], 0.0)
        tail = pl.ds(EDGE + rows, EDGE)
        dbn[j, tail, :] = jnp.where(t < n_t - 1, dbn[j, tail, :], 0.0)

        def tap_step(k, carry):
            first = pl.multiple_of(k * size, size)
            own_part = dbn[j, pl.ds(first + EDGE, size), :]
            result = []
            for tap in range(KERNEL):
                term = own_part * glu[j, pl.ds(first + EDGE - HALF + tap, size), :]
                result.append(carry[tap] + jnp.sum(term.reshape(size // 8, 8, w), axis=0))
            return tuple(result)
        tap_sums = lax.fori_loop(0, rows // size, tap_step, tuple(jnp.zeros((8, w), f32) for _ in range(KERNEL)))
        for tap in range(KERNEL):
            small[0, j, tap:tap + 1, :] = jnp.sum(tap_sums[tap], axis=0, keepdims=True)

        def spread_step(k):
            first = pl.multiple_of(k * size, size)
            part = pl.ds(first, size)
            dglu = sweep(dbn, j, first, True)
            sig_p = sig[j, part, :]
            grad_val = dglu * sig_p
            r.de[part, 0:w] = grad_val.astype(bf16)
            r.de[part, w:2 * w] = (grad_val * val[j, part, :] * (1.0 - sig_p)).astype(bf16)
        loop(rows // size, spread_step)
        put_grad(3, j, 0, dot(a_turn[...], r.de[...], 1, 0).astype(bf16))
        put_grad(3, j, 3 * w, dot(dz_turn[...], act[j], 1, 0).astype(bf16))
        z_s[...] = z_s[...] + dot(r.de[...], wbuf[3, :, block_of(j, width)][:, 0:2 * w], 1, 1)

        @pl.when(j == n_t // 2)
        def _():
            fold_step(5, 1)
            for part in range(CUTS):
                start_all(fold_copies((4, part), 0))
    loop(n_t, conv_back)
    join_norm(2, lambda part: x2[part, :], 1.0)

    dz_turn[...] = turned(dz[...])
    dmix_s, dmix_turn, cq_turn, dcq_s = r.dmix_s, r.dmix_turn, r.cq_turn, r.dcq_s
    a2_turn, rf_out, rf_buf, rf_z = r.a2_turn, r.rf_out, r.rf_buf, r.rf_z

    def mix_back(j):
        put_grad(3, j, 2 * w, dot(dz_turn[...], mix[j].astype(bf16), 1, 0).astype(bf16))
        dmix = dot(dz[...], wbuf[3, :, block_of(j, width)][:, 2 * w:3 * w], 1, 0) * inv_s[j]
        dmix_s[j] = dmix.astype(bf16)
        dmix_turn[j] = dmix.T.astype(bf16)
        cq_turn[j] = turned(cq[j])
        dcq_s[j] = jnp.zeros_like(dcq_s[j])
    loop(n_t, mix_back)
    for stage in range(2, n_link + 1):
        fold_step(5, stage)
    fold_start(3)
    rf_copies = [remote(rf_out.at[k], rf_buf.at[k], r.rf_ss.at[k], r.rf_rs.at[k], z_peers[k]) for k in z_range]

    def keys_back(part, j):
        block = wbuf[2, :, block_of(j, width)]
        piece_rows = block_of(part, rows)
        k_p, v_p = kv[j, piece_rows, :][:, 0:w], kv[j, piece_rows, :][:, w:2 * w]
        product = dmix_s[j].astype(f32) * mix[j]
        for h in range(local_heads):
            mask = head_mask((rows, w), 1, head_dim, h)
            turn_mask = head_mask((w, rows), 0, head_dim, h)
            head = j * local_heads + h
            delta = jnp.sum(keep(mask, product), axis=-1, keepdims=True)
            p_h = probs[head, :, piece_rows]
            grad_p = dot(keep(mask, dmix_s[j]), v_p, 1, 1)
            ds = (p_h.astype(f32) * (grad_p - delta)).astype(bf16)
            probs[head, :, piece_rows] = ds
            dv_h = dot(keep(turn_mask, dmix_turn[j]), p_h, 1, 0)
            dk_h = dot(keep(turn_mask, cq_turn[j]), ds, 1, 0)
            dcq_h = keep(mask, dot(ds, k_p, 1, 0))
            if h == 0:
                dv, dk, dcq = dv_h, dk_h, dcq_h
            else:
                dv, dk, dcq = dv + dv_h, dk + dk_h, dcq + dcq_h
        dcq_s[j] = dcq_s[j] + dcq
        dkv = jnp.concatenate([(dk * scale).T, dv.T], axis=1).astype(bf16)
        kv[j, piece_rows, :] = dkv
        rf_z[...] = rf_z[...] + dot(dkv, block[:, w:3 * w], 1, 1)

    assert len(fold_plan_one) <= n_t
    for k in range(n_t):
        rf_z[...] = jnp.zeros_like(rf_z)
        part = lax.rem(t + 1 + k, n_t)
        loop(n_t, functools.partial(keys_back, part))
        if k < n_t - 1:
            rf_out[k] = rf_z[...].astype(bf16)
            rf_copies[k].start()
        for c, stage in fold_plan_one[k] if k < len(fold_plan_one) else ():
            fold_step(c, stage)
    for part in range(n_t):
        a2_turn[:, part * rows:(part + 1) * rows] = turned(a2_all[part])
    small[0, :, KERNEL:, :] = jnp.zeros_like(small[0, :, KERNEL:, :])

    z_s[...] = jnp.zeros_like(z_s)

    def queries_back(j):
        block = wbuf[2, :, block_of(j, width)]
        pq_turn = turned(pq[j])
        for h in range(local_heads):
            mask = head_mask((rows, w), 1, head_dim, h)
            turn_mask = head_mask((w, rows), 0, head_dim, h)
            back = dot(probs[j * local_heads + h], phase[...], 1, 0)
            spun(back[:, :D // 2], back[:, D // 2:])
            dpq_h = keep(mask, dot(u_s[...], block[:, 3 * w:4 * w], 1, 0))
            pos_h = dot(keep(turn_mask, pq_turn), u_s[...], 1, 0)
            if h == 0:
                dpq, pos = dpq_h, pos_h
            else:
                dpq, pos = dpq + dpq_h, pos + pos_h
        dcq = dcq_s[j] * scale
        dpq = dpq * scale
        small[0, j, KERNEL:KERNEL + 1, :] = jnp.sum(dcq, axis=0, keepdims=True)
        small[0, j, KERNEL + 1:KERNEL + 2, :] = jnp.sum(dpq, axis=0, keepdims=True)
        dq = (dcq + dpq).astype(bf16)
        z_s[...] = z_s[...] + dot(dq, block[:, 0:w], 1, 1)
        put_grad(2, j, 0, dot(a2_turn[:, block_of(t, rows)], dq, 1, 0).astype(bf16))
        put_grad(2, j, w, dot(a2_turn[...], kv[j], 1, 0).astype(bf16))
        put_grad(2, j, 3 * w, (pos.T * scale).astype(bf16))
        for turn in range(n_t):
            chosen = fold_plan_two[turn] if turn < len(fold_plan_two) else ()
            if chosen:
                @pl.when(j == turn)
                def _(chosen=chosen):
                    for c, stage in chosen:
                        fold_step(c, stage, stage < n_link)
    loop(n_t, queries_back)

    fold_start(2)
    small_buf, small_z = r.small_buf, r.small_z
    all_bits = [CORE] + links[0]

    def small_copy(k):
        return remote(small.at[k], small_buf.at[k], r.s_send.at[k], r.s_recv.at[k], (flip(d, all_bits[k]), t))

    small_z_copies = [remote(small.at[len(all_bits), lax.rem(t + k + 1, n_t)], small_z.at[k], r.sz_send.at[0],
                             r.sz_recv.at[0], z_peers[k]) for k in z_range]
    def small_next(k):
        small_copy(k - 1).wait_recv()
        small[k] = small[k - 1] + small_buf[k - 1]
        if k < len(all_bits):
            small_copy(k).start()
        else:
            start_all(small_z_copies)

    small_copy(0).start()
    a_turn[...] = turned(a1[...])
    arrive_all(rf_copies)
    small_next(1)

    def join_rows(part):
        total = z_s[part, :] + rf_z[part, :]
        for k in z_range:
            total = total + rf_buf[k, part, :].astype(f32)
        z_s[part, :] = total
    row_loop(rows, 64, join_rows)
    join_norm(1, lambda part: x1[part, :], 0.5)
    fold_step(2, 0)

    dz_turn[...] = turned(dz[...])
    def fold_middle():
        for c in (4, 3):
            fold_send(c)
        fold_step(1, 0)

    feed_back(dz, dz_turn, a_turn, wbuf.at[0], wbuf.at[1], z_s, r.hid1, r.slope1, grad_chunk(0), grad_chunk(1),
              lambda: fold_start(1), fold_middle)
    fold_start(0)
    join_norm(0, lambda part: x_ref[part, :].astype(f32), 1.0)
    leave(r.dx0)

    def gsum_copy(k):
        return remote(gsum.at[k], r.gsum_buf.at[k], r.g_send.at[k], r.g_recv.at[k], (flip(d, all_bits[k]), t))

    gsum_z_copies = [remote(gsum.at[len(all_bits)], r.gsum_z.at[k], r.gz_send.at[0], r.gz_recv.at[0],
                            z_peers[k]) for k in z_range]
    gsum_copy(0).start()

    def gsum_next(k):
        gsum_copy(k - 1).wait_recv()
        gsum[k] = gsum[k - 1] + r.gsum_buf[k - 1]
        if k < len(all_bits):
            gsum_copy(k).start()
        else:
            start_all(gsum_z_copies)

    chain = 1
    for u, stage in tail_plan(final):
        fold_unit(u, stage)
        if u == (0, CUTS - 1) and chain <= len(all_bits):
            if chain > 1:
                small_next(chain)
            gsum_next(chain)
            chain += 1
    for k in range(chain, len(all_bits) + 1):
        small_next(k)
        gsum_next(k)
    settled(small_z, r.sz_recv.at[0], before)
    total = small[len(all_bits), t]
    for k in z_range:
        total = total + small_z[k]
    r.g_taps[...] = total[0:KERNEL, :]
    for pair in range(2):
        row = total[KERNEL + pair:KERNEL + pair + 1, :]
        for h in range(local_heads):
            place = lax.broadcasted_iota(jnp.int32, (n_bias, w), 1)
            spot_h = (place == lax.broadcasted_iota(jnp.int32, (n_bias, w), 0) + d * n_bias + h * head_dim).astype(f32)
            r.g_bias[pair, h:h + 1, :] = lax.dot_general(row, spot_h, (((1,), (1,)), ((), ())), precision=high,
                                                         preferred_element_type=f32)
    settled(r.gsum_z, r.gz_recv.at[0], before)
    total_g = gsum[len(all_bits)]
    for k in z_range:
        total_g = total_g + r.gsum_z[k]
    spot_g = lax.dot_general(total_g, gain_spot, (((1,), (1,)), ((), ())), precision=high, preferred_element_type=f32)
    r.g_gains[...] = spot_g[0:5, :]

    leave(r.g_taps, r.g_bias, r.g_gains)
    for k, name in enumerate(leaving):
        pltpu.make_async_copy(getattr(r, name[:-len(HBM)]), getattr(r, name), r.out_sem.at[k]).wait()
    settled(taps.at[pl.ds(0, n_t - 1)], r.f_send.at[0], before)
    settled(a2_all.at[pl.ds(0, n_t - 1)], r.a_send.at[0], before)
    settled(small_z, r.sz_send.at[0], before)
    settled(r.gsum_z, r.gz_send.at[0], before)
    sent_all(rf_copies)
    settled(e_buf.at[pl.ds(0, n_t - 1)], r.e_send.at[0], before)
    sent_all(e_copies(n_t - 1, n_t + n_link))
    for k in range(2):
        settled(sum_buf.at[k], r.sum_send.at[k], before)
        settled(sum_z.at[k], r.sumz_send.at[k], before)
    for k in range(len(all_bits)):
        small_copy(k).wait_send()
        gsum_copy(k).wait_send()
    settled(gbuf.at[pl.ds(0, CHUNKS // 2)], r.core_send.at[0], before)
    settled(gbuf.at[0, pl.ds(0, CHUNKS * rows_w), pl.ds(0, (n_t - 1) * width)], r.fz_send.at[0], before)
    for c in range(CHUNKS):
        settled(gbuf.at[0, pl.ds(0, (len(groups) - 1) * rows_w), :], r.fd_send.at[c], before)


def layer_kernel(n_dp, n_t, head_dim, inputs):
    given = SimpleNamespace(**inputs)
    rows, D = given.x.shape
    rows_w, width = given.fu.shape
    w = D // n_t
    frames = rows * n_t
    heads = D // head_dim
    hidden = n_t * width
    n_bits = n_dp.bit_length() - 1
    n_e = n_t - 1 + n_bits
    n_gain = given.gain_in.shape[1]
    n_bias = given.bias_in.shape[2]
    tap_rows = 40
    groups = n_dp // 2
    z = n_t - 1
    sem = pltpu.SemaphoreType.DMA
    vm = pltpu.VMEM
    outs = dict(
        out=((rows, D), f32), dx0=((rows, D), f32), g_gains=((5, n_gain), f32), g_fu=((rows_w, width), f32),
        g_fd=((rows_w, width), f32), g_at=((4, rows_w, w), f32), g_ao=((rows_w, w), f32),
        g_bias=((2, w // head_dim, n_bias), f32), g_cw=((rows_w, 2, w), f32), g_taps=((KERNEL, w), f32),
        g_bn=((2, w), f32), g_co=((rows_w, w), f32), g_su=((rows_w, width), f32), g_sd=((rows_w, width), f32))
    edge_shape = (n_t, rows + 2 * EDGE, w)
    scratch = dict(
        pack=vm((2, rows_w, width), bf16), taps_own=vm((tap_rows, w), f32), wbuf=vm((CHUNKS, n_dp * rows_w, hidden), bf16),
        gbuf=vm((CHUNKS - 2, n_dp * rows_w, hidden), bf16), gains=vm((8, D), f32),
        taps=vm((n_t, tap_rows, w), f32), e_acc=vm((n_bits + 2, 8, D), f32), e_buf=vm((n_e, 8, D), f32),
        phase=vm((frames, D), bf16), spin=vm((2, rows, D // 2), f32), u_s=vm((rows, D), bf16),
        z_s=vm((rows, D), f32), x1=vm((rows, D), f32), x2=vm((rows, D), f32),
        x3=vm((rows, D), f32), a1=vm((rows, D), bf16), a2=vm((rows, D), bf16), a3=vm((rows, D), bf16),
        a4=vm((rows, D), bf16), dz=vm((rows, D), bf16), dz_turn=vm((D, rows), bf16),
        a_turn=vm((D, rows), bf16), a2_all=vm((n_t, rows, D), bf16), a2_turn=vm((D, frames), bf16),
        hid1=vm((rows, hidden), bf16), slope1=vm((rows, hidden), bf16), hid2=vm((rows, hidden), bf16),
        slope2=vm((rows, hidden), bf16), kv=vm((n_t, frames, 2 * w), bf16), cq=vm((n_t, rows, w), bf16),
        pq=vm((n_t, rows, w), bf16), mix=vm((n_t, rows, w), f32), inv_s=vm((n_t, rows, w), f32), probs=vm((heads, rows, frames), bf16),
        s_s=vm((rows, frames), f32), dmix_s=vm((n_t, rows, w), bf16), dmix_turn=vm((n_t, w, rows), bf16),
        cq_turn=vm((n_t, w, rows), bf16), dcq_s=vm((n_t, rows, w), f32),
        rf_z=vm((rows, D), f32), rf_out=vm((z, rows, D), bf16), rf_buf=vm((z, rows, D), bf16),
        glu=vm(edge_shape, f32), bhat=vm(edge_shape, f32), dbn=vm(edge_shape, f32),
        val=vm((n_t, rows, w), f32), sig=vm((n_t, rows, w), f32), act=vm((n_t, rows, w), bf16),
        de=vm((rows, 2 * w), bf16), sums=vm((2, 2 * n_t, w), f32), sum_mid=vm((2, 2 * n_t, w), f32),
        sum_out=vm((2, 2 * n_t, w), f32), sum_buf=vm((2, n_dp - 1, 2 * n_t, w), f32),
        sum_z=vm((2, z, 2 * n_t, w), f32), core_buf=vm((CHUNKS, groups, rows_w, hidden), bf16),
        dp_buf=vm((CHUNKS, 2, groups - 1, rows_w, hidden // 2), bf16), z_buf=vm((CHUNKS, z, rows_w, width), bf16),
        small=vm((n_bits + 1, n_t, tap_rows, w), f32), small_buf=vm((n_bits, n_t, tap_rows, w), f32),
        small_z=vm((z, tap_rows, w), f32), gsum=vm((n_bits + 1, 8, D), f32), gsum_buf=vm((n_bits, 8, D), f32),
        gsum_z=vm((z, 8, D), f32), local_sem=sem((CHUNKS, CUTS)))
    n_link = n_bits - 1
    scratch.update(
        z_send=sem((1,)), z_recv=sem((CHUNKS, CUTS)), d_send=sem((CHUNKS,)), d_recv=sem((CHUNKS, CUTS, n_bits)),
        f_send=sem((1,)), f_recv=sem((1,)), e_send=sem((n_bits + 1,)), e_recv=sem((n_bits + 1,)),
        a_send=sem((1,)), a_recv=sem((1,)), edge_send=sem((3, 2)), edge_recv=sem((3, 2)),
        sum_send=sem((2,)), sum_recv=sem((2,)), sumz_send=sem((2,)), sumz_recv=sem((2,)),
        core_send=sem((1,)), core_recv=sem((CHUNKS, CUTS)), fd_send=sem((CHUNKS,)),
        fd_recv=sem((CHUNKS, CUTS, n_link)), fz_send=sem((1,)), fz_recv=sem((CHUNKS, CUTS)),
        rf_ss=sem((z,)), rf_rs=sem((z,)), s_send=sem((n_bits,)), s_recv=sem((n_bits,)),
        sz_send=sem((1,)), sz_recv=sem((1,)), g_send=sem((n_bits,)), g_recv=sem((n_bits,)),
        gz_send=sem((1,)), gz_recv=sem((1,)))
    for name, (dims, kind) in outs.items():
        scratch[name] = vm(dims, kind)
    scratch.update(out_sem=sem((len(outs),)))
    names = list(inputs) + [name + HBM for name in outs] + list(scratch)
    vmem = pl.BlockSpec(memory_space=pltpu.VMEM)
    result = pl.pallas_call(
        functools.partial(layer_body, names, n_dp, n_t, head_dim),
        name="layer",
        out_shape=tuple(jax.ShapeDtypeStruct(dims, kind) for dims, kind in outs.values()),
        in_specs=[vmem] * len(inputs),
        out_specs=(pl.BlockSpec(memory_space=pl.ANY),) * len(outs),
        scratch_shapes=list(scratch.values()),
        compiler_params=pltpu.CompilerParams(collective_id=0, has_side_effects=True, vmem_limit_bytes=67043328),
    )(*inputs.values())
    return result


def settle_body(*refs):
    count = (len(refs) - 2) // 3
    sources, results, rooms = refs[:count], refs[count:2 * count], refs[2 * count:3 * count]
    sem_in, sem_out = refs[3 * count:]
    loads = [pltpu.make_async_copy(a, b, sem_in.at[k]) for k, (a, b) in enumerate(zip(sources, rooms))]
    stores = [pltpu.make_async_copy(a, b, sem_out.at[k]) for k, (a, b) in enumerate(zip(rooms, results))]
    for copy in loads:
        copy.start()
    for load, store in zip(loads, stores):
        load.wait()
        store.start()
    for copy in stores:
        copy.wait()


def settle(arrays):
    hbm = pl.BlockSpec(memory_space=pl.ANY)
    count = len(arrays)
    sem = pltpu.SemaphoreType.DMA
    return pl.pallas_call(
        settle_body,
        name="settle",
        out_shape=tuple(jax.ShapeDtypeStruct(a.shape, a.dtype) for a in arrays),
        in_specs=[hbm] * count,
        out_specs=(hbm,) * count,
        scratch_shapes=[pltpu.VMEM(a.shape, a.dtype) for a in arrays] + [sem((count,)), sem((count,))],
    )(*arrays)


def angle_tables(frames, width):
    step = 32
    frequency = np.exp(np.arange(width // 2) * (-2.0 * math.log(10000.0) / width))
    coarse = np.arange(frames // step)[:, None] * step * frequency
    fine = np.arange(step)[:, None] * frequency
    return jnp.asarray(np.stack([np.sin(coarse), np.cos(coarse), np.sin(fine), np.cos(fine)]), f32)


def per_device(n_dp, n_t, inputs, out_grad, norm_gains, first_up, first_down, attend_in, attend_out, position_bias,
               convolve_in, depth_kernel, batch_norm, convolve_out, second_up, second_down):
    rows, D = inputs.shape
    w = attend_in.shape[2]
    R = attend_in.shape[1]
    n_bias = position_bias.shape[2]
    head_dim = n_bias * n_dp
    got = layer_kernel(n_dp, n_t, head_dim, dict(
        fu=first_up, fd=first_down.T, at=attend_in, cw=convolve_in, ao=attend_out.T, co=convolve_out.T, su=second_up,
        sd=second_down.T, gain_in=norm_gains, bias_in=position_bias, tap_in=depth_kernel.T, bn_in=batch_norm, x=inputs,
        og=out_grad, tab=angle_tables(rows * n_t, D)))
    (out, dx0, g_gains, g_fu, g_fd, g_at, g_ao, g_bias, g_cw, g_taps, g_bn, g_co, g_su, g_sd) = settle(got)
    return (out, dx0, g_gains, g_fu, g_fd.T, g_at, g_ao.T, g_bias, g_cw, g_taps.T, g_bn, g_co.T, g_su, g_sd.T)


def solution(mesh):
    n_dp, n_t = mesh.shape["dp"], mesh.shape["tensor"]
    row = P(("dp", "tensor"), None)
    gain = P(None, ("dp", "tensor"))
    up = P("dp", "tensor")
    down = P("tensor", "dp")
    weights = (up, down, P(None, "dp", "tensor"), down, P(None, "tensor", "dp"), P("dp", None, "tensor"),
               P("tensor", None), P(None, "tensor"), down, up, down)
    return jax.shard_map(
        functools.partial(per_device, n_dp, n_t), mesh=mesh,
        in_specs=(row, row, gain) + weights,
        out_specs=(row, row, gain) + weights,
        check_vma=False)
```

time: 271 us -> 196 us (0.72)
  Pallas kernels: 254 us -> 195 us
  local copies, waits for them, and re-layouts: 14.5 us -> 0 us
    pallas_call x1, Pallas kernels: 254 us -> 193 us  [layer_kernel(): pl.pallas_call(functools.partial(layer_body, names, n_dp, n_t, head_dim),...]
    unnamed x35 -> x0, local copies, waits for them, and re-layouts: 7.48 us -> none
    transpose x3 -> x0, local copies, waits for them, and re-layouts: 3.96 us -> none  [the longest x1 2.01 us: per_device(): shards[5]]
where the time goes in v4:
time: 196 us
  Pallas kernels  195 us (99%)
    pallas_call x1, Pallas kernels, layer_kernel(): pl.pallas_call(functools.partial(layer_body, names, n_dp, n_t, head_dim),...  193 us

profile of v4, /device:TPU:0, one launch (start us, length us, event | category | flops | bytes accessed | tf_op | source)
XLA Modules:
  0.0 196.3 jit_solution(8010912923837924296)
XLA Ops:
  0.7 193.0 %layer.1 = (f32[256,512]{1,0:T(8,128)}, f32[256,512]{1,0:T(8,128)}, f32[5,16]{1,0:T(8,128)}, f32[64,512]{1,0:T(8,128)}, f32[64,512]{1,0:T(8,128)}, /*index=5*/f3...) custom-call(bf16[64,512]{1,0:T(8,128)(2,1)} %all_refs_0_.1, ...), custom_call_target="tpu_custom_call" | custom-call | tf_op jit(solution)/shard_map/layer/pallas_call | solution.py:1085
  193.6 2.5 %settle.1 = (f32[256,512]{1,0:T(8,128)}, f32[256,512]{1,0:T(8,128)}, f32[5,16]{1,0:T(8,128)}, f32[64,512]{1,0:T(8,128)}, f32[64,512]{1,0:T(8,128)}, /*index=5*/f...) custom-call(f32[256,512]{1,0:T(8,128)} %get-tuple-element.42.refs_0_, ...), custom_call_target="tpu_custom_call" | custom-call | tf_op jit(solution)/shard_map/settle/pallas_call | solution.py:1116

commit v5 on v4

--- a/solution.py
+++ b/solution.py
@@ -99,11 +99,17 @@
     return pl.ds(pl.multiple_of(k * size, size), size)
 
 
-def loop(count, body):
+def loop(count, body, unroll=1):
     def step(k, carry):
         body(k)
         return carry
-    lax.fori_loop(0, count, step, 0)
+    lax.fori_loop(0, count, step, 0, unroll=unroll)
+
+
+def halves(count, body, between, unroll=1):
+    loop(count // 2, body, unroll)
+    between()
+    loop(count - count // 2, lambda k: body(k + count // 2), unroll)
 
 
 def row_loop(rows, size, body):
@@ -130,13 +136,16 @@
 
 def tail_plan(final):
     parts = range(CUTS)
-    plan = [((2, part), 1) for part in parts] + [((0, part), 0) for part in parts]
+    last = CUTS - 1
+    plan = [((2, part), 1, True, None) for part in parts] + [((0, part), 0, False, None) for part in parts]
+    plan += [((1, part), 1, True, (0, 0) if part == 0 else None) for part in parts]
+    for stage in range(2, final):
+        plan += [((2, part), stage, True, None) for part in parts]
+    for stage in range(2, final):
+        plan += [((1, part), stage, True, (0, last) if (stage, part) == (2, 0) else None) for part in parts]
     for stage in range(1, final):
-        plan += [((1, part), stage) for part in parts]
-        if stage + 1 < final:
-            plan += [((2, part), stage + 1) for part in parts]
-        plan += [((0, part), stage) for part in parts]
-    return plan + [((c, part), final) for c in (4, 5, 3, 2, 1, 0) for part in parts]
+        plan += [((0, part), stage, True, None) for part in parts]
+    return plan + [((c, part), final, True, None) for c in (5, 4, 3, 2, 1, 0) for part in parts]
 
 
 def relay_order(stages):
@@ -156,6 +165,7 @@
 
 
 SLAB = 512
+NORM_ROWS = 256
 HBM = "_hbm"
 
 
@@ -169,7 +179,7 @@
         hidden[:, cols] = (pre * sig).astype(bf16)
         slope[:, cols] = (sig * (1.0 + pre * (1.0 - sig))).astype(bf16)
         z_ref[...] = z_ref[...] + dot(hidden[:, cols], down_t[:, cols], 1, 1)
-    loop(up.shape[1] // SLAB, step)
+    loop(up.shape[1] // SLAB, step, 2)
 
 
 def feed_back(dz_ref, dz_turn, a_turn, up, down_t, z_ref, hidden, slope, g_up, g_down, start_down, middle):
@@ -187,7 +197,7 @@
         grad_pre = (dot(dz_ref[...], down_t[:, cols], 1, 0) * slope[:, cols].astype(f32)).astype(bf16)
         g_up[:, cols] = dot(a_turn[...], grad_pre, 1, 0).astype(bf16)
         z_ref[...] = z_ref[...] + dot(grad_pre, up[:, cols], 1, 1)
-    loop(slabs - 1, step)
+    loop(slabs - 1, step, slabs - 1)
     middle()
     step(slabs - 1)
 
@@ -387,14 +397,14 @@
 
     def norm_one(part):
         a1[part, :] = (norm_parts(x_ref[part, :].astype(f32))[0] * gains[0:1, :]).astype(bf16)
-    row_loop(rows, 64, norm_one)
+    row_loop(rows, NORM_ROWS, norm_one)
     feed_rows(a1, wbuf.at[0], wbuf.at[1], z_s, r.hid1, r.slope1)
 
     def norm_two(part):
         value = x_ref[part, :].astype(f32) + 0.5 * z_s[part, :]
         x1[part, :] = value
         a2[part, :] = (norm_parts(value)[0] * gains[1:2, :]).astype(bf16)
-    row_loop(rows, 64, norm_two)
+    row_loop(rows, NORM_ROWS, norm_two)
 
     a_copies = [remote(a2, a2_all.at[t], r.a_send.at[0], r.a_recv.at[0], z_peers[k]) for k in z_range]
     start_all(a_copies)
@@ -441,7 +451,7 @@
         mix[j] = mixture
         inv_s[j] = inverse
         z_s[...] = z_s[...] + dot(mixture.astype(bf16), wbuf[3, :, cols][:, 2 * w:3 * w], 1, 1)
-    loop(n_t, head_group)
+    loop(n_t, head_group, 2)
 
     a3, glu, bhat, val, sig, act = r.a3, r.glu, r.bhat, r.val, r.sig, r.act
     dbn, sums, sum_buf, sum_mid, sum_z = r.dbn, r.sums, r.sum_buf, r.sum_mid, r.sum_z
@@ -451,7 +461,7 @@
         value = x1[part, :] + z_s[part, :]
         x2[part, :] = value
         a3[part, :] = (norm_parts(value)[0] * gains[2:3, :]).astype(bf16)
-    row_loop(rows, 64, norm_three)
+    row_loop(rows, NORM_ROWS, norm_three)
 
     def gate(j):
         block = wbuf[3, :, block_of(j, width)]
@@ -578,14 +588,14 @@
         value = x2[part, :] + z_s[part, :]
         x3[part, :] = value
         a4[part, :] = (norm_parts(value)[0] * gains[3:4, :]).astype(bf16)
-    row_loop(rows, 64, norm_four)
+    row_loop(rows, NORM_ROWS, norm_four)
     feed_rows(a4, wbuf.at[4], wbuf.at[5], z_s, r.hid2, r.slope2)
     gsum = r.gsum
-    gsum[0] = jnp.zeros_like(gsum[0])
+    gsum[...] = jnp.zeros_like(gsum)
     dz, dz_turn, a_turn = r.dz, r.dz_turn, r.a_turn
 
     def add_gain(row, part_sum):
-        gsum[0, row:row + 1, :] = gsum[0, row:row + 1, :] + part_sum
+        gsum[row:row + 1, :] = gsum[row:row + 1, :] + part_sum
 
     def norm_five(part):
         value = x3[part, :] + 0.5 * z_s[part, :]
@@ -594,7 +604,7 @@
         dx[part, :] = grad_in
         dz[part, :] = (0.5 * grad_in).astype(bf16)
         add_gain(4, part_sum)
-    row_loop(rows, 64, norm_five)
+    row_loop(rows, NORM_ROWS, norm_five)
     leave(r.out)
 
     def grad_chunk(c):
@@ -607,7 +617,7 @@
             dx[part, :] = value
             dz[part, :] = (factor * value).astype(bf16)
             add_gain(row, part_sum)
-        row_loop(rows, 64, step)
+        row_loop(rows, NORM_ROWS, step)
 
     folds = [order[::-1] for order in links]
     groups = span(links[0])
@@ -724,11 +734,7 @@
 
     grads = {0: r.g_fu, 1: r.g_fd, 4: r.g_su, 5: r.g_sd}
     final = n_link + 1
-    fold_plan_one = [[(4, 1)], [], [(3, 0)]]
-    fold_plan_two = []
-    for stage in range(2, n_link + 1):
-        fold_plan_two += [[(4, stage)], [(3, stage - 1)]]
-    fold_plan_two += [[], [(3, n_link)]]
+    fold_plan_one = [[], [(5, stage) for stage in range(2, n_link + 1)], [(4, 1), (3, 0)]]
 
     dz_turn[...] = turned(dz[...])
     a_turn[...] = turned(a4[...])
@@ -756,8 +762,8 @@
     loop(n_t, act_back)
     start_all(sum_copies(1))
     edge_start(dbn, 2)
+    sum_middle(1)
     fold_step(5, 0)
-    sum_middle(1)
     fold_step(4, 0, False)
     a_turn[...] = turned(a3[...])
     sum_end(1)
@@ -795,7 +801,7 @@
             return tuple(result)
         tap_sums = lax.fori_loop(0, rows // size, tap_step, tuple(jnp.zeros((8, w), f32) for _ in range(KERNEL)))
         for tap in range(KERNEL):
-            small[0, j, tap:tap + 1, :] = jnp.sum(tap_sums[tap], axis=0, keepdims=True)
+            small[j, tap:tap + 1, :] = jnp.sum(tap_sums[tap], axis=0, keepdims=True)
 
         def spread_step(k):
             first = pl.multiple_of(k * size, size)
@@ -810,17 +816,17 @@
         put_grad(3, j, 3 * w, dot(dz_turn[...], act[j], 1, 0).astype(bf16))
         z_s[...] = z_s[...] + dot(r.de[...], wbuf[3, :, block_of(j, width)][:, 0:2 * w], 1, 1)
 
-        @pl.when(j == n_t // 2)
-        def _():
-            fold_step(5, 1)
-            for part in range(CUTS):
-                start_all(fold_copies((4, part), 0))
+    def conv_middle():
+        fold_step(5, 1)
+        for part in range(CUTS):
+            start_all(fold_copies((4, part), 0))
     loop(n_t, conv_back)
+    conv_middle()
     join_norm(2, lambda part: x2[part, :], 1.0)
 
     dz_turn[...] = turned(dz[...])
     dmix_s, dmix_turn, cq_turn, dcq_s = r.dmix_s, r.dmix_turn, r.cq_turn, r.dcq_s
-    a2_turn, rf_out, rf_buf, rf_z = r.a2_turn, r.rf_out, r.rf_buf, r.rf_z
+    a2_turn, rf_out, rf_buf = r.a2_turn, r.rf_out, r.rf_buf
 
     def mix_back(j):
         put_grad(3, j, 2 * w, dot(dz_turn[...], mix[j].astype(bf16), 1, 0).astype(bf16))
@@ -830,8 +836,6 @@
         cq_turn[j] = turned(cq[j])
         dcq_s[j] = jnp.zeros_like(dcq_s[j])
     loop(n_t, mix_back)
-    for stage in range(2, n_link + 1):
-        fold_step(5, stage)
     fold_start(3)
     rf_copies = [remote(rf_out.at[k], rf_buf.at[k], r.rf_ss.at[k], r.rf_rs.at[k], z_peers[k]) for k in z_range]
 
@@ -859,23 +863,22 @@
         dcq_s[j] = dcq_s[j] + dcq
         dkv = jnp.concatenate([(dk * scale).T, dv.T], axis=1).astype(bf16)
         kv[j, piece_rows, :] = dkv
-        rf_z[...] = rf_z[...] + dot(dkv, block[:, w:3 * w], 1, 1)
+        z_s[...] = z_s[...] + dot(dkv, block[:, w:3 * w], 1, 1)
 
     assert len(fold_plan_one) <= n_t
     for k in range(n_t):
-        rf_z[...] = jnp.zeros_like(rf_z)
+        z_s[...] = jnp.zeros_like(z_s)
         part = lax.rem(t + 1 + k, n_t)
-        loop(n_t, functools.partial(keys_back, part))
+        loop(n_t, functools.partial(keys_back, part), 2)
         if k < n_t - 1:
-            rf_out[k] = rf_z[...].astype(bf16)
+            rf_out[k] = z_s[...].astype(bf16)
             rf_copies[k].start()
         for c, stage in fold_plan_one[k] if k < len(fold_plan_one) else ():
-            fold_step(c, stage)
+            fold_step(c, stage, stage < n_link)
     for part in range(n_t):
         a2_turn[:, part * rows:(part + 1) * rows] = turned(a2_all[part])
-    small[0, :, KERNEL:, :] = jnp.zeros_like(small[0, :, KERNEL:, :])
-
-    z_s[...] = jnp.zeros_like(z_s)
+    small[:, KERNEL:, :] = jnp.zeros_like(small[:, KERNEL:, :])
+
 
     def queries_back(j):
         block = wbuf[2, :, block_of(j, width)]
@@ -893,57 +896,53 @@
                 dpq, pos = dpq + dpq_h, pos + pos_h
         dcq = dcq_s[j] * scale
         dpq = dpq * scale
-        small[0, j, KERNEL:KERNEL + 1, :] = jnp.sum(dcq, axis=0, keepdims=True)
-        small[0, j, KERNEL + 1:KERNEL + 2, :] = jnp.sum(dpq, axis=0, keepdims=True)
+        small[j, KERNEL:KERNEL + 1, :] = jnp.sum(dcq, axis=0, keepdims=True)
+        small[j, KERNEL + 1:KERNEL + 2, :] = jnp.sum(dpq, axis=0, keepdims=True)
         dq = (dcq + dpq).astype(bf16)
         z_s[...] = z_s[...] + dot(dq, block[:, 0:w], 1, 1)
         put_grad(2, j, 0, dot(a2_turn[:, block_of(t, rows)], dq, 1, 0).astype(bf16))
         put_grad(2, j, w, dot(a2_turn[...], kv[j], 1, 0).astype(bf16))
         put_grad(2, j, 3 * w, (pos.T * scale).astype(bf16))
-        for turn in range(n_t):
-            chosen = fold_plan_two[turn] if turn < len(fold_plan_two) else ()
-            if chosen:
-                @pl.when(j == turn)
-                def _(chosen=chosen):
-                    for c, stage in chosen:
-                        fold_step(c, stage, stage < n_link)
-    loop(n_t, queries_back)
+
+    def fold_some(plan):
+        for c, stage in plan:
+            fold_step(c, stage, stage < n_link)
+    middle_plan = [(4, stage) for stage in range(2, n_link + 1)]
+    halves(n_t, queries_back, lambda: fold_some(middle_plan), 2)
 
     fold_start(2)
-    small_buf, small_z = r.small_buf, r.small_z
-    all_bits = [CORE] + links[0]
-
-    def small_copy(k):
-        return remote(small.at[k], small_buf.at[k], r.s_send.at[k], r.s_recv.at[k], (flip(d, all_bits[k]), t))
-
-    small_z_copies = [remote(small.at[len(all_bits), lax.rem(t + k + 1, n_t)], small_z.at[k], r.sz_send.at[0],
-                             r.sz_recv.at[0], z_peers[k]) for k in z_range]
-    def small_next(k):
-        small_copy(k - 1).wait_recv()
-        small[k] = small[k - 1] + small_buf[k - 1]
-        if k < len(all_bits):
-            small_copy(k).start()
-        else:
-            start_all(small_z_copies)
-
-    small_copy(0).start()
+    small_z, small_mid, small_buf = r.small_z, r.small_mid, r.small_buf
+    small_z_copies = [remote(small.at[lax.rem(t + k + 1, n_t)], small_z.at[k], r.sz_send.at[0], r.sz_recv.at[0],
+                             z_peers[k]) for k in z_range]
+    small_copies = [remote(small_mid, small_buf.at[k], r.s_send.at[0], r.s_recv.at[0], d_peers[k])
+                    for k in range(n_dp - 1)]
+
+    def small_middle():
+        settled(small_z, r.sz_recv.at[0], before)
+        total = small[t]
+        for k in z_range:
+            total = total + small_z[k]
+        small_mid[...] = total
+        start_all(small_copies)
+    start_all(small_z_copies)
     a_turn[...] = turned(a1[...])
+    fold_some([(3, 1)])
+    fold_step(2, 0)
+    fold_some([(3, stage) for stage in range(2, n_link + 1)])
     arrive_all(rf_copies)
-    small_next(1)
 
     def join_rows(part):
-        total = z_s[part, :] + rf_z[part, :]
+        total = z_s[part, :]
         for k in z_range:
             total = total + rf_buf[k, part, :].astype(f32)
         z_s[part, :] = total
-    row_loop(rows, 64, join_rows)
+    row_loop(rows, NORM_ROWS, join_rows)
     join_norm(1, lambda part: x1[part, :], 0.5)
-    fold_step(2, 0)
+    for c in (5, 4, 3):
+        fold_send(c)
 
     dz_turn[...] = turned(dz[...])
     def fold_middle():
-        for c in (4, 3):
-            fold_send(c)
         fold_step(1, 0)
 
     feed_back(dz, dz_turn, a_turn, wbuf.at[0], wbuf.at[1], z_s, r.hid1, r.slope1, grad_chunk(0), grad_chunk(1),
@@ -952,36 +951,30 @@
     join_norm(0, lambda part: x_ref[part, :].astype(f32), 1.0)
     leave(r.dx0)
 
-    def gsum_copy(k):
-        return remote(gsum.at[k], r.gsum_buf.at[k], r.g_send.at[k], r.g_recv.at[k], (flip(d, all_bits[k]), t))
-
-    gsum_z_copies = [remote(gsum.at[len(all_bits)], r.gsum_z.at[k], r.gz_send.at[0], r.gz_recv.at[0],
-                            z_peers[k]) for k in z_range]
-    gsum_copy(0).start()
-
-    def gsum_next(k):
-        gsum_copy(k - 1).wait_recv()
-        gsum[k] = gsum[k - 1] + r.gsum_buf[k - 1]
-        if k < len(all_bits):
-            gsum_copy(k).start()
-        else:
-            start_all(gsum_z_copies)
-
-    chain = 1
-    for u, stage in tail_plan(final):
-        fold_unit(u, stage)
-        if u == (0, CUTS - 1) and chain <= len(all_bits):
-            if chain > 1:
-                small_next(chain)
-            gsum_next(chain)
-            chain += 1
-    for k in range(chain, len(all_bits) + 1):
-        small_next(k)
-        gsum_next(k)
-    settled(small_z, r.sz_recv.at[0], before)
-    total = small[len(all_bits), t]
-    for k in z_range:
-        total = total + small_z[k]
+    gsum_copies = [remote(gsum, r.gsum_buf.at[k], r.g_send.at[0], r.g_recv.at[0], d_peers[k])
+                   for k in range(n_dp - 1)]
+    gsum_z_copies = [remote(r.gsum_mid, r.gsum_z.at[k], r.gz_send.at[0], r.gz_recv.at[0], z_peers[k])
+                     for k in z_range]
+    start_all(gsum_copies)
+
+    def gsum_middle():
+        settled(r.gsum_buf, r.g_recv.at[0], before)
+        total = gsum[...]
+        for k in range(n_dp - 1):
+            total = total + r.gsum_buf[k]
+        r.gsum_mid[...] = total
+        start_all(gsum_z_copies)
+    small_middle()
+    for u, stage, go, other in tail_plan(final):
+        fold_unit(u, stage, go)
+        if other is not None:
+            start_all(fold_copies(other, 0))
+        if (u, stage) == ((0, CUTS - 1), 1):
+            gsum_middle()
+    settled(small_buf, r.s_recv.at[0], before)
+    total = small_mid[...]
+    for k in range(n_dp - 1):
+        total = total + small_buf[k]
     r.g_taps[...] = total[0:KERNEL, :]
     for pair in range(2):
         row = total[KERNEL + pair:KERNEL + pair + 1, :]
@@ -991,7 +984,7 @@
             r.g_bias[pair, h:h + 1, :] = lax.dot_general(row, spot_h, (((1,), (1,)), ((), ())), precision=high,
                                                          preferred_element_type=f32)
     settled(r.gsum_z, r.gz_recv.at[0], before)
-    total_g = gsum[len(all_bits)]
+    total_g = r.gsum_mid[...]
     for k in z_range:
         total_g = total_g + r.gsum_z[k]
     spot_g = lax.dot_general(total_g, gain_spot, (((1,), (1,)), ((), ())), precision=high, preferred_element_type=f32)
@@ -1010,9 +1003,8 @@
     for k in range(2):
         settled(sum_buf.at[k], r.sum_send.at[k], before)
         settled(sum_z.at[k], r.sumz_send.at[k], before)
-    for k in range(len(all_bits)):
-        small_copy(k).wait_send()
-        gsum_copy(k).wait_send()
+    settled(small_buf, r.s_send.at[0], before)
+    settled(r.gsum_buf, r.g_send.at[0], before)
     settled(gbuf.at[pl.ds(0, CHUNKS // 2)], r.core_send.at[0], before)
     settled(gbuf.at[0, pl.ds(0, CHUNKS * rows_w), pl.ds(0, (n_t - 1) * width)], r.fz_send.at[0], before)
     for c in range(CHUNKS):
@@ -1056,16 +1048,16 @@
         pq=vm((n_t, rows, w), bf16), mix=vm((n_t, rows, w), f32), inv_s=vm((n_t, rows, w), f32), probs=vm((heads, rows, frames), bf16),
         s_s=vm((rows, frames), f32), dmix_s=vm((n_t, rows, w), bf16), dmix_turn=vm((n_t, w, rows), bf16),
         cq_turn=vm((n_t, w, rows), bf16), dcq_s=vm((n_t, rows, w), f32),
-        rf_z=vm((rows, D), f32), rf_out=vm((z, rows, D), bf16), rf_buf=vm((z, rows, D), bf16),
+        rf_out=vm((z, rows, D), bf16), rf_buf=vm((z, rows, D), bf16),
         glu=vm(edge_shape, f32), bhat=vm(edge_shape, f32), dbn=vm(edge_shape, f32),
         val=vm((n_t, rows, w), f32), sig=vm((n_t, rows, w), f32), act=vm((n_t, rows, w), bf16),
         de=vm((rows, 2 * w), bf16), sums=vm((2, 2 * n_t, w), f32), sum_mid=vm((2, 2 * n_t, w), f32),
         sum_out=vm((2, 2 * n_t, w), f32), sum_buf=vm((2, n_dp - 1, 2 * n_t, w), f32),
         sum_z=vm((2, z, 2 * n_t, w), f32), core_buf=vm((CHUNKS, groups, rows_w, hidden), bf16),
         dp_buf=vm((CHUNKS, 2, groups - 1, rows_w, hidden // 2), bf16), z_buf=vm((CHUNKS, z, rows_w, width), bf16),
-        small=vm((n_bits + 1, n_t, tap_rows, w), f32), small_buf=vm((n_bits, n_t, tap_rows, w), f32),
-        small_z=vm((z, tap_rows, w), f32), gsum=vm((n_bits + 1, 8, D), f32), gsum_buf=vm((n_bits, 8, D), f32),
-        gsum_z=vm((z, 8, D), f32), local_sem=sem((CHUNKS, CUTS)))
+        small=vm((n_t, tap_rows, w), f32), small_buf=vm((n_dp - 1, tap_rows, w), f32),
+        small_mid=vm((tap_rows, w), f32), small_z=vm((z, tap_rows, w), f32), gsum=vm((8, D), f32),
+        gsum_buf=vm((n_dp - 1, 8, D), f32), gsum_mid=vm((8, D), f32), gsum_z=vm((z, 8, D), f32), local_sem=sem((CHUNKS, CUTS)))
     n_link = n_bits - 1
     scratch.update(
         z_send=sem((1,)), z_recv=sem((CHUNKS, CUTS)), d_send=sem((CHUNKS,)), d_recv=sem((CHUNKS, CUTS, n_bits)),
@@ -1074,8 +1066,8 @@
         sum_send=sem((2,)), sum_recv=sem((2,)), sumz_send=sem((2,)), sumz_recv=sem((2,)),
         core_send=sem((1,)), core_recv=sem((CHUNKS, CUTS)), fd_send=sem((CHUNKS,)),
         fd_recv=sem((CHUNKS, CUTS, n_link)), fz_send=sem((1,)), fz_recv=sem((CHUNKS, CUTS)),
-        rf_ss=sem((z,)), rf_rs=sem((z,)), s_send=sem((n_bits,)), s_recv=sem((n_bits,)),
-        sz_send=sem((1,)), sz_recv=sem((1,)), g_send=sem((n_bits,)), g_recv=sem((n_bits,)),
+        rf_ss=sem((z,)), rf_rs=sem((z,)), s_send=sem((1,)), s_recv=sem((1,)),
+        sz_send=sem((1,)), sz_recv=sem((1,)), g_send=sem((1,)), g_recv=sem((1,)),
         gz_send=sem((1,)), gz_recv=sem((1,)))
     for name, (dims, kind) in outs.items():
         scratch[name] = vm(dims, kind)

time: 196 us -> 190 us (0.969)
  Pallas kernels: 195 us -> 189 us
    pallas_call x1, Pallas kernels: 193 us -> 187 us  [layer_kernel(): pl.pallas_call(functools.partial(layer_body, names, n_dp, n_t, head_dim),...]
where the time goes in v5:
time: 190 us
  Pallas kernels  189 us (99%)
    pallas_call x1, Pallas kernels, layer_kernel(): pl.pallas_call(functools.partial(layer_body, names, n_dp, n_t, head_dim),...  187 us

profile of v5, /device:TPU:0, one launch (start us, length us, event | category | flops | bytes accessed | tf_op | source)
XLA Modules:
  0.0 190.2 jit_solution(1696026295601777857)
XLA Ops:
  0.7 186.8 %layer.1 = (f32[256,512]{1,0:T(8,128)}, f32[256,512]{1,0:T(8,128)}, f32[5,16]{1,0:T(8,128)}, f32[64,512]{1,0:T(8,128)}, f32[64,512]{1,0:T(8,128)}, /*index=5*/f3...) custom-call(bf16[64,512]{1,0:T(8,128)(2,1)} %all_refs_0_.1, ...), custom_call_target="tpu_custom_call" | custom-call | tf_op jit(solution)/shard_map/layer/pallas_call | solution.py:1077
  187.5 2.5 %settle.1 = (f32[256,512]{1,0:T(8,128)}, f32[256,512]{1,0:T(8,128)}, f32[5,16]{1,0:T(8,128)}, f32[64,512]{1,0:T(8,128)}, f32[64,512]{1,0:T(8,128)}, /*index=5*/f...) custom-call(f32[256,512]{1,0:T(8,128)} %get-tuple-element.42.refs_0_, ...), custom_call_target="tpu_custom_call" | custom-call | tf_op jit(solution)/shard_map/settle/pallas_call | solution.py:1108

commit v6 on v5

--- a/solution.py
+++ b/solution.py
@@ -928,7 +928,6 @@
     a_turn[...] = turned(a1[...])
     fold_some([(3, 1)])
     fold_step(2, 0)
-    fold_some([(3, stage) for stage in range(2, n_link + 1)])
     arrive_all(rf_copies)
 
     def join_rows(part):
@@ -938,6 +937,7 @@
         z_s[part, :] = total
     row_loop(rows, NORM_ROWS, join_rows)
     join_norm(1, lambda part: x1[part, :], 0.5)
+    fold_some([(3, stage) for stage in range(2, n_link + 1)])
     for c in (5, 4, 3):
         fold_send(c)
 

time: 190 us -> 189 us (level)
  no operation moved by 1% of the time
where the time goes in v6:
time: 189 us
  Pallas kernels  188 us (99%)
    pallas_call x1, Pallas kernels, layer_kernel(): pl.pallas_call(functools.partial(layer_body, names, n_dp, n_t, head_dim),...  186 us

profile of v6, /device:TPU:0, one launch (start us, length us, event | category | flops | bytes accessed | tf_op | source)
XLA Modules:
  0.0 189.1 jit_solution(14752069775119007196)
XLA Ops:
  0.7 185.7 %layer.1 = (f32[256,512]{1,0:T(8,128)}, f32[256,512]{1,0:T(8,128)}, f32[5,16]{1,0:T(8,128)}, f32[64,512]{1,0:T(8,128)}, f32[64,512]{1,0:T(8,128)}, /*index=5*/f3...) custom-call(bf16[64,512]{1,0:T(8,128)(2,1)} %all_refs_0_.1, ...), custom_call_target="tpu_custom_call" | custom-call | tf_op jit(solution)/shard_map/layer/pallas_call | solution.py:1077
  186.4 2.5 %settle.1 = (f32[256,512]{1,0:T(8,128)}, f32[256,512]{1,0:T(8,128)}, f32[5,16]{1,0:T(8,128)}, f32[64,512]{1,0:T(8,128)}, f32[64,512]{1,0:T(8,128)}, /*index=5*/f...) custom-call(f32[256,512]{1,0:T(8,128)} %get-tuple-element.42.refs_0_, ...), custom_call_target="tpu_custom_call" | custom-call | tf_op jit(solution)/shard_map/settle/pallas_call | solution.py:1108
